TPU v7x, 32 devices: a whole 2x2x4 slice. The times are simulated.
32 devices in a mesh: shard: 8 (over z, y), rep: 4 (over x, core).
Axes of the slice: x: 2, y: 2, z: 4, core: 2. Of those that a mesh axis runs over, the one named last changes fastest.
Arguments:
- tokens: bfloat16 [32768, 1024], P(('shard', 'rep')), may hold values from -6 to 6
- lengths: int32 [32], P(('shard', 'rep')), may hold values from 256 to 1024, as said below
- variate_ids: int32 [32, 1024], P(('shard', 'rep')), may hold values from 0 to 3
- time_ids: int32 [32, 1024], P(('shard', 'rep')), may hold values from 0 to 1023
- attn_gain: bfloat16 [1024], P('shard'), may hold values from 0.5 to 1.5
- w_qkv: bfloat16 [1024, 3072], P('shard'), may hold values from -0.1875 to 0.1875
- attn_bias: bfloat16 [2, 16], P(None, 'shard'), may hold values from -1 to 1
- w_out: bfloat16 [1024, 1024], P('shard'), may hold values from -0.75 to 0.75
- ffn_gain: bfloat16 [1024], P('shard'), may hold values from 0.5 to 1.5
- w_in: bfloat16 [1024, 8192], P('shard'), may hold values from -0.1875 to 0.1875
- w_down: bfloat16 [4096, 1024], P('shard'), may hold values from -0.09375 to 0.09375
- cotangent: bfloat16 [32768, 1024], P(('shard', 'rep')), may hold values from -6 to 6
Outputs:
- result: bfloat16 [32768, 1024], P(('shard', 'rep'))
- grad_tokens: float32 [32768, 1024], P(('shard', 'rep'))
- grad_attn_gain: float32 [1024], P('shard')
- grad_qkv: float32 [1024, 3072], P('shard')
- grad_bias: float32 [2, 16], P(None, 'shard')
- grad_out: float32 [1024, 1024], P('shard')
- grad_ffn_gain: float32 [1024], P('shard')
- grad_in: float32 [1024, 8192], P('shard')
- grad_down: float32 [4096, 1024], P('shard')
Inputs may be any that keep to these rules, and one draw needn't show every extreme that they name: `lengths`: some sequence has all 1024 positions valid.
All inputs are finite; a program needn't handle non-finite values.
Results may differ from a plain program's by a relative error of at most 0.029.
Values may be sent and summed in bfloat16 or wider, within the bound.
A program may use at most 384 MiB of HBM per device.

v0:
```python
import jax
import jax.numpy as jnp
from jax import lax
from jax.sharding import PartitionSpec as P

D = 1024
HEADS = 16
HEAD_DIM = 64
FF = 4096


norm_eps = 1e-06
rope_base = 10000.0
masked_score = -1000000000.0


def contract_rows(first_op, second_op):
    return lax.dot_general(
        first_op, second_op, (((0,), (0,)), ((), ())), preferred_element_type=jnp.float32
    )


def times_transpose(first_op, second_op):
    return lax.dot_general(
        first_op, second_op, (((1,), (1,)), ((), ())), preferred_element_type=jnp.float32
    )


def rope_tables(time_rows, head_dim):
    half_dim = head_dim // 2
    exponent = jnp.arange(half_dim).astype(jnp.float32) * (2.0 / head_dim)
    inverse = jnp.exp(-jnp.log(rope_base) * exponent)
    angles = time_rows.astype(jnp.float32)[:, None] * inverse[None, :]
    angles = jnp.concatenate([angles, angles], axis=1)
    return (jnp.cos(angles)[:, None, :], jnp.sin(angles)[:, None, :])


def rotate(values, cos_table, sin_table):
    half_dim = values.shape[-1] // 2
    turned = jnp.concatenate([-values[..., half_dim:], values[..., :half_dim]], axis=-1)
    return values * cos_table + turned * sin_table


def rotate_back(grad_vals, cos_table, sin_table):
    scaled = grad_vals * sin_table
    half_dim = grad_vals.shape[-1] // 2
    turned = jnp.concatenate([scaled[..., half_dim:], -scaled[..., :half_dim]], axis=-1)
    return grad_vals * cos_table + turned


def score_block(query_rows, key_rows, var_rows, var_all, key_valid, bias, score_scale):
    raw_scores = (
        jnp.einsum("qhd,khd->hqk", query_rows, key_rows, preferred_element_type=jnp.float32)
        * score_scale
    )
    same_var = var_rows[:, None] == var_all[None, :]
    raw_scores = raw_scores + jnp.where(
        same_var[None], bias[0][:, None, None], bias[1][:, None, None]
    )
    return (jnp.where(key_valid[None, None, :], raw_scores, masked_score), same_var)


def attend_forward(query, key_rows, values, var_all, key_valid, bias):
    length = query.shape[0]
    block_rows = min(512, length)
    score_scale = query.shape[-1] ** (-0.5)
    pieces = []
    lse_parts = []
    for row_start in range(0, length, block_rows):
        scores, same_var = score_block(
            query[row_start : row_start + block_rows],
            key_rows,
            var_all[row_start : row_start + block_rows],
            var_all,
            key_valid,
            bias,
            score_scale,
        )
        row_peak = jnp.max(scores, axis=2, keepdims=True)
        exp_scores = jnp.exp(scores - row_peak)
        row_total = jnp.sum(exp_scores, axis=2, keepdims=True)
        soft_probs = (exp_scores / row_total).astype(jnp.bfloat16)
        pieces.append(
            jnp.einsum("hqk,khd->qhd", soft_probs, values, preferred_element_type=jnp.float32)
        )
        lse_parts.append((row_peak + jnp.log(row_total))[:, :, 0])
    return (jnp.concatenate(pieces, axis=0), jnp.concatenate(lse_parts, axis=1))


def attend_backward(query, key_rows, values, var_all, key_valid, bias, log_sums, grad_attended):
    length = query.shape[0]
    block_rows = min(512, length)
    score_scale = query.shape[-1] ** (-0.5)
    d_keys = jnp.zeros(key_rows.shape, jnp.float32)
    d_values = jnp.zeros(values.shape, jnp.float32)
    d_bias = jnp.zeros((2, bias.shape[1]), jnp.float32)
    d_query_parts = []
    for row_start in range(0, length, block_rows):
        query_rows = query[row_start : row_start + block_rows]
        scores, same_var = score_block(
            query_rows,
            key_rows,
            var_all[row_start : row_start + block_rows],
            var_all,
            key_valid,
            bias,
            score_scale,
        )
        soft_probs = jnp.exp(scores - log_sums[:, row_start : row_start + block_rows][:, :, None])
        grad_block = grad_attended[row_start : row_start + block_rows]
        d_values = d_values + jnp.einsum(
            "hqk,qhd->khd",
            soft_probs.astype(jnp.bfloat16),
            grad_block,
            preferred_element_type=jnp.float32,
        )
        d_probs = jnp.einsum("qhd,khd->hqk", grad_block, values, preferred_element_type=jnp.float32)
        row_inner = jnp.sum(soft_probs * d_probs, axis=2, keepdims=True)
        d_scores = (soft_probs * (d_probs - row_inner)).astype(jnp.bfloat16)
        same_mask = same_var.astype(jnp.bfloat16)
        in_same = jnp.einsum("hqk,qk->h", d_scores, same_mask, preferred_element_type=jnp.float32)
        in_other = jnp.einsum(
            "hqk,qk->h", d_scores, 1.0 - same_mask, preferred_element_type=jnp.float32
        )
        d_bias = d_bias + jnp.stack([in_same, in_other])
        d_query_parts.append(
            jnp.einsum("hqk,khd->qhd", d_scores, key_rows, preferred_element_type=jnp.float32)
            * score_scale
        )
        d_keys = (
            d_keys
            + jnp.einsum("hqk,qhd->khd", d_scores, query_rows, preferred_element_type=jnp.float32)
            * score_scale
        )
    return (jnp.concatenate(d_query_parts, axis=0), d_keys, d_values, d_bias)


def shards(
    tokens,
    lengths,
    variate_ids,
    time_ids,
    attn_gain,
    w_qkv,
    attn_bias,
    w_out,
    ffn_gain,
    w_in,
    w_down,
    cotangent,
):
    seq_count, length = variate_ids.shape
    row_count = seq_count * length
    gain_one, qkv_weight, bias_full, out_weight, gain_two, in_weight, down_weight = (
        lax.all_gather(attn_gain, "shard", axis=0, tiled=True),
        lax.all_gather(w_qkv, "shard", axis=0, tiled=True),
        lax.all_gather(attn_bias, "shard", axis=1, tiled=True),
        lax.all_gather(w_out, "shard", axis=0, tiled=True),
        lax.all_gather(ffn_gain, "shard", axis=0, tiled=True),
        lax.all_gather(w_in, "shard", axis=0, tiled=True),
        lax.all_gather(w_down, "shard", axis=0, tiled=True),
    )
    positions = jnp.arange(length)
    key_valid = positions[None, :] < lengths[:, None]
    row_valid = key_valid.reshape(row_count, 1)
    cos_table, sin_table = rope_tables(time_ids.reshape(row_count), HEAD_DIM)
    inputs = tokens.astype(jnp.float32)
    inv_one = lax.rsqrt(jnp.mean(inputs * inputs, axis=1, keepdims=True) + norm_eps)
    normed_one = (inputs * inv_one * gain_one).astype(jnp.bfloat16)
    projected = jnp.dot(normed_one, qkv_weight, preferred_element_type=jnp.float32)
    shaped = projected.reshape(row_count, 3, HEADS, HEAD_DIM)
    query = rotate(shaped[:, 0], cos_table, sin_table).astype(jnp.bfloat16)
    key_rows = rotate(shaped[:, 1], cos_table, sin_table).astype(jnp.bfloat16)
    values = shaped[:, 2].astype(jnp.bfloat16)
    seq_shape = (seq_count, length, HEADS, HEAD_DIM)

    def forward_one(seq_items):
        one_query, one_keys, one_values, one_vars, one_valid = seq_items
        return attend_forward(one_query, one_keys, one_values, one_vars, one_valid, bias_full)

    attended, log_sums = lax.map(
        forward_one,
        (
            query.reshape(seq_shape),
            key_rows.reshape(seq_shape),
            values.reshape(seq_shape),
            variate_ids,
            key_valid,
        ),
    )
    attended_low = attended.reshape(row_count, D).astype(jnp.bfloat16)
    hidden = inputs + jnp.dot(attended_low, out_weight, preferred_element_type=jnp.float32)
    inv_two = lax.rsqrt(jnp.mean(hidden * hidden, axis=1, keepdims=True) + norm_eps)
    normed_two = (hidden * inv_two * gain_two).astype(jnp.bfloat16)
    gate_up = jnp.dot(normed_two, in_weight, preferred_element_type=jnp.float32)
    gate_part = gate_up[:, :FF]
    up_part = gate_up[:, FF:]
    sigmoid_gate = jax.nn.sigmoid(gate_part)
    swish_gate = gate_part * sigmoid_gate
    activated = (swish_gate * up_part).astype(jnp.bfloat16)
    result = (hidden + jnp.dot(activated, down_weight, preferred_element_type=jnp.float32)).astype(
        jnp.bfloat16
    )
    gain_one, qkv_weight, bias_full, out_weight, gain_two, in_weight, down_weight = (
        lax.all_gather(attn_gain, "shard", axis=0, tiled=True),
        lax.all_gather(w_qkv, "shard", axis=0, tiled=True),
        lax.all_gather(attn_bias, "shard", axis=1, tiled=True),
        lax.all_gather(w_out, "shard", axis=0, tiled=True),
        lax.all_gather(ffn_gain, "shard", axis=0, tiled=True),
        lax.all_gather(w_in, "shard", axis=0, tiled=True),
        lax.all_gather(w_down, "shard", axis=0, tiled=True),
    )
    grad_rows = jnp.where(row_valid, cotangent, jnp.zeros_like(cotangent))
    grad_down = contract_rows(activated, grad_rows)
    d_act = times_transpose(grad_rows, down_weight)
    d_gate = d_act * up_part * sigmoid_gate * (1.0 + gate_part * (1.0 - sigmoid_gate))
    d_up = d_act * swish_gate
    d_gate_up = jnp.concatenate([d_gate, d_up], axis=1).astype(jnp.bfloat16)
    grad_in = contract_rows(normed_two, d_gate_up)
    d_normed_two = times_transpose(d_gate_up, in_weight)
    unit_two = hidden * inv_two
    grad_gain_two = jnp.sum(d_normed_two * unit_two, axis=0)
    scaled_two = d_normed_two * gain_two
    d_hidden = grad_rows.astype(jnp.float32) + inv_two * (
        scaled_two - unit_two * jnp.mean(scaled_two * unit_two, axis=1, keepdims=True)
    )
    d_branch = d_hidden.astype(jnp.bfloat16)
    grad_out = contract_rows(attended_low, d_branch)
    d_attended = times_transpose(d_branch, out_weight).astype(jnp.bfloat16)

    def backward_one(seq_items):
        one_query, one_keys, one_values, one_vars, one_valid, one_sums, one_grad = seq_items
        return attend_backward(
            one_query, one_keys, one_values, one_vars, one_valid, bias_full, one_sums, one_grad
        )

    d_query, d_keys, d_values, d_bias_seq = lax.map(
        backward_one,
        (
            query.reshape(seq_shape),
            key_rows.reshape(seq_shape),
            values.reshape(seq_shape),
            variate_ids,
            key_valid,
            log_sums,
            d_attended.reshape(seq_shape),
        ),
    )
    grad_bias = jnp.sum(d_bias_seq, axis=0)
    d_query = rotate_back(d_query.reshape(row_count, HEADS, HEAD_DIM), cos_table, sin_table)
    d_keys = rotate_back(d_keys.reshape(row_count, HEADS, HEAD_DIM), cos_table, sin_table)
    d_projected = (
        jnp.stack([d_query, d_keys, d_values.reshape(row_count, HEADS, HEAD_DIM)], axis=1)
        .reshape(row_count, 3 * D)
        .astype(jnp.bfloat16)
    )
    grad_qkv = contract_rows(normed_one, d_projected)
    d_normed_one = times_transpose(d_projected, qkv_weight)
    unit_one = inputs * inv_one
    grad_gain_one = jnp.sum(d_normed_one * unit_one, axis=0)
    scaled_one = d_normed_one * gain_one
    grad_tokens = d_hidden + inv_one * (
        scaled_one - unit_one * jnp.mean(scaled_one * unit_one, axis=1, keepdims=True)
    )
    owned_grads = (
        lax.psum_scatter(
            grad_gain_one.astype(jnp.bfloat16), "shard", scatter_dimension=0, tiled=True
        ).astype(jnp.float32),
        lax.psum_scatter(
            grad_qkv.astype(jnp.bfloat16), "shard", scatter_dimension=0, tiled=True
        ).astype(jnp.float32),
        lax.psum_scatter(
            grad_bias.astype(jnp.bfloat16), "shard", scatter_dimension=1, tiled=True
        ).astype(jnp.float32),
        lax.psum_scatter(
            grad_out.astype(jnp.bfloat16), "shard", scatter_dimension=0, tiled=True
        ).astype(jnp.float32),
        lax.psum_scatter(
            grad_gain_two.astype(jnp.bfloat16), "shard", scatter_dimension=0, tiled=True
        ).astype(jnp.float32),
        lax.psum_scatter(
            grad_in.astype(jnp.bfloat16), "shard", scatter_dimension=0, tiled=True
        ).astype(jnp.float32),
        lax.psum_scatter(
            grad_down.astype(jnp.bfloat16), "shard", scatter_dimension=0, tiled=True
        ).astype(jnp.float32),
    )
    owned_grads = (
        lax.psum(owned_grads[0].astype(jnp.bfloat16), "rep").astype(jnp.float32),
        lax.psum(owned_grads[1].astype(jnp.bfloat16), "rep").astype(jnp.float32),
        lax.psum(owned_grads[2].astype(jnp.bfloat16), "rep").astype(jnp.float32),
        lax.psum(owned_grads[3].astype(jnp.bfloat16), "rep").astype(jnp.float32),
        lax.psum(owned_grads[4].astype(jnp.bfloat16), "rep").astype(jnp.float32),
        lax.psum(owned_grads[5].astype(jnp.bfloat16), "rep").astype(jnp.float32),
        lax.psum(owned_grads[6].astype(jnp.bfloat16), "rep").astype(jnp.float32),
    )
    sum_gain_one, sum_qkv, sum_bias, sum_out, sum_gain_two, sum_in, sum_down = owned_grads
    return (
        result,
        grad_tokens,
        sum_gain_one,
        sum_qkv,
        sum_bias,
        sum_out,
        sum_gain_two,
        sum_in,
        sum_down,
    )


def solution(mesh):
    placed = (
        P(("shard", "rep"), None),
        P(("shard", "rep")),
        P(("shard", "rep"), None),
        P(("shard", "rep"), None),
        P("shard"),
        P("shard", None),
        P(None, "shard"),
        P("shard", None),
        P("shard"),
        P("shard", None),
        P("shard", None),
        P(("shard", "rep"), None),
    )
    return jax.shard_map(
        shards,
        mesh=mesh,
        in_specs=placed,
        out_specs=(
            P(("shard", "rep"), None),
            P(("shard", "rep"), None),
            P("shard"),
            P("shard", None),
            P(None, "shard"),
            P("shard", None),
            P("shard"),
            P("shard", None),
            P("shard", None),
        ),
        check_vma=False,
    )
```

profile of v0, /device:TPU:1, one launch (start us, length us, event | category | flops | bytes accessed | tf_op | source)
XLA Modules:
  0.0 1461.6 jit_solution(17255788785433120697)
XLA Ops:
  16.3 18.1 %all-gather.1 = bf16[8,2,2]{2,1,0:T(2,128)(2,1)S(1)} all-gather(bf16[1,2,2]{2,1,0:T(2,128)(2,1)S(1)} %bitcast.162), channel_id=1, replica_groups=mesh['shard'=8,'rep'=4] {'shard'}, dimensions={0}, use_global_device_ids=true | all-gather | bytes 72 | tf_op jit(solution)/shard_map/all_gather | solution.py:157
  72.6 38.3 %all-gather.8.cloned.1.call-done = bf16[1024,3072]{1,0:T(8,128)(2,1)} async-done(((bf16[128,3072]{1,0:T(8,128)(2,1)}), bf16[1024,3072]{1,0:T(8,128)(2,1)}) %all-gather.8.cloned.1.call-update) | async-done | bytes 6291472 | tf_op jit(solution)/shard_map/all_gather | solution.py:156
  128.4 16.1 %fusion.76 = (f32[16,512]{1,0:T(8,128)S(1)}, f32[16,512,1024]{2,1,0:T(8,128)}) fusion(bf16[16]{0:T(256)(128)(2,1)S(1)} %get-tuple-element.158, bf16[16]{0:T(256)(128)(2,1)S(1)} %get-tuple-element.157, pred[512,1024]{1,0:T(8,128)(4,1)S(1)} %copy-done.27, bf16[1024,16,64]{0,2,1:T(8,128)(2,1)S(1)} %get-tuple-element.126, ...), kind=kOutput, calls=%fused_computation.151 | convolution fusion | flops 1124065280 | bytes 37259264 | tf_op jit(solution)/shard_map/while/body/eval_jaxpr/qhd,khd->hqk/dot_general | solution.py:53
  144.4 15.6 %fusion.77 = (f32[16,512]{1,0:T(8,128)S(1)}, f32[16,512,1024]{2,1,0:T(8,128)}) fusion(bf16[16]{0:T(256)(128)(2,1)S(1)} %get-tuple-element.158, bf16[16]{0:T(256)(128)(2,1)S(1)} %get-tuple-element.157, pred[512,1024]{1,0:T(8,128)(4,1)S(1)} %get-tuple-element.153, bf16[1024,16,64]{0,2,1:T(8,128)(2,1)S(1)} %get-tuple-element.126, ...), kind=kOutput, calls=%fused_computation.152 | convolution fusion | flops 1124065280 | bytes 37259264 | tf_op jit(solution)/shard_map/while/body/eval_jaxpr/qhd,khd->hqk/dot_general | solution.py:53
  160.1 15.9 %fusion.5 = f32[16,512]{1,0:T(8,128)S(1)} fusion(f32[16,512,1024]{2,1,0:T(8,128)} %get-tuple-element.160, f32[16,512]{1,0:T(8,128)S(1)} %get-tuple-element.159), kind=kLoop, calls=%fused_computation.21 | loop fusion | flops 16769024 | bytes 33619968 | tf_op jit(solution)/shard_map/while/body/eval_jaxpr/reduce_sum | solution.py:81
  190.0 25.0 %fusion.46 = bf16[512,16,64]{0,2,1:T(8,128)(2,1)S(1)} fusion(f32[16,512,1024]{2,1,0:T(8,128)} %get-tuple-element.160, f32[16,512]{1,0:T(8,128)S(1)} %fusion.5, f32[16,512]{1,0:T(8,128)S(1)} %get-tuple-element.159, f32[1024,3,16,64]{0,3,2,1:T(8,128)} %bitcast.123), kind=kOutput, calls=%fused_computation.103 | convolution fusion | flops 1099431936 | bytes 36765696 | tf_op jit(solution)/shard_map/while/body/eval_jaxpr/hqk,khd->qhd/dot_general | solution.py:84
  237.9 151.1 %all-gather.12.cloned.1.call-done = bf16[1024,8192]{1,0:T(8,128)(2,1)} async-done(((bf16[128,8192]{1,0:T(8,128)(2,1)}), bf16[1024,8192]{1,0:T(8,128)(2,1)}) %all-gather.12.cloned.1.call-update) | async-done | bytes 16777232 | tf_op jit(solution)/shard_map/all_gather | solution.py:160
  389.0 28.6 %fusion.72 = f32[1024,8192]{1,0:T(8,128)} fusion(bf16[1024,8192]{1,0:T(8,128)(2,1)} %all-gather.12.cloned.1.call-done, f32[1024,1024]{0,1:T(8,128)} %get-tuple-element.164, f32[1024]{0:T(1024)S(1)} %bitcast.151, f32[1024]{0:T(1024)S(1)} %add_rsqrt_fusion), kind=kOutput, calls=%fused_computation.147 | convolution fusion | flops 17183014912 | bytes 54534144 | tf_op jit(solution)/shard_map/dot_general | solution.py:195
  417.6 96.5 %all-gather.14.cloned.1.call-done = bf16[4096,1024]{1,0:T(8,128)(2,1)} async-done(((bf16[512,1024]{1,0:T(8,128)(2,1)}), bf16[4096,1024]{1,0:T(8,128)(2,1)}) %all-gather.14.cloned.1.call-update) | async-done | bytes 8388624 | tf_op jit(solution)/shard_map/all_gather | solution.py:161
  514.1 27.9 %multiply_convert_fusion.3 = (bf16[1024,4096]{1,0:T(8,128)(2,1)}, bf16[1024,4096]{1,0:T(8,128)(2,1)}, bf16[1024,4096]{1,0:T(8,128)(2,1)}) fusion(f32[1024,8192]{1,0:T(8,128)} %fusion.72, bf16[4096,1024]{1,0:T(8,128)(2,1)} %all-gather.14.cloned.1.call-done, bf16[1024,1024]{0,1:T(8,128)(2,1)S(1)} %copy-done.11, pred[1024]{0:T(1024)(128)(4,1)S(1)} %copy-done.44), kind=kOutput, calls=%fused_computation.30 | convolution fusion | flops 8653897728 | bytes 69207040 | tf_op jit(solution)/shard_map/dot_general | solution.py:24
  542.0 27.9 %multiply_reduce_fusion.2 = (bf16[1024]{0:T(1024)(128)(2,1)}, f32[1024]{0:T(1024)S(1)}, f32[1024,1024]{0,1:T(8,128)}) fusion(f32[1024,1024]{0,1:T(8,128)} %get-tuple-element.164, f32[1024]{0:T(1024)S(1)} %add_rsqrt_fusion, f32[1024]{0:T(1024)S(1)} %bitcast.152, bf16[1024,8192]{1,0:T(8,128)(2,1)} %all-gather.12.cloned.1.call-done, ...), kind=kOutput, calls=%fused_computation.72 | convolution fusion | flops 17219715072 | bytes 41957376 | tf_op jit(solution)/shard_map/dot_general | solution.py:24
  585.8 15.5 %fusion.8 = f32[16,64,1024]{2,1,0:T(8,128)} fusion(bf16[512,16,64]{0,2,1:T(8,128)(2,1)S(1)} %bitcast.133, f32[16,512,1024]{2,1,0:T(8,128)} %get-tuple-element.160, f32[16,512]{1,0:T(8,128)S(1)} %log_add_fusion), kind=kOutput, calls=%fused_computation.24 | convolution fusion | flops 1090519040 | bytes 38830080 | tf_op jit(solution)/shard_map/while/body/eval_jaxpr/hqk,qhd->khd/dot_general | solution.py:111
  601.3 25.0 %multiply_reduce_fusion = (f32[16,512]{1,0:T(8,128)S(1)}, f32[16,512,1024]{2,1,0:T(8,128)}) fusion(f32[16,512,1024]{2,1,0:T(8,128)} %get-tuple-element.160, f32[16,512]{1,0:T(8,128)S(1)} %log_add_fusion, bf16[512,16,64]{0,2,1:T(8,128)(2,1)} %bitcast.134, f32[1024,3,16,64]{0,3,2,1:T(8,128)} %bitcast.124), kind=kOutput, calls=%fused_computation.9 | convolution fusion | flops 1098899456 | bytes 70320128 | tf_op jit(solution)/shard_map/while/body/eval_jaxpr/qhd,khd->hqk/dot_general | solution.py:117
  626.3 24.1 %multiply_reduce_fusion.1 = (f32[16,512]{1,0:T(8,128)S(1)}, f32[16,512,1024]{2,1,0:T(8,128)}) fusion(f32[16,512,1024]{2,1,0:T(8,128)} %get-tuple-element.162, f32[16,512]{1,0:T(8,128)S(1)} %copy-done.25, bf16[512,16,64]{0,2,1:T(8,128)(2,1)} %bitcast.131, f32[1024,3,16,64]{0,3,2,1:T(8,128)S(1)} %bitcast.130), kind=kOutput, calls=%fused_computation.12 | convolution fusion | flops 1098899456 | bytes 70320128 | tf_op jit(solution)/shard_map/while/body/eval_jaxpr/qhd,khd->hqk/dot_general | solution.py:117
  650.4 58.0 %fusion = (f32[16]{0:T(128)}, f32[16]{0:T(128)}, bf16[16,512,1024]{2,1,0:T(8,128)(2,1)}, f32[16]{0:T(128)}, f32[16]{0:T(128)}, /*index=5*/bf16[16,512,1024]{2,1,0:T(8,128)(2,1)}) fusion(f32[1024,512]{0,1:T(8,128)} %get-tuple-element.154, f32[1024,512]{0,1:T(8,128)} %get-tuple-element.152, f32[16,512,1024]{2,1,0:T(8,128)} %get-tuple-element.167, ...), kind=kLoop, calls=%fused_computation.4 | loop fusion | flops 150994880 | bytes 176292096 | tf_op jit(solution)/shard_map/while/body/eval_jaxpr/hqk,qk->h/dot_general | solution.py:121
  766.0 16.8 %fusion.36 = bf16[1024,1,16,64]{0,3,2,1:T(8,128)(2,1)} fusion(f32[16,64,1024]{2,1,0:T(8,128)} %fusion.8, bf16[512,16,64]{0,2,1:T(8,128)(2,1)S(1)} %bitcast.132, f32[16,512,1024]{2,1,0:T(8,128)} %get-tuple-element.162, f32[16,512]{1,0:T(8,128)S(1)} %copy-done.25), kind=kOutput, calls=%fused_computation.80 | convolution fusion | flops 1092616192 | bytes 40927232 | tf_op jit(solution)/shard_map/while/body/eval_jaxpr/hqk,qhd->khd/dot_general | solution.py:111
  798.9 15.0 %convolution_convert_fusion.1 = bf16[4096,1024]{1,0:T(8,128)(2,1)} fusion(bf16[1024,4096]{1,0:T(8,128)(2,1)} %get-tuple-element.124, bf16[1024,1024]{0,1:T(8,128)(2,1)} %copy.52, pred[1024]{0:T(1024)(128)(4,1)S(1)} %copy-done.45), kind=kOutput, calls=%fused_computation.38 | convolution fusion | flops 8595177472 | bytes 18875392 | tf_op jit(solution)/shard_map/dot_general | solution.py:18
  814.7 25.5 %convolution_convert_fusion = bf16[1024,8192]{1,0:T(8,128)(2,1)} fusion(bf16[1024,4096]{1,0:T(8,128)(2,1)} %get-tuple-element.123, bf16[1024,4096]{1,0:T(8,128)(2,1)} %get-tuple-element.122, f32[1024,1024]{0,1:T(8,128)} %get-tuple-element.164, f32[1024]{0:T(1024)S(1)} %bitcast.154, f32[1024]{0:T(1024)S(1)} %copy-done.36), kind=kOutput, calls=%fused_computation.36 | convolution fusion | flops 17224957952 | bytes 37756928 | tf_op jit(solution)/shard_map/dot_general | solution.py:18
  842.7 15.4 %add_convert_fusion.1 = bf16[1024,1024]{0,1:T(8,128)(2,1)} fusion(f32[1024,1024]{0,1:T(8,128)} %get-tuple-element.164, bf16[1024,4096]{1,0:T(8,128)(2,1)} %get-tuple-element.124, bf16[4096,1024]{1,0:T(8,128)(2,1)} %all-gather.14.cloned.1.call-done), kind=kOutput, calls=%fused_computation.76 | convolution fusion | flops 8592031744 | bytes 23068672 | tf_op jit(solution)/shard_map/dot_general | solution.py:201
  862.2 56.8 %reduce-scatter.6.cloned.1.call-done = bf16[128,3072]{1,0:T(8,128)(2,1)} async-done(((bf16[1024,3072]{1,0:T(8,128)(2,1)}), bf16[128,3072]{1,0:T(8,128)(2,1)}) %reduce-scatter.6.cloned.1.call-update) | async-done | bytes 786448 | tf_op jit(solution)/shard_map/reduce_scatter | solution.py:269
  919.0 152.7 %reduce-scatter.12.cloned.1.call-done = bf16[512,1024]{1,0:T(8,128)(2,1)} async-done(((bf16[4096,1024]{1,0:T(8,128)(2,1)}), bf16[512,1024]{1,0:T(8,128)(2,1)}) %reduce-scatter.12.cloned.1.call-update) | async-done | bytes 1048592 | tf_op jit(solution)/shard_map/reduce_scatter | solution.py:284
  1071.7 285.9 %reduce-scatter.10.cloned.1.call-done = bf16[128,8192]{1,0:T(8,128)(2,1)} async-done(((bf16[1024,8192]{1,0:T(8,128)(2,1)}), bf16[128,8192]{1,0:T(8,128)(2,1)}) %reduce-scatter.10.cloned.1.call-update) | async-done | bytes 2097168 | tf_op jit(solution)/shard_map/reduce_scatter | solution.py:281
  1369.9 16.2 %all-reduce.3 = (bf16[1024]{0:T(1024)(128)(2,1)S(1)}, bf16[2,16]{1,0:T(2,128)(2,1)S(1)}, bf16[1024]{0:T(1024)(128)(2,1)S(1)}) all-reduce(bf16[1024]{0:T(1024)(128)(2,1)S(1)} %get-tuple-element.108, bf16[2,16]{1,0:T(2,128)(2,1)S(1)} %fusion.67, bf16[1024]{0:T(1024)(128)(2,1)S(1)} %copy-done.42), channel_id=2, replica_groups=mesh['shard'=8,'rep'=4] {'shard'}, use_global_device_ids=true, to_apply=%region_11.12.clone | all-reduce | flops 2080 | bytes 8320
  1409.4 35.9 %all-reduce.8.cloned.1.call-done = (bf16[128,3072]{1,0:T(8,128)(2,1)}, bf16[128,1024]{1,0:T(8,128)(2,1)}, bf16[128,8192]{1,0:T(8,128)(2,1)}, bf16[512,1024]{1,0:T(8,128)(2,1)}) async-done(((bf16[128,3072]{1,0:T(8,128)(2,1)}, bf16[128,1024]{1,0:T(8,128)(2,1)}, bf16[128,8192]{1,0:T(8,128)(2,1)}, bf16[512,1024]{1,0:T(8,128)(2,1)}), (bf16[128,3072]{1,0:T(8,128)(2,1)}, bf16[128,1024]{1,0:T(8,128)(2,1)}, ...) | async-done | bytes 4194320 | tf_op jit(solution)/shard_map/psum | solution.py:290
  (201 shorter events, 241.2 us)
Async XLA Ops:
  7.2 103.7 %all-gather.8.cloned.1.call-start = ((), (), s32[]{:S(2)}) async-start(), calls=%async_computation.4 | async-start | bytes 7077888 | tf_op jit(solution)/shard_map/all_gather | solution.py:156
  7.9 221.7 %all-gather.10.cloned.1.call-start = ((), (), s32[]{:S(2)}) async-start(), calls=%async_computation.5 | async-start | bytes 2359296 | tf_op jit(solution)/shard_map/all_gather | solution.py:158
  8.7 380.3 %all-gather.12.cloned.1.call-start = ((), (), s32[]{:S(2)}) async-start(), calls=%async_computation.6 | async-start | bytes 18874368 | tf_op jit(solution)/shard_map/all_gather | solution.py:160
  9.4 504.7 %all-gather.14.cloned.1.call-start = ((), (), s32[]{:S(2)}) async-start(), calls=%async_computation.7 | async-start | bytes 9437184 | tf_op jit(solution)/shard_map/all_gather | solution.py:161
  10.0 852.2 %reduce-scatter.8.cloned.1.call-start = ((), (), s32[]{:S(2)}) async-start(), calls=%async_computation.9 | async-start | bytes 2359296 | tf_op jit(solution)/shard_map/reduce_scatter | solution.py:275
  10.1 37.3 %copy-start.47 = (bf16[128]{0:T(256)(128)(2,1)S(1)}, bf16[128]{0:T(256)(128)(2,1)}, u32[]{:S(2)}) copy-start(bf16[128]{0:T(256)(128)(2,1)} %param.20) | copy-start | bytes 772
  16.1 128.3 %copy-start.43 = (pred[1024]{0:T(1024)(128)(4,1)}, pred[1024]{0:T(1024)(128)(4,1)S(1)}, u32[]{:S(2)}) copy-start(pred[1024]{0:T(1024)(128)(4,1)S(1)} %iota_compare_fusion) | copy-start | bytes 3076
  47.4 63.5 %copy-start.29 = (f32[8,1,128]{2,1,0:T(1,128)}, f32[8,1,128]{2,1,0:T(1,128)S(1)}, u32[]{:S(2)}) copy-start(f32[8,1,128]{2,1,0:T(1,128)S(1)} %convert_element_type.210) | copy-start | bytes 12292
  64.8 58.1 %copy-start.19 = (f32[1024,64]{0,1:T(8,128)}, f32[1024,64]{0,1:T(8,128)S(1)}, u32[]{:S(2)}) copy-start(f32[1024,64]{0,1:T(8,128)S(1)} %get-tuple-element.145) | copy-start | bytes 786436
  64.8 58.1 %copy-start.21 = (f32[1024,64]{0,1:T(8,128)}, f32[1024,64]{0,1:T(8,128)S(1)}, u32[]{:S(2)}) copy-start(f32[1024,64]{0,1:T(8,128)S(1)} %get-tuple-element.146) | copy-start | bytes 786436
  67.9 52.4 %copy-start.2 = (bf16[1024,1024]{0,1:T(8,128)(2,1)}, bf16[1024,1024]{0,1:T(8,128)(2,1)S(1)}, u32[]{:S(2)}) copy-start(bf16[1024,1024]{0,1:T(8,128)(2,1)S(1)} %copy.47) | copy-start | bytes 6291460
  68.4 51.9 %copy-start.31 = (f32[1024]{0:T(1024)}, f32[1024]{0:T(1024)S(1)}, u32[]{:S(2)}) copy-start(f32[1024]{0:T(1024)S(1)} %add_rsqrt_fusion.1) | copy-start | bytes 12292
  182.4 32.6 %slice-start = ((s8[12582912]{0:T(1024)(128)(4,1)}), s8[4194304]{0:T(1024)(128)(4,1)S(1)}, s32[]{:S(2)}) async-start(s8[12582912]{0:T(1024)(128)(4,1)} %bitcast.125), calls=%async_computation.13 | async-start | bytes 8388608
  190.0 25.0 %slice-start.1 = ((s8[12582912]{0:T(1024)(128)(4,1)}), s8[4194304]{0:T(1024)(128)(4,1)S(1)}, s32[]{:S(2)}) async-start(s8[12582912]{0:T(1024)(128)(4,1)} %bitcast.125), calls=%async_computation.14 | async-start | bytes 8388608
  230.4 158.5 %copy-start.33 = (f32[8,1,128]{2,1,0:T(1,128)S(1)}, f32[8,1,128]{2,1,0:T(1,128)}, u32[]{:S(2)}) copy-start(f32[8,1,128]{2,1,0:T(1,128)} %convert_element_type.211) | copy-start | bytes 12292
  237.2 332.7 %copy-start.35 = (f32[1024]{0:T(1024)}, f32[1024]{0:T(1024)S(1)}, u32[]{:S(2)}) copy-start(f32[1024]{0:T(1024)S(1)} %add_rsqrt_fusion) | copy-start | bytes 12292
  389.0 125.1 %copy-start.11 = (bf16[1024,1024]{0,1:T(8,128)(2,1)S(1)}, bf16[1024,1024]{0,1:T(8,128)(2,1)}, u32[]{:S(2)}) copy-start(bf16[1024,1024]{0,1:T(8,128)(2,1)} %copy.52) | copy-start | bytes 6291460
  389.0 125.1 %copy-start.44 = (pred[1024]{0:T(1024)(128)(4,1)S(1)}, pred[1024]{0:T(1024)(128)(4,1)}, u32[]{:S(2)}) copy-start(pred[1024]{0:T(1024)(128)(4,1)} %copy-done.43) | copy-start | bytes 3076
  542.0 27.9 %copy-start.17 = (f32[1024,1024]{0,1:T(8,128)S(1)}, f32[1024,1024]{0,1:T(8,128)}, u32[]{:S(2)}) copy-start(f32[1024,1024]{0,1:T(8,128)} %get-tuple-element.164) | copy-start | bytes 12582916
  585.8 40.5 %slice-start.3 = ((s8[12582912]{0:T(1024)(128)(4,1)}), s8[4194304]{0:T(1024)(128)(4,1)S(1)}, s32[]{:S(2)}) async-start(s8[12582912]{0:T(1024)(128)(4,1)} %bitcast.128), calls=%async_computation.16 | async-start | bytes 8388608
  732.8 186.2 %reduce-scatter.6.cloned.1.call-start = ((), (), s32[]{:S(2)}) async-start(), calls=%async_computation.8 | async-start | bytes 7077888 | tf_op jit(solution)/shard_map/reduce_scatter | solution.py:269
  798.3 273.4 %reduce-scatter.12.cloned.1.call-start = ((), (), s32[]{:S(2)}) async-start(), calls=%async_computation.11 | async-start | bytes 9437184 | tf_op jit(solution)/shard_map/reduce_scatter | solution.py:284
  814.0 543.6 %reduce-scatter.10.cloned.1.call-start = ((), (), s32[]{:S(2)}) async-start(), calls=%async_computation.10 | async-start | bytes 18874368 | tf_op jit(solution)/shard_map/reduce_scatter | solution.py:281
  840.1 605.1 %all-reduce.8.cloned.1.call-start = ((), (), s32[]{:S(2)}) async-start(), calls=%async_computation.12 | async-start | bytes 8388608 | tf_op jit(solution)/shard_map/psum | solution.py:290
  (42 other events, 337.8 us)
Sparse Core Ops, SparseCore 0:
  10.2 100.6 all-gather.7
  113.1 46.8 all-gather.9
  162.1 226.7 all-gather.11
  390.9 123.1 all-gather.13
  732.9 64.8 reduce-scatter.7
  801.2 117.7 reduce-scatter.5
  922.6 149.0 reduce-scatter.11
  1075.9 281.6 reduce-scatter.9
  1360.2 85.0 all-reduce.7
where the time goes:
time: 1470 us; the launch traced here: 1460 us
  waiting for transfers between devices  820 us (56%)
  matrix products  385 us (26%)
  other arithmetic  127 us (9%)
  blocking collectives  71.7 us (5%)
  local copies, waits for them, and re-layouts  41 us (3%)
  between operations  16.6 us (1%)
    reduce_scatter x1, waiting for transfers between devices, shards(): lax.psum_scatter(grad_in.astype(jnp.bfloat16), 'shard', scatter_dimension...  286 us
    reduce_scatter x1, waiting for transfers between devices, shards(): lax.psum_scatter(grad_down.astype(jnp.bfloat16), 'shard', scatter_dimensi...  153 us
    all_gather x1, waiting for transfers between devices, shards(): lax.all_gather(w_in, 'shard', axis=0, tiled=True)  151 us
    all_gather x1, waiting for transfers between devices, shards(): lax.all_gather(w_down, 'shard', axis=0, tiled=True)  96.5 us
    dot_general x4, matrix products, times_transpose(): lax.dot_general(first_op, second_op, (((1,), (1,)), ((), ())), preferred_...  72.6 us
    dot_general x1, other arithmetic, attend_backward(): jnp.einsum('hqk,qk->h', d_scores, same_mask, preferred_element_type=jnp.f...  58 us
    reduce_scatter x1, waiting for transfers between devices, shards(): lax.psum_scatter(grad_qkv.astype(jnp.bfloat16), 'shard', scatter_dimensio...  56.8 us
    dot_general x4, matrix products, contract_rows(): lax.dot_general(first_op, second_op, (((0,), (0,)), ((), ())), preferred_...  53 us
  transfers between devices with their start and end apart: 9, of which 7 were waited for; matrix products, arithmetic and copies ran while one was open for 21% of the time, Pallas kernels for 0%

commit v1 on v0

--- a/solution.py
+++ b/solution.py
@@ -1,6 +1,10 @@
+import functools
+
 import jax
 import jax.numpy as jnp
 from jax import lax
+from jax.experimental import pallas as pl
+from jax.experimental.pallas import tpu as pltpu
 from jax.sharding import PartitionSpec as P
 
 D = 1024
@@ -12,6 +16,486 @@
 norm_eps = 1e-06
 rope_base = 10000.0
 masked_score = -1000000000.0
+
+
+MESH = pl.DeviceIdType.MESH
+ANY = pl.BlockSpec(memory_space=pl.ANY)
+
+
+class Net:
+    def __init__(self, line):
+        shard, rep = lax.axis_index("shard"), lax.axis_index("rep")
+        self.line = line
+        self.z, self.y = shard // 2, shard % 2
+        self.x, self.core = rep // 2, rep % 2
+        self.own = shard
+        self.sibling = (shard, self.x * 2 + 1 - self.core)
+        self.across_x = (shard, (1 - self.x) * 2 + self.core)
+        self.across_y = (self.z * 2 + 1 - self.y, rep)
+        self.above = (jnp.minimum(self.z + 1, line - 1) * 2 + self.y, rep)
+        self.below = (jnp.maximum(self.z - 1, 0) * 2 + self.y, rep)
+        self.has_above = self.z < line - 1
+        self.has_below = self.z > 0
+
+    def greet(self):
+        barrier = pltpu.get_barrier_semaphore()
+
+        def hail(partner):
+            pl.semaphore_signal(barrier, inc=1, device_id=partner, device_id_type=MESH)
+
+        for partner in (self.sibling, self.across_x, self.across_y):
+            hail(partner)
+        pl.when(self.has_above)(lambda: hail(self.above))
+        pl.when(self.has_below)(lambda: hail(self.below))
+        neighbours = jnp.where(self.has_above, 1, 0) + jnp.where(self.has_below, 1, 0)
+        pl.semaphore_wait(barrier, 3 + neighbours)
+
+
+def aligned(value, step):
+    return pl.multiple_of(value, step)
+
+
+def gather_count(line):
+    return 2 * line + 3 * 2 * line
+
+
+def gather_steps(net, source, full, local_sem, send_sem, recv_sem):
+    line = net.line
+    half, columns = source.shape[0] // 2, source.shape[1]
+    split = columns % 1024 == 0
+    only = columns * 3 // 8 if split else 0
+    shared = columns - 2 * only
+    rows = pl.ds(aligned(net.core * half, half), half)
+    carried = pl.ds(aligned(net.x * only, 128), only + shared) if split else pl.ds(0, columns)
+    lone = pl.ds(aligned(net.x * (only + shared), 128), only) if split else None
+
+    def remote(origin, landing, index, target):
+        return pltpu.make_async_remote_copy(
+            src_ref=origin,
+            dst_ref=landing,
+            send_sem=send_sem.at[index],
+            recv_sem=recv_sem.at[index],
+            device_id=target,
+            device_id_type=MESH,
+        )
+
+    def piece(z, y):
+        return full.at[z * 2 + y, rows, carried]
+
+    def over_z(z, target, base):
+        return remote(piece(z, net.y), piece(z, net.y), base + z, target)
+
+    def over_y(z):
+        return remote(piece(z, net.y), piece(z, net.y), 2 * line + z, net.across_y)
+
+    def over_x(z, y):
+        part = full.at[z * 2 + y, rows, lone]
+        return remote(part, part, 3 * line + y * line + z, net.across_x)
+
+    def to_core(z, y):
+        part = full.at[z * 2 + y, rows]
+        return remote(part, part, 5 * line + y * line + z, net.sibling)
+
+    mine = source.at[rows, carried]
+    local = pltpu.make_async_copy(source, full.at[net.own], local_sem)
+    first_y = remote(mine, piece(net.z, net.y), 2 * line + net.z, net.across_y)
+    first_up = remote(mine, piece(net.z, net.y), net.z, net.above)
+    first_down = remote(mine, piece(net.z, net.y), line + net.z, net.below)
+
+    def onward(z, y):
+        if split:
+            over_x(z, y).start()
+        else:
+            to_core(z, y).start()
+
+    def start():
+        first_y.start()
+        pl.when(net.has_above)(first_up.start)
+        pl.when(net.has_below)(first_down.start)
+        local.start()
+
+    def arrive(hops):
+        @pl.when(net.z >= hops)
+        def _():
+            z = net.z - hops
+            over_z(z, net.above, 0).wait_recv()
+            pl.when(net.has_above)(over_z(z, net.above, 0).start)
+            over_y(z).start()
+            onward(z, net.y)
+
+        @pl.when(net.z < line - hops)
+        def _():
+            z = net.z + hops
+            over_z(z, net.below, line).wait_recv()
+            pl.when(net.has_below)(over_z(z, net.below, line).start)
+            over_y(z).start()
+            onward(z, net.y)
+
+    def arrive_y(hops):
+        def one(z):
+            remote(piece(z, 1 - net.y), piece(z, 1 - net.y), 2 * line + z, net.across_y).wait_recv()
+            onward(z, 1 - net.y)
+
+        if hops == 0:
+            one(net.z)
+        else:
+            pl.when(net.z >= hops)(lambda: one(net.z - hops))
+            pl.when(net.z < line - hops)(lambda: one(net.z + hops))
+
+    def arrive_x(hops, own_y):
+        def one(z):
+            y = net.y if own_y else 1 - net.y
+            part = full.at[z * 2 + y, rows, pl.ds(aligned((1 - net.x) * (only + shared), 128), only)]
+            remote(part, part, 3 * line + y * line + z, net.across_x).wait_recv()
+            to_core(z, y).start()
+
+        if not split:
+            return
+        if hops == 0:
+            one(net.z)
+        else:
+            pl.when(net.z >= hops)(lambda: one(net.z - hops))
+            pl.when(net.z < line - hops)(lambda: one(net.z + hops))
+
+    def step(hops):
+        def run():
+            arrive_y(hops - 1)
+            if hops < line:
+                arrive(hops)
+            if hops >= 2:
+                arrive_x(hops - 2, False)
+                arrive_x(hops - 1, True)
+
+        return run
+
+    def last():
+        arrive_x(line - 1, False)
+
+    def finish():
+        local.wait()
+        first_y.wait_send()
+
+        @pl.when(net.has_above)
+        def _():
+            first_up.wait_send()
+            for hops in range(1, line - 1):
+                pl.when(net.z >= hops)(over_z(net.z - hops, net.above, 0).wait_send)
+
+        @pl.when(net.has_below)
+        def _():
+            first_down.wait_send()
+            for hops in range(1, line - 1):
+                pl.when(net.z < line - hops)(over_z(net.z + hops, net.below, line).wait_send)
+
+        for z in range(line):
+
+            def others():
+                over_y(z).wait_send()
+                if split:
+                    over_x(z, net.y).wait_send()
+                to_core(z, net.y).wait()
+
+            pl.when(net.z != z)(others)
+            if split:
+                over_x(z, 1 - net.y).wait_send()
+            to_core(z, 1 - net.y).wait()
+
+    return [start] + [step(hops) for hops in range(1, line + 1)] + [last, finish]
+
+
+def gather_scratch(line, tensors):
+    copies = gather_count(line)
+    return [
+        pltpu.SemaphoreType.DMA((tensors,)),
+        pltpu.SemaphoreType.DMA((tensors, copies)),
+        pltpu.SemaphoreType.DMA((tensors, copies)),
+    ]
+
+
+REDUCE_BUFFERS = 9
+
+
+def reduce_split(columns):
+    only = columns // 4 if columns % 512 == 0 else 0
+    return only, columns - 2 * only
+
+
+def reduce_scratch(line, shards, half, columns, dtype):
+    only, shared = reduce_split(columns)
+    carried = only + shared
+    return [
+        pltpu.VMEM((shards, half, columns), dtype),
+        pltpu.VMEM((shards, half, columns), dtype),
+        pltpu.VMEM((shards, half, max(only, 128)), dtype),
+        pltpu.VMEM((line, half, carried), dtype),
+        pltpu.VMEM((line + 1, half, carried), dtype),
+        pltpu.VMEM((half, carried), dtype),
+        pltpu.VMEM((half, columns), dtype),
+        pltpu.VMEM((half, columns), dtype),
+        pltpu.VMEM((2 * half, columns), jnp.float32),
+    ]
+
+
+def reduce_count(line):
+    return 3 * line + 4
+
+
+def reduce_steps(net, grad, out, column_start, buffers, local_sem, send_sem, recv_sem):
+    kept, got, from_x, from_y, from_z, late_x, final, swapped, wide = buffers
+    line = net.line
+    shards, half, width = kept.shape
+    only, shared = reduce_split(width)
+    both = only + shared
+    columns = pl.ds(column_start, width)
+    mine = pl.ds(aligned(net.core * half, half), half)
+    theirs = pl.ds(aligned((1 - net.core) * half, half), half)
+    if only:
+        carried = pl.ds(aligned(net.x * only, 128), both)
+        lone = pl.ds(aligned(net.x * both, 128), only)
+        their_lone = pl.ds(aligned((1 - net.x) * both, 128), only)
+    else:
+        carried = pl.ds(0, width)
+    middle = pl.ds(only, shared)
+
+    def remote(origin, landing, index, target):
+        return pltpu.make_async_remote_copy(
+            src_ref=origin,
+            dst_ref=landing,
+            send_sem=send_sem.at[index],
+            recv_sem=recv_sem.at[index],
+            device_id=target,
+            device_id_type=MESH,
+        )
+
+    local = pltpu.make_async_copy(grad.at[:, mine, columns], kept, local_sem.at[0])
+    halves = remote(grad.at[:, theirs, columns], got, 2 * line, net.sibling)
+    written = pltpu.make_async_copy(wide, out.at[:, columns], local_sem.at[1])
+    to_core = remote(final, swapped, 2 * line + 1, net.sibling)
+    end_x = remote(kept.at[net.own, :, carried], late_x, 2 * line + 2, net.across_x)
+    if only:
+        over_x = remote(kept.at[:, :, their_lone], from_x, 2 * line + 3, net.across_x)
+
+    def over_y(z):
+        part = kept.at[z * 2 + 1 - net.y, :, carried]
+        return remote(part, from_y.at[z], 2 * line + 4 + z, net.across_y)
+
+    def up(z):
+        return remote(kept.at[z * 2 + net.y, :, carried], from_z.at[z + 1], z, net.above)
+
+    def down(z):
+        return remote(kept.at[z * 2 + net.y, :, carried], from_z.at[z], line + z, net.below)
+
+    def add(shard, part):
+        kept[shard, :, carried] = kept[shard, :, carried] + part
+
+    def first():
+        halves.start()
+        local.start()
+
+    def second():
+        local.wait()
+        halves.wait_recv()
+
+        @pl.loop(0, shards)
+        def _(shard):
+            kept[shard] = kept[shard] + got[shard]
+
+        if only:
+            over_x.start()
+
+    def third():
+        if only:
+            over_x.wait_recv()
+
+            @pl.loop(0, shards)
+            def _(shard):
+                kept[shard, :, lone] = kept[shard, :, lone] + from_x[shard]
+
+        for z in range(line):
+            over_y(z).start()
+
+    def fourth():
+        for z in range(line):
+            over_y(z).wait_recv()
+
+        @pl.loop(0, line)
+        def _(z):
+            add(z * 2 + net.y, from_y[z])
+
+    def hop(step):
+        def run():
+            @pl.when(net.z == step)
+            def _():
+                for z in range(line - 1, step, -1):
+                    if step > 0:
+                        up(z).wait_recv()
+                        add(z * 2 + net.y, from_z[z + 1])
+                    up(z).start()
+
+            @pl.when(net.z == line - 1 - step)
+            def _():
+                for z in range(line - 1 - step):
+                    if step > 0:
+                        down(z).wait_recv()
+                        add(z * 2 + net.y, from_z[z])
+                    down(z).start()
+
+        return run
+
+    def land():
+        @pl.when(net.has_below)
+        def _():
+            up(net.z).wait_recv()
+            add(net.own, from_z[net.z + 1])
+
+        @pl.when(net.has_above)
+        def _():
+            down(net.z).wait_recv()
+            add(net.own, from_z[net.z])
+
+        end_x.start()
+
+    def meet():
+        end_x.wait_recv()
+        if only:
+            final[:, lone] = kept[net.own, :, lone]
+            for x in range(2):
+
+                @pl.when(net.x == x)
+                def _():
+                    start = 0 if x == 1 else shared
+                    final[:, (1 - x) * both : (1 - x) * both + only] = late_x[:, start : start + only]
+                    other = shared * 0 + (only if x == 1 else 0)
+                    final[:, only:both] = kept[net.own, :, only:both] + late_x[:, other : other + shared]
+        else:
+            final[...] = kept[net.own] + late_x[...]
+        to_core.start()
+        wide[mine, :] = final[...].astype(jnp.float32)
+
+    def swap():
+        to_core.wait_recv()
+        wide[theirs, :] = swapped[...].astype(jnp.float32)
+        written.start()
+
+    def finish():
+        written.wait()
+        halves.wait_send()
+        if only:
+            over_x.wait_send()
+        for z in range(line):
+            over_y(z).wait_send()
+            pl.when(net.z < z)(up(z).wait_send)
+            pl.when(net.z > z)(down(z).wait_send)
+        end_x.wait_send()
+        to_core.wait_send()
+
+    hops = [hop(step) for step in range(line - 1)]
+
+    def fourth_and_hop():
+        fourth()
+        hops[0]()
+
+    return [first, second, third, fourth_and_hop] + hops[1:] + [land, meet, swap, finish]
+
+
+def staggered(step_lists, gap=1):
+    ticks = (len(step_lists) - 1) * gap + max(len(steps) for steps in step_lists)
+    out = []
+    for tick in range(ticks):
+        row = []
+        for index, steps in enumerate(step_lists):
+            at = tick - index * gap
+            if 0 <= at < len(steps):
+                row.append(steps[at])
+        out.append(row)
+    return out
+
+
+def reduce_chunks(shape):
+    shards, rows, columns = shape
+    width = columns
+    while width % 1024 == 0 and shards * (rows // 2) * width > (1 << 19):
+        width //= 2
+    return width, columns // width
+
+
+def gather_kernel(ring, count, *refs):
+    sources, fulls = refs[:count], refs[count : 2 * count]
+    local_sem, send_sem, recv_sem = refs[2 * count :]
+    net = Net(ring)
+    net.greet()
+    lists = [
+        gather_steps(net, sources[i], fulls[i], local_sem.at[i], send_sem.at[i], recv_sem.at[i])
+        for i in range(count)
+    ]
+    for step in range(len(lists[0])):
+        for steps in lists:
+            steps[step]()
+
+
+def gather_all(ring, shards, parts):
+    return pl.pallas_call(
+        functools.partial(gather_kernel, ring, len(parts)),
+        out_shape=[jax.ShapeDtypeStruct((shards,) + part.shape, part.dtype) for part in parts],
+        in_specs=[ANY] * len(parts),
+        out_specs=[ANY] * len(parts),
+        scratch_shapes=gather_scratch(ring, len(parts)),
+        compiler_params=pltpu.CompilerParams(collective_id=1, has_side_effects=True),
+        name="gather_all",
+    )(*parts)
+
+
+def reduce_kernel(ring, plan, *refs):
+    count = len(plan)
+    grads, outs = refs[:count], refs[count : 2 * count]
+    refs = refs[2 * count :]
+    local_sem, send_sem, recv_sem = refs[:3]
+    refs = refs[3:]
+    net = Net(ring)
+    net.greet()
+    lists = []
+    for index, (width, chunks) in enumerate(plan):
+        for chunk in range(chunks):
+            number = len(lists)
+            lists.append(
+                reduce_steps(
+                    net,
+                    grads[index],
+                    outs[index],
+                    chunk * width,
+                    refs[REDUCE_BUFFERS * number : REDUCE_BUFFERS * (number + 1)],
+                    local_sem.at[number],
+                    send_sem.at[number],
+                    recv_sem.at[number],
+                )
+            )
+    for row in staggered(lists):
+        for step in row:
+            step()
+
+
+def reduce_all(ring, grads, collective):
+    plan = [reduce_chunks(grad.shape) for grad in grads]
+    total = sum(chunks for _, chunks in plan)
+    scratch = [
+        pltpu.SemaphoreType.DMA((total, 2)),
+        pltpu.SemaphoreType.DMA((total, reduce_count(ring))),
+        pltpu.SemaphoreType.DMA((total, reduce_count(ring))),
+    ]
+    for grad, (width, chunks) in zip(grads, plan):
+        for _ in range(chunks):
+            scratch += reduce_scratch(ring, grad.shape[0], grad.shape[1] // 2, width, grad.dtype)
+    return pl.pallas_call(
+        functools.partial(reduce_kernel, ring, plan),
+        out_shape=[jax.ShapeDtypeStruct(grad.shape[1:], jnp.float32) for grad in grads],
+        in_specs=[ANY] * len(grads),
+        out_specs=[ANY] * len(grads),
+        scratch_shapes=scratch,
+        compiler_params=pltpu.CompilerParams(
+            collective_id=collective, has_side_effects=True, vmem_limit_bytes=60 << 20
+        ),
+        name="reduce_all",
+    )(*grads)
 
 
 def contract_rows(first_op, second_op):
@@ -135,7 +619,58 @@
     return (jnp.concatenate(d_query_parts, axis=0), d_keys, d_values, d_bias)
 
 
+def gathered(line, attn_gain, w_qkv, attn_bias, w_out, ffn_gain, w_in, w_down):
+    if not line:
+        return tuple(
+            lax.all_gather(part, "shard", axis=axis, tiled=True)
+            for part, axis in (
+                (attn_gain, 0),
+                (w_qkv, 0),
+                (attn_bias, 1),
+                (w_out, 0),
+                (ffn_gain, 0),
+                (w_in, 0),
+                (w_down, 0),
+            )
+        )
+    shards, heads = lax.axis_size("shard"), attn_bias.shape[1]
+    small = jnp.zeros((16, 128), jnp.float32)
+    small = small.at[0].set(attn_gain.astype(jnp.float32)).at[1].set(ffn_gain.astype(jnp.float32))
+    small = small.at[2:4, :heads].set(attn_bias.astype(jnp.float32))
+    small, *full = gather_all(line, shards, [small, w_qkv, w_out, w_in, w_down])
+    qkv, out, into, down = (part.reshape(-1, part.shape[2]) for part in full)
+    low = small.astype(jnp.bfloat16)
+    bias = jnp.swapaxes(low[:, 2:4, :heads], 0, 1).reshape(2, -1)
+    return (low[:, 0].reshape(-1), qkv, bias, out, low[:, 1].reshape(-1), into, down)
+
+
+def reduced(line, gain_one, qkv, bias, out, gain_two, into, down):
+    if not line:
+        grads = ((gain_one, 0), (qkv, 0), (bias, 1), (out, 0), (gain_two, 0), (into, 0), (down, 0))
+        owned = [
+            lax.psum_scatter(
+                grad.astype(jnp.bfloat16), "shard", scatter_dimension=axis, tiled=True
+            )
+            for grad, axis in grads
+        ]
+        return tuple(lax.psum(part, "rep").astype(jnp.float32) for part in owned)
+    shards = lax.axis_size("shard")
+    heads = bias.shape[1] // shards
+    small = jnp.zeros((shards, 16, 128), jnp.float32)
+    small = small.at[:, 0].set(gain_one.reshape(shards, -1)).at[:, 1].set(gain_two.reshape(shards, -1))
+    small = small.at[:, 2:4, :heads].set(jnp.swapaxes(bias.reshape(2, shards, heads), 0, 1))
+
+    def cut(grad):
+        return grad.astype(jnp.bfloat16).reshape(shards, -1, grad.shape[1])
+
+    (sum_down,) = reduce_all(line, [cut(down)], 2)
+    (sum_in,) = reduce_all(line, [cut(into)], 3)
+    sum_out, sum_qkv, small = reduce_all(line, [cut(out), cut(qkv), small], 4)
+    return (small[0], sum_qkv, small[2:4, :heads], sum_out, small[1], sum_in, sum_down)
+
+
 def shards(
+    line,
     tokens,
     lengths,
     variate_ids,
@@ -151,14 +686,8 @@
 ):
     seq_count, length = variate_ids.shape
     row_count = seq_count * length
-    gain_one, qkv_weight, bias_full, out_weight, gain_two, in_weight, down_weight = (
-        lax.all_gather(attn_gain, "shard", axis=0, tiled=True),
-        lax.all_gather(w_qkv, "shard", axis=0, tiled=True),
-        lax.all_gather(attn_bias, "shard", axis=1, tiled=True),
-        lax.all_gather(w_out, "shard", axis=0, tiled=True),
-        lax.all_gather(ffn_gain, "shard", axis=0, tiled=True),
-        lax.all_gather(w_in, "shard", axis=0, tiled=True),
-        lax.all_gather(w_down, "shard", axis=0, tiled=True),
+    gain_one, qkv_weight, bias_full, out_weight, gain_two, in_weight, down_weight = gathered(
+        line, attn_gain, w_qkv, attn_bias, w_out, ffn_gain, w_in, w_down
     )
     positions = jnp.arange(length)
     key_valid = positions[None, :] < lengths[:, None]
@@ -201,15 +730,6 @@
     result = (hidden + jnp.dot(activated, down_weight, preferred_element_type=jnp.float32)).astype(
         jnp.bfloat16
     )
-    gain_one, qkv_weight, bias_full, out_weight, gain_two, in_weight, down_weight = (
-        lax.all_gather(attn_gain, "shard", axis=0, tiled=True),
-        lax.all_gather(w_qkv, "shard", axis=0, tiled=True),
-        lax.all_gather(attn_bias, "shard", axis=1, tiled=True),
-        lax.all_gather(w_out, "shard", axis=0, tiled=True),
-        lax.all_gather(ffn_gain, "shard", axis=0, tiled=True),
-        lax.all_gather(w_in, "shard", axis=0, tiled=True),
-        lax.all_gather(w_down, "shard", axis=0, tiled=True),
-    )
     grad_rows = jnp.where(row_valid, cotangent, jnp.zeros_like(cotangent))
     grad_down = contract_rows(activated, grad_rows)
     d_act = times_transpose(grad_rows, down_weight)
@@ -262,39 +782,9 @@
     grad_tokens = d_hidden + inv_one * (
         scaled_one - unit_one * jnp.mean(scaled_one * unit_one, axis=1, keepdims=True)
     )
-    owned_grads = (
-        lax.psum_scatter(
-            grad_gain_one.astype(jnp.bfloat16), "shard", scatter_dimension=0, tiled=True
-        ).astype(jnp.float32),
-        lax.psum_scatter(
-            grad_qkv.astype(jnp.bfloat16), "shard", scatter_dimension=0, tiled=True
-        ).astype(jnp.float32),
-        lax.psum_scatter(
-            grad_bias.astype(jnp.bfloat16), "shard", scatter_dimension=1, tiled=True
-        ).astype(jnp.float32),
-        lax.psum_scatter(
-            grad_out.astype(jnp.bfloat16), "shard", scatter_dimension=0, tiled=True
-        ).astype(jnp.float32),
-        lax.psum_scatter(
-            grad_gain_two.astype(jnp.bfloat16), "shard", scatter_dimension=0, tiled=True
-        ).astype(jnp.float32),
-        lax.psum_scatter(
-            grad_in.astype(jnp.bfloat16), "shard", scatter_dimension=0, tiled=True
-        ).astype(jnp.float32),
-        lax.psum_scatter(
-            grad_down.astype(jnp.bfloat16), "shard", scatter_dimension=0, tiled=True
-        ).astype(jnp.float32),
-    )
-    owned_grads = (
-        lax.psum(owned_grads[0].astype(jnp.bfloat16), "rep").astype(jnp.float32),
-        lax.psum(owned_grads[1].astype(jnp.bfloat16), "rep").astype(jnp.float32),
-        lax.psum(owned_grads[2].astype(jnp.bfloat16), "rep").astype(jnp.float32),
-        lax.psum(owned_grads[3].astype(jnp.bfloat16), "rep").astype(jnp.float32),
-        lax.psum(owned_grads[4].astype(jnp.bfloat16), "rep").astype(jnp.float32),
-        lax.psum(owned_grads[5].astype(jnp.bfloat16), "rep").astype(jnp.float32),
-        lax.psum(owned_grads[6].astype(jnp.bfloat16), "rep").astype(jnp.float32),
-    )
-    sum_gain_one, sum_qkv, sum_bias, sum_out, sum_gain_two, sum_in, sum_down = owned_grads
+    sum_gain_one, sum_qkv, sum_bias, sum_out, sum_gain_two, sum_in, sum_down = reduced(
+        line, grad_gain_one, grad_qkv, grad_bias, grad_out, grad_gain_two, grad_in, grad_down
+    )
     return (
         result,
         grad_tokens,
@@ -323,8 +813,9 @@
         P("shard", None),
         P(("shard", "rep"), None),
     )
+    line = mesh.shape["shard"] // 2 if (mesh.shape["shard"], mesh.shape["rep"]) == (8, 4) else 0
     return jax.shard_map(
-        shards,
+        functools.partial(shards, line),
         mesh=mesh,
         in_specs=placed,
         out_specs=(

time: 1470 us -> 955 us (0.65)
  waiting for transfers between devices: 820 us -> 0 us
  Pallas kernels: 0 us -> 394 us
  blocking collectives: 71.7 us -> 0 us
    reduce_scatter x4 -> x0, waiting for transfers between devices: 495 us -> none  [the longest x1 286 us: shards(): lax.psum_scatter(grad_in.astype(jnp.bfloat16), 'shard', scatter_dimension...]
    pallas_call x0 -> x4, Pallas kernels: none -> 394 us  [the longest x3 252 us: reduce_all(): pl.pallas_call(functools.partial(reduce_kernel, ring, plan), out_shape=[j...]
    all_gather x4 -> x0, waiting for transfers between devices: 286 us -> none  [the longest x1 151 us: shards(): lax.all_gather(w_in, 'shard', axis=0, tiled=True)]
    all_gather x3 -> x0, blocking collectives: 46 us -> none  [the longest x1 18.1 us: shards(): lax.all_gather(attn_bias, 'shard', axis=1, tiled=True)]
    psum x1 -> x0, waiting for transfers between devices: 35.9 us -> none  [shards(): lax.psum(owned_grads[1].astype(jnp.bfloat16), 'rep').astype(jnp.float32)]
    unnamed x1 -> x0, blocking collectives: 16.2 us -> none
    unnamed x124 -> x86, local copies, waits for them, and re-layouts: 38.3 us -> 33.9 us
  transfers between devices with their start and end apart: 9 -> 0, of which waited for: 7 -> 0; matrix products, arithmetic and copies ran while one was open for 21% -> 0% of each run, Pallas kernels for 0% -> 0%
where the time goes in v1:
time: 955 us; the launch traced here: 949 us
  Pallas kernels  394 us (41%)
  matrix products  372 us (39%)
  other arithmetic  129 us (14%)
  local copies, waits for them, and re-layouts  51.5 us (5%)
    pallas_call x3, Pallas kernels, reduce_all(): pl.pallas_call(functools.partial(reduce_kernel, ring, plan), out_shape=[j...  252 us
    pallas_call x1, Pallas kernels, gather_all(): pl.pallas_call(functools.partial(gather_kernel, ring, len(parts)), out_sh...  142 us
    dot_general x4, matrix products, times_transpose(): lax.dot_general(first_op, second_op, (((1,), (1,)), ((), ())), preferred_...  67.4 us
    dot_general x1, other arithmetic, attend_backward(): jnp.einsum('hqk,qk->h', d_scores, same_mask, preferred_element_type=jnp.f...  57.1 us
    dot_general x4, matrix products, contract_rows(): lax.dot_general(first_op, second_op, (((0,), (0,)), ((), ())), preferred_...  54.8 us
    dot_general x2, matrix products, attend_backward(): jnp.einsum('qhd,khd->hqk', grad_block, values, preferred_element_type=jnp...  47.7 us
    dot_general x2, matrix products, score_block(): jnp.einsum('qhd,khd->hqk', query_rows, key_rows, preferred_element_type=j...  34.5 us
    unnamed x86, local copies, waits for them, and re-layouts  33.9 us

profile of v1, /device:TPU:1, one launch (start us, length us, event | category | flops | bytes accessed | tf_op | source)
XLA Modules:
  0.0 948.6 jit_solution(17190087637406276741)
XLA Ops:
  19.9 142.3 %gather_all.1 = (f32[8,16,128]{2,1,0:T(8,128)}, bf16[8,128,3072]{2,1,0:T(8,128)(2,1)}, bf16[8,128,1024]{2,1,0:T(8,128)(2,1)}, bf16[8,128,8192]{2,1,0:T(8,128)(2,1)}, bf16[8,512,1024]{2,1,0:T(8,128)(2,1)}) custom-call(f32[16,128]{1,0:T(8,128)} %copy-done.28, bf16[128,3072]{1,0:T(8,128)(2,1)} %refs_1_.1, bf16[128,1024]{1,0:T(8,128)(2,1)} %refs_2_.1, ...), custom_call_target="tpu_custom_call" | custom-call | tf_op jit(solution)/shard_map/gather_all/pallas_call | solution.py:437
  195.6 17.2 %fusion.79 = (f32[16,512]{1,0:T(8,128)S(1)}, f32[16,512,1024]{2,1,0:T(8,128)}) fusion(bf16[16]{0:T(256)(128)(2,1)S(1)} %broadcast_in_dim.203, bf16[16]{0:T(256)(128)(2,1)S(1)} %broadcast_in_dim.201, pred[512,1024]{1,0:T(8,128)(4,1)S(1)} %get-tuple-element.241, bf16[1024,16,64]{0,2,1:T(8,128)(2,1)} %get-tuple-element.215, ...), kind=kOutput, calls=%fused_computation.158 | convolution fusion | flops 1124065280 | bytes 37258304 | tf_op jit(solution)/shard_map/while/body/eval_jaxpr/qhd,khd->hqk/dot_general | solution.py:537
  212.9 14.4 %fusion.5 = f32[16,512]{1,0:T(8,128)S(1)} fusion(f32[16,512,1024]{2,1,0:T(8,128)} %get-tuple-element.251, f32[16,512]{1,0:T(8,128)S(1)} %get-tuple-element.250), kind=kLoop, calls=%fused_computation.21 | loop fusion | flops 16769024 | bytes 33619968 | tf_op jit(solution)/shard_map/while/body/eval_jaxpr/reduce_sum | solution.py:565
  227.9 12.8 %fusion.48 = bf16[16,64,512]{2,1,0:T(8,128)(2,1)S(1)} fusion(f32[16,512,1024]{2,1,0:T(8,128)} %get-tuple-element.251, f32[16,512]{1,0:T(8,128)S(1)} %fusion.5, f32[16,512]{1,0:T(8,128)S(1)} %get-tuple-element.250, f32[1024,3,16,64]{0,3,2,1:T(8,128)S(1)} %fusion.41), kind=kOutput, calls=%fused_computation.103 | convolution fusion | flops 1099431936 | bytes 36765696 | tf_op jit(solution)/shard_map/while/body/eval_jaxpr/hqk,khd->qhd/dot_general | solution.py:568
  240.7 17.3 %fusion.80 = (f32[16,512]{1,0:T(8,128)S(1)}, f32[16,512,1024]{2,1,0:T(8,128)}) fusion(bf16[16]{0:T(256)(128)(2,1)S(1)} %broadcast_in_dim.203, bf16[16]{0:T(256)(128)(2,1)S(1)} %broadcast_in_dim.201, pred[512,1024]{1,0:T(8,128)(4,1)S(1)} %get-tuple-element.246, bf16[1024,16,64]{0,2,1:T(8,128)(2,1)} %get-tuple-element.215, ...), kind=kOutput, calls=%fused_computation.159 | convolution fusion | flops 1124065280 | bytes 37258304 | tf_op jit(solution)/shard_map/while/body/eval_jaxpr/qhd,khd->hqk/dot_general | solution.py:537
  258.0 14.3 %fusion.4 = f32[16,512]{1,0:T(8,128)S(1)} fusion(f32[16,512,1024]{2,1,0:T(8,128)} %get-tuple-element.253, f32[16,512]{1,0:T(8,128)S(1)} %get-tuple-element.252), kind=kLoop, calls=%fused_computation.20 | loop fusion | flops 16769024 | bytes 33619968 | tf_op jit(solution)/shard_map/while/body/eval_jaxpr/reduce_sum | solution.py:565
  272.9 13.0 %fusion.49 = bf16[16,64,512]{2,1,0:T(8,128)(2,1)S(1)} fusion(f32[16,512,1024]{2,1,0:T(8,128)} %get-tuple-element.253, f32[16,512]{1,0:T(8,128)S(1)} %fusion.4, f32[16,512]{1,0:T(8,128)S(1)} %get-tuple-element.252, f32[1024,3,16,64]{0,3,2,1:T(8,128)S(1)} %fusion.41), kind=kOutput, calls=%fused_computation.104 | convolution fusion | flops 1099431936 | bytes 36765696 | tf_op jit(solution)/shard_map/while/body/eval_jaxpr/hqk,khd->qhd/dot_general | solution.py:568
  293.6 28.6 %fusion.75 = f32[1024,8192]{1,0:T(8,128)} fusion(bf16[1024,8192]{1,0:T(8,128)(2,1)} %bitcast.176, f32[1024,1024]{0,1:T(8,128)} %get-tuple-element.255, f32[1024]{0:T(1024)S(1)} %bitcast.169, f32[1024]{0:T(1024)S(1)} %add_rsqrt_fusion), kind=kOutput, calls=%fused_computation.154 | convolution fusion | flops 17183014912 | bytes 54534144 | tf_op jit(solution)/shard_map/dot_general | solution.py:724
  322.1 28.0 %multiply_convert_fusion.3 = (bf16[1024,4096]{1,0:T(8,128)(2,1)}, bf16[1024,4096]{1,0:T(8,128)(2,1)}, bf16[1024,4096]{1,0:T(8,128)(2,1)}) fusion(f32[1024,8192]{1,0:T(8,128)} %fusion.75, bf16[4096,1024]{1,0:T(8,128)(2,1)} %bitcast.178, bf16[1024,1024]{0,1:T(8,128)(2,1)S(1)} %copy-done.13, pred[1024]{0:T(1024)(128)(4,1)S(1)} %iota_compare_fusion), kind=kOutput, calls=%fused_computation.30 | convolution fusion | flops 8653897728 | bytes 69207040 | tf_op jit(solution)/shard_map/dot_general | solution.py:508
  350.2 15.4 %add_convert_fusion = bf16[1024,1024]{0,1:T(8,128)(2,1)} fusion(f32[1024,1024]{0,1:T(8,128)} %get-tuple-element.255, bf16[1024,4096]{1,0:T(8,128)(2,1)} %get-tuple-element.213, bf16[4096,1024]{1,0:T(8,128)(2,1)} %bitcast.179), kind=kOutput, calls=%fused_computation.75 | convolution fusion | flops 8592031744 | bytes 23068672 | tf_op jit(solution)/shard_map/dot_general | solution.py:730
  365.6 27.6 %multiply_reduce_fusion.2 = (f32[1024]{0:T(1024)}, f32[1024]{0:T(1024)S(1)}, f32[1024,1024]{0,1:T(8,128)}) fusion(f32[1024,1024]{0,1:T(8,128)} %get-tuple-element.255, f32[1024]{0:T(1024)S(1)} %add_rsqrt_fusion, f32[1024]{0:T(1024)S(1)} %bitcast.170, bf16[1024,8192]{1,0:T(8,128)(2,1)} %bitcast.177, bf16[1024,4096]{1,0:T(8,128)(2,1)} %get-tuple-element.212, ...), kind=kOutput, calls=%fused_computation.71 | convolution fusion | flops 17219715072 | bytes 41959424 | tf_op jit(solution)/shard_map/dot_general | solution.py:508
  393.1 25.1 %convolution_convert_fusion = bf16[1024,8192]{1,0:T(8,128)(2,1)} fusion(bf16[1024,4096]{1,0:T(8,128)(2,1)} %get-tuple-element.212, bf16[1024,4096]{1,0:T(8,128)(2,1)} %get-tuple-element.211, f32[1024,1024]{0,1:T(8,128)} %get-tuple-element.255, f32[1024]{0:T(1024)S(1)} %bitcast.171, f32[1024]{0:T(1024)S(1)} %add_rsqrt_fusion), kind=kOutput, calls=%fused_computation.36 | convolution fusion | flops 17224957952 | bytes 37756928 | tf_op jit(solution)/shard_map/dot_general | solution.py:502
  418.3 104.6 %reduce_all.4 = f32[128,8192]{1,0:T(8,128)} custom-call(bf16[8,128,8192]{2,1,0:T(8,128)(2,1)} %bitcast.134), custom_call_target="tpu_custom_call" | custom-call | tf_op jit(solution)/shard_map/reduce_all/pallas_call | solution.py:488
  533.4 14.7 %convolution_convert_fusion.1 = bf16[4096,1024]{1,0:T(8,128)(2,1)} fusion(bf16[1024,4096]{1,0:T(8,128)(2,1)} %get-tuple-element.213, bf16[1024,1024]{0,1:T(8,128)(2,1)S(1)} %copy-done.13, pred[1024]{0:T(1024)(128)(4,1)S(1)} %iota_compare_fusion), kind=kOutput, calls=%fused_computation.39 | convolution fusion | flops 8595177472 | bytes 18875392 | tf_op jit(solution)/shard_map/dot_general | solution.py:502
  548.1 77.6 %reduce_all.5 = f32[512,1024]{1,0:T(8,128)} custom-call(bf16[8,512,1024]{2,1,0:T(8,128)(2,1)} %bitcast.139), custom_call_target="tpu_custom_call" | custom-call | tf_op jit(solution)/shard_map/reduce_all/pallas_call | solution.py:488
  634.9 15.5 %fusion.8 = f32[16,64,1024]{2,1,0:T(8,128)} fusion(bf16[512,16,64]{0,2,1:T(8,128)(2,1)S(1)} %bitcast.135, f32[16,512,1024]{2,1,0:T(8,128)} %get-tuple-element.251, f32[16,512]{1,0:T(8,128)S(1)} %copy-done.23), kind=kOutput, calls=%fused_computation.24 | convolution fusion | flops 1090519040 | bytes 38830080 | tf_op jit(solution)/shard_map/while/body/eval_jaxpr/hqk,qhd->khd/dot_general | solution.py:595
  650.5 16.2 %add_bitcast_fusion = bf16[1024,1,16,64]{0,3,2,1:T(8,128)(2,1)} fusion(f32[16,64,1024]{2,1,0:T(8,128)} %fusion.8, bf16[512,16,64]{0,2,1:T(8,128)(2,1)S(1)} %bitcast.137, f32[16,512,1024]{2,1,0:T(8,128)} %get-tuple-element.253, f32[16,512]{1,0:T(8,128)S(1)} %copy-done.24), kind=kOutput, calls=%fused_computation.72 | convolution fusion | flops 1092616192 | bytes 40927232 | tf_op jit(solution)/shard_map/while/body/eval_jaxpr/hqk,qhd->khd/dot_general | solution.py:595
  666.7 23.7 %multiply_reduce_fusion.1 = (f32[16,512]{1,0:T(8,128)S(1)}, f32[16,512,1024]{2,1,0:T(8,128)}) fusion(f32[16,512,1024]{2,1,0:T(8,128)} %get-tuple-element.253, f32[16,512]{1,0:T(8,128)S(1)} %copy-done.24, bf16[512,16,64]{0,2,1:T(8,128)(2,1)S(1)} %bitcast.138, f32[1024,3,16,64]{0,3,2,1:T(8,128)} %copy-done), kind=kOutput, calls=%fused_computation.12 | convolution fusion | flops 1098899456 | bytes 70320128 | tf_op jit(solution)/shard_map/while/body/eval_jaxpr/qhd,khd->hqk/dot_general | solution.py:601
  690.4 23.9 %multiply_reduce_fusion = (f32[16,512]{1,0:T(8,128)S(1)}, f32[16,512,1024]{2,1,0:T(8,128)}) fusion(f32[16,512,1024]{2,1,0:T(8,128)} %get-tuple-element.251, f32[16,512]{1,0:T(8,128)S(1)} %copy-done.23, bf16[512,16,64]{0,2,1:T(8,128)(2,1)S(1)} %bitcast.136, f32[1024,3,16,64]{0,3,2,1:T(8,128)} %copy-done), kind=kOutput, calls=%fused_computation.9 | convolution fusion | flops 1098899456 | bytes 70320128 | tf_op jit(solution)/shard_map/while/body/eval_jaxpr/qhd,khd->hqk/dot_general | solution.py:601
  714.3 57.1 %fusion = (f32[16]{0:T(128)S(1)}, f32[16]{0:T(128)S(1)}, bf16[16,512,1024]{2,1,0:T(8,128)(2,1)}, f32[16]{0:T(128)S(1)}, f32[16]{0:T(128)S(1)}, /*index=5*/bf16[16,512,1024]{2,1,0:T(8,128)(2,1)}) fusion(f32[1024,512]{0,1:T(8,128)} %get-tuple-element.247, f32[1024,512]{0,1:T(8,128)} %get-tuple-element.245, f32[16,512,1024]{2,1,0:T(8,128)} %get-tuple-element.258, ...), kind=kLoop, calls=%fused_computation.4 | loop fusion | flops 150994880 | bytes 176292096 | tf_op jit(solution)/shard_map/while/body/eval_jaxpr/hqk,qk->h/dot_general | solution.py:605
  783.1 13.0 %multiply_bitcast_fusion.3 = (f32[512,16,64]{0,2,1:T(8,128)}, f32[512,1,16,64]{0,3,2,1:T(8,128)}) fusion(bf16[1024,16,64]{0,2,1:T(8,128)(2,1)S(1)} %copy-done.6, bf16[16,512,1024]{2,1,0:T(8,128)(2,1)} %get-tuple-element.210), kind=kOutput, calls=%fused_computation.99 | convolution fusion | flops 1074266112 | bytes 23068672 | tf_op jit(solution)/shard_map/while/body/eval_jaxpr/hqk,khd->qhd/dot_general | solution.py:611
  796.1 13.7 %bitcast_multiply_fusion = (f32[1024,16,64]{0,2,1:T(8,128)}, f32[16,64,1024]{2,1,0:T(8,128)}) fusion(f32[1024,64]{0,1:T(8,128)S(1)} %copy-done.17, f32[16,64,1024]{2,1,0:T(8,128)} %fusion.62, bf16[16,512,1024]{2,1,0:T(8,128)(2,1)} %get-tuple-element.266, bf16[1024,16,64]{0,2,1:T(8,128)(2,1)} %get-tuple-element.214), kind=kOutput, calls=%fused_computation.69 | convolution fusion | flops 1075838976 | bytes 30670848 | tf_op jit(solution)/shard_map/while/body/eval_jaxpr/hqk,qhd->khd/dot_general | solution.py:616
  809.8 13.2 %multiply_bitcast_fusion.1 = (f32[512,16,64]{0,2,1:T(8,128)}, f32[512,1,16,64]{0,3,2,1:T(8,128)}) fusion(bf16[1024,16,64]{0,2,1:T(8,128)(2,1)S(1)} %copy-done.6, bf16[16,512,1024]{2,1,0:T(8,128)(2,1)} %get-tuple-element.266), kind=kOutput, calls=%fused_computation.97 | convolution fusion | flops 1074266112 | bytes 23068672 | tf_op jit(solution)/shard_map/while/body/eval_jaxpr/hqk,khd->qhd/dot_general | solution.py:611
  866.8 69.9 %reduce_all.3 = (f32[128,1024]{1,0:T(8,128)}, f32[128,3072]{1,0:T(8,128)}, f32[16,128]{1,0:T(8,128)}) custom-call(bf16[8,128,1024]{2,1,0:T(8,128)(2,1)} %bitcast.149, bf16[8,128,3072]{2,1,0:T(8,128)(2,1)} %bitcast.147, f32[8,16,128]{2,1,0:T(8,128)} %copy-done.26), custom_call_target="tpu_custom_call" | custom-call | tf_op jit(solution)/shard_map/reduce_all/pallas_call | solution.py:488
  (145 shorter events, 147.5 us)
Async XLA Ops:
  5.1 9.5 %copy-start.28 = (f32[16,128]{1,0:T(8,128)}, f32[16,128]{1,0:T(8,128)S(1)}, u32[]{:S(2)}) copy-start(f32[16,128]{1,0:T(8,128)S(1)} %scatter.29.refs_0_) | copy-start | bytes 24580
  6.9 184.9 %copy-start.18 = (f32[1024,64]{0,1:T(8,128)}, f32[1024,64]{0,1:T(8,128)S(1)}, u32[]{:S(2)}) copy-start(f32[1024,64]{0,1:T(8,128)S(1)} %get-tuple-element.234) | copy-start | bytes 786436
  6.9 184.9 %copy-start.20 = (f32[1024,64]{0,1:T(8,128)}, f32[1024,64]{0,1:T(8,128)S(1)}, u32[]{:S(2)}) copy-start(f32[1024,64]{0,1:T(8,128)S(1)} %get-tuple-element.235) | copy-start | bytes 786436
  9.9 7.2 copy-start.3
  10.4 162.6 %copy-start.29 = (f32[1024]{0:T(1024)}, f32[1024]{0:T(1024)S(1)}, u32[]{:S(2)}) copy-start(f32[1024]{0:T(1024)S(1)} %add_rsqrt_fusion.1) | copy-start | bytes 12292
  163.7 9.4 copy-start.31
  183.2 89.7 %copy-start = (f32[1024,3,16,64]{0,3,2,1:T(8,128)}, f32[1024,3,16,64]{0,3,2,1:T(8,128)S(1)}, u32[]{:S(2)}) copy-start(f32[1024,3,16,64]{0,3,2,1:T(8,128)S(1)} %fusion.41) | copy-start | bytes 37748740
  293.6 28.6 %copy-start.13 = (bf16[1024,1024]{0,1:T(8,128)(2,1)S(1)}, bf16[1024,1024]{0,1:T(8,128)(2,1)}, u32[]{:S(2)}) copy-start(bf16[1024,1024]{0,1:T(8,128)(2,1)} %copy.72) | copy-start | bytes 6291460
  548.1 77.6 %copy-start.22 = (bf16[1024,16,64]{0,2,1:T(8,128)(2,1)S(1)}, bf16[1024,16,64]{0,2,1:T(8,128)(2,1)}, u32[]{:S(2)}) copy-start(bf16[1024,16,64]{0,2,1:T(8,128)(2,1)} %pad_maximum_fusion.3) | copy-start | bytes 6291460
  625.7 6.1 copy-start.8
  625.7 6.1 copy-start.36
  634.9 15.5 %copy-start.24 = (f32[16,512]{1,0:T(8,128)S(1)}, f32[16,512]{1,0:T(8,128)}, u32[]{:S(2)}) copy-start(f32[16,512]{1,0:T(8,128)} %log_add_fusion.1) | copy-start | bytes 98308
  690.4 23.9 %copy-start.10 = (f32[1024,512]{0,1:T(8,128)S(1)}, f32[1024,512]{0,1:T(8,128)}, u32[]{:S(2)}) copy-start(f32[1024,512]{0,1:T(8,128)} %get-tuple-element.240) | copy-start | bytes 6291460
  771.8 11.3 %copy-start.6 = (bf16[1024,16,64]{0,2,1:T(8,128)(2,1)S(1)}, bf16[1024,16,64]{0,2,1:T(8,128)(2,1)}, u32[]{:S(2)}) copy-start(bf16[1024,16,64]{0,2,1:T(8,128)(2,1)} %get-tuple-element.215) | copy-start | bytes 6291460
  783.1 13.0 %copy-start.17 = (f32[1024,64]{0,1:T(8,128)S(1)}, f32[1024,64]{0,1:T(8,128)}, u32[]{:S(2)}) copy-start(f32[1024,64]{0,1:T(8,128)} %get-tuple-element.233) | copy-start | bytes 786436
  809.8 13.2 %copy-start.19 = (f32[1024,64]{0,1:T(8,128)S(1)}, f32[1024,64]{0,1:T(8,128)}, u32[]{:S(2)}) copy-start(f32[1024,64]{0,1:T(8,128)} %copy-done.18) | copy-start | bytes 786436
  832.0 5.5 slice-start
  833.6 5.2 slice-start.1
  833.6 5.2 copy-start.30
  833.6 5.2 copy-start.32
  838.9 9.5 copy-start.16
  848.3 8.9 copy-start.9
  860.2 5.4 copy-start.34
  936.7 7.3 copy-start.7
  (15 other events, 38.5 us)

commit v2 on v1

v2 whole, which is shorter than its diff:
```python
import functools

import jax
import jax.numpy as jnp
from jax import lax
from jax.experimental import pallas as pl
from jax.experimental.pallas import tpu as pltpu
from jax.sharding import PartitionSpec as P

HEADS = 16
HEAD_DIM = 64


norm_eps = 1e-06
rope_base = 10000.0
masked_score = -1000000000.0

MESH = pl.DeviceIdType.MESH
ANY = pl.BlockSpec(memory_space=pl.ANY)


class Net:
    def __init__(self, line):
        shard, rep = lax.axis_index("shard"), lax.axis_index("rep")
        self.line = line
        self.z, self.y = shard // 2, shard % 2
        self.x, self.core = rep // 2, rep % 2
        self.own = shard
        self.sibling = (shard, self.x * 2 + 1 - self.core)
        self.across_x = (shard, (1 - self.x) * 2 + self.core)
        self.across_y = (self.z * 2 + 1 - self.y, rep)
        self.above = (jnp.minimum(self.z + 1, line - 1) * 2 + self.y, rep)
        self.below = (jnp.maximum(self.z - 1, 0) * 2 + self.y, rep)
        self.has_above = self.z < line - 1
        self.has_below = self.z > 0

    def greet(self):
        barrier = pltpu.get_barrier_semaphore()

        def hail(partner):
            pl.semaphore_signal(barrier, inc=1, device_id=partner, device_id_type=MESH)

        for partner in (self.sibling, self.across_x, self.across_y):
            hail(partner)
        pl.when(self.has_above)(lambda: hail(self.above))
        pl.when(self.has_below)(lambda: hail(self.below))
        neighbours = jnp.where(self.has_above, 1, 0) + jnp.where(self.has_below, 1, 0)
        pl.semaphore_wait(barrier, 3 + neighbours)


def aligned(value, step):
    return pl.multiple_of(value, step)


def gather_count(line):
    return 2 * line + 3 * 2 * line


def gather_steps(net, source, full, local_sem, send_sem, recv_sem):
    line = net.line
    half, columns = source.shape[0] // 2, source.shape[1]
    split = columns % 1024 == 0
    only = columns * 3 // 8 if split else 0
    shared = columns - 2 * only
    rows = pl.ds(aligned(net.core * half, half), half)
    carried = pl.ds(aligned(net.x * only, 128), only + shared) if split else pl.ds(0, columns)
    lone = pl.ds(aligned(net.x * (only + shared), 128), only) if split else None

    def remote(origin, landing, index, target):
        return pltpu.make_async_remote_copy(
            src_ref=origin,
            dst_ref=landing,
            send_sem=send_sem.at[index],
            recv_sem=recv_sem.at[index],
            device_id=target,
            device_id_type=MESH,
        )

    def piece(z, y):
        return full.at[z * 2 + y, rows, carried]

    def over_z(z, target, base):
        return remote(piece(z, net.y), piece(z, net.y), base + z, target)

    def over_y(z):
        return remote(piece(z, net.y), piece(z, net.y), 2 * line + z, net.across_y)

    def over_x(z, y):
        part = full.at[z * 2 + y, rows, lone]
        return remote(part, part, 3 * line + y * line + z, net.across_x)

    def to_core(z, y):
        part = full.at[z * 2 + y, rows]
        return remote(part, part, 5 * line + y * line + z, net.sibling)

    mine = source.at[rows, carried]
    local = pltpu.make_async_copy(source, full.at[net.own], local_sem)
    first_y = remote(mine, piece(net.z, net.y), 2 * line + net.z, net.across_y)
    first_up = remote(mine, piece(net.z, net.y), net.z, net.above)
    first_down = remote(mine, piece(net.z, net.y), line + net.z, net.below)

    def onward(z, y):
        if split:
            over_x(z, y).start()
        else:
            to_core(z, y).start()

    def start():
        first_y.start()
        pl.when(net.has_above)(first_up.start)
        pl.when(net.has_below)(first_down.start)
        local.start()

    def arrive(hops):
        @pl.when(net.z >= hops)
        def _():
            z = net.z - hops
            over_z(z, net.above, 0).wait_recv()
            pl.when(net.has_above)(over_z(z, net.above, 0).start)
            over_y(z).start()
            onward(z, net.y)

        @pl.when(net.z < line - hops)
        def _():
            z = net.z + hops
            over_z(z, net.below, line).wait_recv()
            pl.when(net.has_below)(over_z(z, net.below, line).start)
            over_y(z).start()
            onward(z, net.y)

    def arrive_y(hops):
        def one(z):
            remote(piece(z, 1 - net.y), piece(z, 1 - net.y), 2 * line + z, net.across_y).wait_recv()
            onward(z, 1 - net.y)

        if hops == 0:
            one(net.z)
        else:
            pl.when(net.z >= hops)(lambda: one(net.z - hops))
            pl.when(net.z < line - hops)(lambda: one(net.z + hops))

    def arrive_x(hops, own_y):
        def one(z):
            y = net.y if own_y else 1 - net.y
            part = full.at[z * 2 + y, rows, pl.ds(aligned((1 - net.x) * (only + shared), 128), only)]
            remote(part, part, 3 * line + y * line + z, net.across_x).wait_recv()
            to_core(z, y).start()

        if not split:
            return
        if hops == 0:
            one(net.z)
        else:
            pl.when(net.z >= hops)(lambda: one(net.z - hops))
            pl.when(net.z < line - hops)(lambda: one(net.z + hops))

    def step(hops):
        def run():
            arrive_y(hops - 1)
            if hops < line:
                arrive(hops)
            if hops >= 2:
                arrive_x(hops - 2, False)
                arrive_x(hops - 1, True)

        return run

    def last():
        arrive_x(line - 1, False)

    def finish():
        local.wait()
        first_y.wait_send()

        @pl.when(net.has_above)
        def _():
            first_up.wait_send()
            for hops in range(1, line - 1):
                pl.when(net.z >= hops)(over_z(net.z - hops, net.above, 0).wait_send)

        @pl.when(net.has_below)
        def _():
            first_down.wait_send()
            for hops in range(1, line - 1):
                pl.when(net.z < line - hops)(over_z(net.z + hops, net.below, line).wait_send)

        for z in range(line):

            def others():
                over_y(z).wait_send()
                if split:
                    over_x(z, net.y).wait_send()
                to_core(z, net.y).wait()

            pl.when(net.z != z)(others)
            if split:
                over_x(z, 1 - net.y).wait_send()
            to_core(z, 1 - net.y).wait()

    return [start] + [step(hops) for hops in range(1, line + 1)] + [last, finish]


def gather_scratch(line, tensors):
    copies = gather_count(line)
    return [
        pltpu.SemaphoreType.DMA((tensors,)),
        pltpu.SemaphoreType.DMA((tensors, copies)),
        pltpu.SemaphoreType.DMA((tensors, copies)),
    ]


REDUCE_BUFFERS = 9


def reduce_split(columns):
    only = columns // 4 if columns % 512 == 0 else 0
    return only, columns - 2 * only


def reduce_scratch(line, shards, half, columns, dtype):
    only, shared = reduce_split(columns)
    carried = only + shared
    return [
        pltpu.VMEM((shards, half, columns), dtype),
        pltpu.VMEM((shards, half, columns), dtype),
        pltpu.VMEM((shards, half, max(only, 128)), dtype),
        pltpu.VMEM((line, half, carried), dtype),
        pltpu.VMEM((line + 1, half, carried), dtype),
        pltpu.VMEM((half, carried), dtype),
        pltpu.VMEM((half, columns), dtype),
        pltpu.VMEM((half, columns), dtype),
        pltpu.VMEM((2 * half, columns), jnp.float32),
    ]


def reduce_count(line):
    return 3 * line + 4


def reduce_steps(net, grad, out, column_start, out_start, buffers, local_sem, send_sem, recv_sem):
    kept, got, from_x, from_y, from_z, late_x, final, swapped, wide = buffers
    line = net.line
    shards, half, width = kept.shape
    only, shared = reduce_split(width)
    both = only + shared
    columns = pl.ds(column_start, width)
    mine = pl.ds(aligned(net.core * half, half), half)
    theirs = pl.ds(aligned((1 - net.core) * half, half), half)
    if only:
        carried = pl.ds(aligned(net.x * only, 128), both)
        lone = pl.ds(aligned(net.x * both, 128), only)
        their_lone = pl.ds(aligned((1 - net.x) * both, 128), only)
    else:
        carried = pl.ds(0, width)

    def remote(origin, landing, index, target):
        return pltpu.make_async_remote_copy(
            src_ref=origin,
            dst_ref=landing,
            send_sem=send_sem.at[index],
            recv_sem=recv_sem.at[index],
            device_id=target,
            device_id_type=MESH,
        )

    local = pltpu.make_async_copy(grad.at[:, mine, columns], kept, local_sem.at[0])
    halves = remote(grad.at[:, theirs, columns], got, 2 * line, net.sibling)
    written = pltpu.make_async_copy(wide, out.at[:, pl.ds(out_start, width)], local_sem.at[1])
    to_core = remote(final, swapped, 2 * line + 1, net.sibling)
    end_x = remote(kept.at[net.own, :, carried], late_x, 2 * line + 2, net.across_x)
    if only:
        over_x = remote(kept.at[:, :, their_lone], from_x, 2 * line + 3, net.across_x)

    def over_y(z):
        part = kept.at[z * 2 + 1 - net.y, :, carried]
        return remote(part, from_y.at[z], 2 * line + 4 + z, net.across_y)

    def up(z):
        return remote(kept.at[z * 2 + net.y, :, carried], from_z.at[z + 1], z, net.above)

    def down(z):
        return remote(kept.at[z * 2 + net.y, :, carried], from_z.at[z], line + z, net.below)

    def add(shard, part):
        kept[shard, :, carried] = kept[shard, :, carried] + part

    def first():
        halves.start()
        local.start()

    def second():
        local.wait()
        halves.wait_recv()

        @pl.loop(0, shards)
        def _(shard):
            kept[shard] = kept[shard] + got[shard]

        if only:
            over_x.start()

    def third():
        if only:
            over_x.wait_recv()

            @pl.loop(0, shards)
            def _(shard):
                kept[shard, :, lone] = kept[shard, :, lone] + from_x[shard]

        for z in range(line):
            over_y(z).start()

    def fourth():
        for z in range(line):
            over_y(z).wait_recv()

        @pl.loop(0, line)
        def _(z):
            add(z * 2 + net.y, from_y[z])

    def hop(step):
        def run():
            @pl.when(net.z == step)
            def _():
                for z in range(line - 1, step, -1):
                    if step > 0:
                        up(z).wait_recv()
                        add(z * 2 + net.y, from_z[z + 1])
                    up(z).start()

            @pl.when(net.z == line - 1 - step)
            def _():
                for z in range(line - 1 - step):
                    if step > 0:
                        down(z).wait_recv()
                        add(z * 2 + net.y, from_z[z])
                    down(z).start()

        return run

    def land():
        @pl.when(net.has_below)
        def _():
            up(net.z).wait_recv()
            add(net.own, from_z[net.z + 1])

        @pl.when(net.has_above)
        def _():
            down(net.z).wait_recv()
            add(net.own, from_z[net.z])

        end_x.start()

    def meet():
        end_x.wait_recv()
        if only:
            final[:, lone] = kept[net.own, :, lone]
            for x in range(2):

                @pl.when(net.x == x)
                def _():
                    start = 0 if x == 1 else shared
                    final[:, (1 - x) * both : (1 - x) * both + only] = late_x[:, start : start + only]
                    other = shared * 0 + (only if x == 1 else 0)
                    final[:, only:both] = kept[net.own, :, only:both] + late_x[:, other : other + shared]
        else:
            final[...] = kept[net.own] + late_x[...]
        to_core.start()
        wide[mine, :] = final[...].astype(jnp.float32)

    def swap():
        to_core.wait_recv()
        wide[theirs, :] = swapped[...].astype(jnp.float32)
        written.start()

    def finish():
        written.wait()
        halves.wait_send()
        if only:
            over_x.wait_send()
        for z in range(line):
            over_y(z).wait_send()
            pl.when(net.z < z)(up(z).wait_send)
            pl.when(net.z > z)(down(z).wait_send)
        end_x.wait_send()
        to_core.wait_send()

    hops = [hop(step) for step in range(line - 1)]

    def fourth_and_hop():
        fourth()
        hops[0]()

    return [first, second, third, fourth_and_hop] + hops[1:] + [land, meet, swap, finish]


def staggered(step_lists, gap=1):
    ticks = (len(step_lists) - 1) * gap + max(len(steps) for steps in step_lists)
    out = []
    for tick in range(ticks):
        row = []
        for index, steps in enumerate(step_lists):
            at = tick - index * gap
            if 0 <= at < len(steps):
                row.append(steps[at])
        out.append(row)
    return out


def reduce_chunks(shape):
    shards, rows, columns = shape
    width = columns
    while width % 1024 == 0 and shards * (rows // 2) * width > (1 << 19):
        width //= 2
    return width, columns // width


ROWS_BY_ROWS = (((0,), (0,)), ((), ()))
COLUMNS_BY_COLUMNS = (((1,), (1,)), ((), ()))


def product(first_op, second_op, dims=(((1,), (0,)), ((), ()))):
    return lax.dot_general(first_op, second_op, dims, preferred_element_type=jnp.float32)


def inverse_rms(values):
    return lax.rsqrt(jnp.mean(values * values, axis=1, keepdims=True) + norm_eps)


class Carried:
    def __init__(self, line, collective, gathers=(), reduces=()):
        self.line, self.collective = line, collective
        self.gathers, self.reduces = list(gathers), list(reduces)
        self.operands = list(self.gathers)
        self.results = []
        shards = lax.axis_size("shard")
        for part in self.gathers:
            self.results.append(jax.ShapeDtypeStruct((shards,) + part.shape, part.dtype))
        self.scratch = gather_scratch(line, len(self.gathers)) if self.gathers else []
        self.plans = []
        chunks = 0
        for grads in self.reduces:
            plan = [reduce_chunks(grad.shape) for grad in grads]
            self.plans.append(plan)
            chunks += sum(count for _, count in plan)
            self.operands += grads
            columns = sum(grad.shape[2] for grad in grads)
            self.results.append(jax.ShapeDtypeStruct((grads[0].shape[1], columns), jnp.float32))
        if chunks:
            copies = reduce_count(line)
            self.scratch += [
                pltpu.SemaphoreType.DMA((chunks, 2)),
                pltpu.SemaphoreType.DMA((chunks, copies)),
                pltpu.SemaphoreType.DMA((chunks, copies)),
            ]
        for grads, plan in zip(self.reduces, self.plans):
            for grad, (width, count) in zip(grads, plan):
                for _ in range(count):
                    self.scratch += reduce_scratch(line, grad.shape[0], grad.shape[1] // 2, width, grad.dtype)

    def rows(self, net, operands, results, scratch):
        lists = []
        if self.gathers:
            local, send, recv = scratch[:3]
            scratch = scratch[3:]
            for index in range(len(self.gathers)):
                lists.append(
                    gather_steps(
                        net, operands[index], results[index], local.at[index], send.at[index], recv.at[index]
                    )
                )
        operands, results = operands[len(self.gathers) :], results[len(self.gathers) :]
        if self.reduces:
            local, send, recv = scratch[:3]
            scratch = scratch[3:]
        number = 0
        for target, (grads, plan) in enumerate(zip(self.reduces, self.plans)):
            start = 0
            for grad, (width, count) in zip(grads, plan):
                source = operands[0]
                operands = operands[1:]
                for chunk in range(count):
                    lists.append(
                        reduce_steps(
                            net,
                            source,
                            results[target],
                            chunk * width,
                            start + chunk * width,
                            scratch[:REDUCE_BUFFERS],
                            local.at[number],
                            send.at[number],
                            recv.at[number],
                        )
                    )
                    scratch = scratch[REDUCE_BUFFERS:]
                    number += 1
                start += grad.shape[2]
        return staggered(lists)


def carry(body, carried, *, grid, out_shape, in_specs, out_specs, scratch_shapes, name, operands, head=0):
    if carried is None:
        return list(
            pl.pallas_call(
                body,
                grid=(grid,),
                out_shape=out_shape,
                in_specs=in_specs,
                out_specs=out_specs,
                scratch_shapes=scratch_shapes,
                compiler_params=pltpu.CompilerParams(vmem_limit_bytes=60 << 20),
                name=name,
            )(*operands)
        ), []
    counts = [len(in_specs), len(carried.operands), len(out_specs), len(carried.results), len(scratch_shapes)]
    ends = [sum(counts[: i + 1]) for i in range(len(counts))]

    def kernel(*refs):
        own_in, more_in = refs[: ends[0]], refs[ends[0] : ends[1]]
        own_out, more_out = refs[ends[1] : ends[2]], refs[ends[2] : ends[3]]
        own_scratch, more_scratch = refs[ends[3] : ends[4]], refs[ends[4] :]
        step = pl.program_id(0)
        net = Net(carried.line)
        rows = carried.rows(net, more_in, more_out, more_scratch)
        pl.when(step == 0)(net.greet)
        middle = rows[:-1]
        at = [head + (index * (grid - head)) // len(middle) for index in range(len(middle))]
        at[0] = 0
        for place in sorted(set(at)):

            @pl.when(step == place)
            def _():
                for index, row in enumerate(middle):
                    if at[index] == place:
                        for action in row:
                            action()

        body(*own_in, *own_out, *own_scratch)

        @pl.when(step == grid - 1)
        def _():
            for action in rows[-1]:
                action()

    results = pl.pallas_call(
        kernel,
        grid=(grid,),
        out_shape=list(out_shape) + carried.results,
        in_specs=list(in_specs) + [ANY] * len(carried.operands),
        out_specs=list(out_specs) + [ANY] * len(carried.results),
        scratch_shapes=list(scratch_shapes) + carried.scratch,
        compiler_params=pltpu.CompilerParams(
            collective_id=carried.collective, has_side_effects=True, vmem_limit_bytes=63 << 20
        ),
        name=name,
    )(*operands, *carried.operands)
    return list(results[: len(out_shape)]), list(results[len(out_shape) :])


def carry_alone(carried, name):
    return carry(
        lambda: None,
        carried,
        grid=1,
        out_shape=[],
        in_specs=[],
        out_specs=[],
        scratch_shapes=[],
        name=name,
        operands=[],
    )[1]


def whole(*shape):
    return pl.BlockSpec(shape, lambda step: (0,) * len(shape), pipeline_mode=pl.Buffered(1))


def like(shape, dtype):
    return jax.ShapeDtypeStruct(shape, dtype)


def project_kernel(turned, x_ref, gain_ref, w_ref, cos_ref, sin_ref, out_ref, normed_ref):
    step = pl.program_id(0)

    @pl.when(step == 0)
    def _():
        values = x_ref[...].astype(jnp.float32)
        normed = values * inverse_rms(values) * gain_ref[...]
        normed_ref[...] = normed.T.astype(jnp.bfloat16)

    out = product(w_ref[...], normed_ref[...], ROWS_BY_ROWS)

    @pl.when(step < turned)
    def _():
        cos, sin = cos_ref[...], sin_ref[...]
        half = cos.shape[0]
        for start in range(0, out.shape[0], 2 * half):
            first, second = out[start : start + half], out[start + half : start + 2 * half]
            out_ref[start : start + half, :] = (first * cos - second * sin).astype(jnp.bfloat16)
            out_ref[start + half : start + 2 * half, :] = (second * cos + first * sin).astype(jnp.bfloat16)

    @pl.when(step >= turned)
    def _():
        out_ref[...] = out.astype(jnp.bfloat16)


def project(x, gain, weight, cos_t, sin_t, carried):
    rows, width = x.shape
    columns = weight.shape[1]
    block = 512
    return carry(
        functools.partial(project_kernel, 2 * width // block),
        carried,
        grid=columns // block,
        out_shape=[like((columns, rows), jnp.bfloat16), like((width, rows), jnp.bfloat16)],
        in_specs=[
            whole(rows, width),
            whole(1, width),
            pl.BlockSpec((width, block), lambda step: (0, step)),
            whole(*cos_t.shape),
            whole(*sin_t.shape),
        ],
        out_specs=[
            pl.BlockSpec((block, rows), lambda step: (step, 0)),
            pl.BlockSpec((width, rows), lambda step: (0, 0)),
        ],
        scratch_shapes=[],
        name="project",
        operands=[x, gain, weight, cos_t, sin_t],
    )


def branch_kernel(att_ref, w_ref, x_ref, gain_ref, hidden_ref, normed_ref):
    hidden = x_ref[...].astype(jnp.float32) + product(att_ref[...], w_ref[...], ROWS_BY_ROWS)
    hidden_ref[...] = hidden
    normed_ref[...] = (hidden * inverse_rms(hidden) * gain_ref[...]).astype(jnp.bfloat16)


def branch(attended_t, weight, x, gain, carried):
    rows, width = x.shape
    block = 256
    row = pl.BlockSpec((block, width), lambda step: (step, 0))
    return carry(
        branch_kernel,
        carried,
        grid=rows // block,
        out_shape=[like((rows, width), jnp.float32), like((rows, width), jnp.bfloat16)],
        in_specs=[
            pl.BlockSpec((width, block), lambda step: (0, step)),
            whole(*weight.shape),
            row,
            whole(1, width),
        ],
        out_specs=[row, row],
        scratch_shapes=[],
        name="branch",
        operands=[attended_t, weight, x, gain],
    )


def widen_kernel(normed_ref, gate_ref, up_ref, act_ref, to_gate_ref, to_up_ref):
    normed = normed_ref[...]
    gate = product(normed, gate_ref[...])
    up = product(normed, up_ref[...])
    sigmoid = jax.nn.sigmoid(gate)
    swish = gate * sigmoid
    act_ref[...] = (swish * up).astype(jnp.bfloat16)
    to_gate_ref[...] = (up * sigmoid * (1.0 + gate * (1.0 - sigmoid))).astype(jnp.bfloat16)
    to_up_ref[...] = swish.astype(jnp.bfloat16)


def widen(normed, weight, carried):
    rows, width = normed.shape
    inner = weight.shape[1] // 2
    block = 512
    steps = inner // block
    part = pl.BlockSpec((rows, block), lambda step: (0, step))
    return carry(
        widen_kernel,
        carried,
        grid=steps,
        out_shape=[like((rows, inner), jnp.bfloat16)] * 3,
        in_specs=[
            whole(rows, width),
            pl.BlockSpec((width, block), lambda step: (0, step)),
            pl.BlockSpec((width, block), lambda step: (0, steps + step)),
        ],
        out_specs=[part] * 3,
        scratch_shapes=[],
        name="widen",
        operands=[normed, weight, weight],
    )


def narrow_kernel(
    steps, act_ref, to_gate_ref, to_up_ref, w_ref, given_ref, hidden_ref, result_ref, grad_ref, d_gate_ref, d_up_ref, acc_ref
):
    step = pl.program_id(0)
    act, weight, given = act_ref[...], w_ref[...], given_ref[...]
    part = product(act, weight)

    @pl.when(step == 0)
    def _():
        acc_ref[...] = hidden_ref[...] + part

    @pl.when(step > 0)
    def _():
        acc_ref[...] += part

    @pl.when(step == steps - 1)
    def _():
        result_ref[...] = acc_ref[...].astype(jnp.bfloat16)

    grad_ref[...] = product(act, given, ROWS_BY_ROWS).astype(jnp.bfloat16)
    d_act = product(given, weight, COLUMNS_BY_COLUMNS)
    d_gate_ref[...] = (d_act * to_gate_ref[...].astype(jnp.float32)).astype(jnp.bfloat16)
    d_up_ref[...] = (d_act * to_up_ref[...].astype(jnp.float32)).astype(jnp.bfloat16)


def narrow(act, to_gate, to_up, weight, given, hidden, carried):
    rows, inner = act.shape
    width = weight.shape[1]
    block = 512
    steps = inner // block
    part = pl.BlockSpec((rows, block), lambda step: (0, step))
    down = pl.BlockSpec((block, width), lambda step: (step, 0))
    return carry(
        functools.partial(narrow_kernel, steps),
        carried,
        grid=steps,
        out_shape=[
            like((rows, width), jnp.bfloat16),
            like((inner, width), jnp.bfloat16),
            like((rows, inner), jnp.bfloat16),
            like((rows, inner), jnp.bfloat16),
        ],
        in_specs=[part, part, part, down, whole(rows, width), whole(rows, width)],
        out_specs=[pl.BlockSpec((rows, width), lambda step: (0, 0)), down, part, part],
        scratch_shapes=[pltpu.VMEM((rows, width), jnp.float32)],
        name="narrow",
        operands=[act, to_gate, to_up, weight, given, hidden],
    )


def grad_in_kernel(normed_ref, d_gate_ref, d_up_ref, to_gate_ref, to_up_ref, turned_ref):
    @pl.when(pl.program_id(0) == 0)
    def _():
        turned_ref[...] = normed_ref[...].T

    to_gate_ref[...] = product(turned_ref[...], d_gate_ref[...]).astype(jnp.bfloat16)
    to_up_ref[...] = product(turned_ref[...], d_up_ref[...]).astype(jnp.bfloat16)


def grad_into(normed, d_gate, d_up, carried):
    rows, width = normed.shape
    inner = d_gate.shape[1]
    block = 512
    part = pl.BlockSpec((rows, block), lambda step: (0, step))
    out = pl.BlockSpec((width, block), lambda step: (0, step))
    return carry(
        grad_in_kernel,
        carried,
        grid=inner // block,
        out_shape=[like((width, inner), jnp.bfloat16)] * 2,
        in_specs=[whole(rows, width), part, part],
        out_specs=[out, out],
        scratch_shapes=[pltpu.VMEM((width, rows), jnp.bfloat16)],
        name="grad_in",
        operands=[normed, d_gate, d_up],
    )


def norm_back(d_normed, values, gain):
    inverse = inverse_rms(values)
    unit = values * inverse
    scaled = d_normed * gain
    mean = jnp.mean(scaled * unit, axis=1, keepdims=True)
    return inverse * (scaled - unit * mean), jnp.sum(d_normed * unit, axis=0, keepdims=True)


def ffn_back_kernel(
    steps, d_gate_ref, d_up_ref, gate_ref, up_ref, hidden_ref, gain_ref, given_ref, d_hidden_ref, d_branch_ref, grad_gain_ref, acc_ref
):
    step = pl.program_id(0)
    part = product(d_gate_ref[...], gate_ref[...], COLUMNS_BY_COLUMNS)
    part = part + product(d_up_ref[...], up_ref[...], COLUMNS_BY_COLUMNS)

    @pl.when(step == 0)
    def _():
        acc_ref[...] = part

    @pl.when(step > 0)
    def _():
        acc_ref[...] += part

    @pl.when(step == steps - 1)
    def _():
        through, grad_gain = norm_back(acc_ref[...], hidden_ref[...], gain_ref[...])
        d_hidden = given_ref[...].astype(jnp.float32) + through
        d_hidden_ref[...] = d_hidden
        d_branch_ref[...] = d_hidden.astype(jnp.bfloat16)
        grad_gain_ref[...] = grad_gain


def ffn_back(d_gate, d_up, weight, hidden, gain, given, carried):
    rows, width = hidden.shape
    inner = d_gate.shape[1]
    block = 512
    steps = inner // block
    part = pl.BlockSpec((rows, block), lambda step: (0, step))
    full = pl.BlockSpec((rows, width), lambda step: (0, 0))
    return carry(
        functools.partial(ffn_back_kernel, steps),
        carried,
        grid=steps,
        out_shape=[
            like((rows, width), jnp.float32),
            like((rows, width), jnp.bfloat16),
            like((1, width), jnp.float32),
        ],
        in_specs=[
            part,
            part,
            pl.BlockSpec((width, block), lambda step: (0, step)),
            pl.BlockSpec((width, block), lambda step: (0, steps + step)),
            whole(rows, width),
            whole(1, width),
            whole(rows, width),
        ],
        out_specs=[full, full, pl.BlockSpec((1, width), lambda step: (0, 0))],
        scratch_shapes=[pltpu.VMEM((rows, width), jnp.float32)],
        name="ffn_back",
        operands=[d_gate, d_up, weight, weight, hidden, gain, given],
    )


def branch_back_kernel(att_ref, w_ref, d_branch_ref, grad_ref, given_ref):
    d_branch = d_branch_ref[...]
    grad_ref[...] = product(att_ref[...], d_branch).astype(jnp.bfloat16)
    given_ref[...] = product(w_ref[...], d_branch, COLUMNS_BY_COLUMNS).astype(jnp.bfloat16)


def branch_back(attended_t, weight, d_branch, carried):
    rows, width = d_branch.shape
    block = 256
    out = pl.BlockSpec((block, width), lambda step: (step, 0))
    turned = pl.BlockSpec((block, rows), lambda step: (step, 0))
    return carry(
        branch_back_kernel,
        carried,
        grid=attended_t.shape[0] // block,
        out_shape=[like(weight.shape, jnp.bfloat16), like(attended_t.shape, jnp.bfloat16)],
        in_specs=[turned, out, whole(rows, width)],
        out_specs=[out, turned],
        scratch_shapes=[],
        name="branch_back",
        operands=[attended_t, weight, d_branch],
    )


def project_back_kernel(
    steps, normed_ref, dq_ref, dk_ref, dv_ref, w_ref, x_ref, gain_ref, d_hidden_ref, grad_ref, tokens_ref, grad_gain_ref, acc_ref
):
    step = pl.program_id(0)
    third = steps // 3

    def run(d_ref):
        d_part = d_ref[...]
        grad_ref[...] = product(normed_ref[...], d_part, COLUMNS_BY_COLUMNS).astype(jnp.bfloat16)
        part = product(w_ref[...], d_part)

        @pl.when(step == 0)
        def _():
            acc_ref[...] = part

        @pl.when(step > 0)
        def _():
            acc_ref[...] += part

    for index, d_ref in enumerate((dq_ref, dk_ref, dv_ref)):
        pl.when(step // third == index)(functools.partial(run, d_ref))

    @pl.when(step == steps - 1)
    def _():
        values = x_ref[...].astype(jnp.float32)
        through, grad_gain = norm_back(acc_ref[...].T, values, gain_ref[...])
        tokens_ref[...] = d_hidden_ref[...] + through
        grad_gain_ref[...] = grad_gain


def project_back(normed_t, dq, dk, dv, weight, x, gain, d_hidden, carried):
    rows, width = x.shape
    columns = weight.shape[1]
    block = 512
    steps = columns // block
    third = steps // 3
    full = pl.BlockSpec((rows, width), lambda step: (0, 0))

    def part(which):
        return pl.BlockSpec(
            (block, rows), lambda step: (jnp.clip(step - which * third, 0, third - 1), 0)
        )

    return carry(
        functools.partial(project_back_kernel, steps),
        carried,
        grid=steps,
        out_shape=[
            like((width, columns), jnp.bfloat16),
            like((rows, width), jnp.float32),
            like((1, width), jnp.float32),
        ],
        in_specs=[
            whole(*normed_t.shape),
            part(0),
            part(1),
            part(2),
            pl.BlockSpec((width, block), lambda step: (0, step)),
            whole(rows, width),
            whole(1, width),
            whole(rows, width),
        ],
        out_specs=[
            pl.BlockSpec((width, block), lambda step: (0, step)),
            full,
            pl.BlockSpec((1, width), lambda step: (0, 0)),
        ],
        scratch_shapes=[pltpu.VMEM((width, rows), jnp.float32)],
        name="project_back",
        operands=[normed_t, dq, dk, dv, weight, x, gain, d_hidden],
    )


LOG2E = 1.4426950408889634
FEATURES = 16


def two_parts(value):
    high = value.astype(jnp.bfloat16)
    return high, (value - high.astype(jnp.float32)).astype(jnp.bfloat16)


def three_parts(value):
    high, rest = value.astype(jnp.bfloat16), None
    rest = value - high.astype(jnp.float32)
    middle = rest.astype(jnp.bfloat16)
    return high, middle, (rest - middle.astype(jnp.float32)).astype(jnp.bfloat16)


def key_features(variates, valid):
    length = variates.shape[1]
    masks = [(variates == v).astype(jnp.float32) for v in range(4)]
    ones = jnp.ones((1, length), jnp.float32)
    invalid = 1.0 - valid
    rows = masks + masks + [invalid, ones, ones, ones, jnp.zeros((FEATURES - 12, length), jnp.float32)]
    return jnp.concatenate(rows, axis=0).astype(jnp.bfloat16)


def query_features(variates, same, other, log_sums):
    length = variates.shape[1]
    highs, lows = [], []
    for v in range(4):
        bias = jnp.where(variates == v, same, other) * LOG2E
        high, low = two_parts(bias)
        highs.append(high.astype(jnp.float32))
        lows.append(low.astype(jnp.float32))
    if log_sums is None:
        minus = [jnp.zeros((3, length), jnp.float32)]
    else:
        minus = [part.astype(jnp.float32) for part in three_parts(-log_sums)]
    mask = jnp.full((1, length), masked_score, jnp.float32)
    rows = highs + lows + [mask] + minus + [jnp.zeros((FEATURES - 12, length), jnp.float32)]
    return jnp.concatenate(rows, axis=0).astype(jnp.bfloat16)


def contract_depth(first_op, second_op):
    return lax.dot_general(
        first_op, second_op, (((1,), (0,)), ((), ())), preferred_element_type=jnp.float32
    )


def scaled_query(query_t, score_scale):
    return two_parts(query_t.astype(jnp.float32) * (score_scale * LOG2E))


def attend_kernel(blocks, bias_ref, q_ref, k_ref, v_ref, var_ref, valid_ref, o_ref, wide_ref, lse_ref, query_ref):
    head = pl.program_id(0)
    depth, length = q_ref.shape
    width = length // blocks
    same, other = bias_ref[0, head], bias_ref[1, head]
    variates = var_ref[...]
    high, low = scaled_query(q_ref[...], depth ** (-0.5))
    query_ref[...] = jnp.concatenate([high, low, query_features(variates, same, other, None)], axis=0)
    key_t = k_ref[...]
    keys = jnp.concatenate([key_t, key_t, key_features(variates, valid_ref[...])], axis=0).T
    ones = jnp.concatenate(
        [jnp.ones((1, length), jnp.float32), jnp.zeros((FEATURES - 1, length), jnp.float32)], axis=0
    ).astype(jnp.bfloat16)
    values = jnp.concatenate([v_ref[...], ones], axis=0)
    for block in range(blocks):
        at = pl.ds(block * width, width)
        scores = contract_depth(keys, query_ref[:, at])
        peak = jnp.max(scores, axis=0, keepdims=True)
        weights = jnp.exp2(scores - peak).astype(jnp.bfloat16)
        summed = contract_depth(values, weights)
        total = summed[depth : depth + 1]
        attended = summed[:depth] / total
        wide_ref[:, at] = attended
        o_ref[:, at] = attended.astype(jnp.bfloat16)
        lse_ref[0, :, at] = peak + jnp.log2(total)


def attend_forward(qkv_t, variates, valid, bias, heads, carried):
    rows, length = qkv_t.shape
    depth = rows // (3 * heads)

    def part(which):
        return pl.BlockSpec((depth, length), lambda head: (which * heads + head, 0))

    row = pl.BlockSpec((1, length), lambda head: (0, 0))
    return carry(
        functools.partial(attend_kernel, 1),
        carried,
        grid=heads,
        out_shape=[
            jax.ShapeDtypeStruct((heads * depth, length), jnp.bfloat16),
            jax.ShapeDtypeStruct((heads * depth, length), jnp.float32),
            jax.ShapeDtypeStruct((heads, 1, length), jnp.float32),
        ],
        in_specs=[
            pl.BlockSpec(memory_space=pltpu.SMEM),
            part(0),
            part(1),
            part(2),
            row,
            row,
        ],
        out_specs=[
            pl.BlockSpec((depth, length), lambda head: (head, 0)),
            pl.BlockSpec((depth, length), lambda head: (head, 0)),
            pl.BlockSpec((1, 1, length), lambda head: (head, 0, 0)),
        ],
        scratch_shapes=[pltpu.VMEM((2 * depth + FEATURES, length), jnp.bfloat16)],
        name="attend_forward",
        operands=[bias, qkv_t, qkv_t, qkv_t, variates, valid],
    )


def turn_back(grad_t, cos_t, sin_t):
    half = cos_t.shape[0]
    first, second = grad_t[:half], grad_t[half:]
    return jnp.concatenate(
        [first * cos_t + second * sin_t, second * cos_t - first * sin_t], axis=0
    )


def attend_back_kernel(
    blocks, bias_ref, q_ref, k_ref, v_ref, go_ref, wide_ref, lse_ref, var_ref, valid_ref, cos_ref, sin_ref,
    dq_ref, dk_ref, dv_ref, db_ref, query_ref, given_ref, dk_acc, dv_acc,
):
    head = pl.program_id(0)
    depth, length = q_ref.shape
    width = length // blocks
    scale = depth ** (-0.5)
    same, other = bias_ref[0, head], bias_ref[1, head]
    variates = var_ref[...]
    features = key_features(variates, valid_ref[...])
    high, low = scaled_query(q_ref[...], scale)
    query_ref[...] = jnp.concatenate([high, low, query_features(variates, same, other, lse_ref[0])], axis=0)
    key_t = k_ref[...]
    keys = jnp.concatenate([key_t, key_t, features], axis=0).T
    keys_low = jnp.concatenate([key_t, features], axis=0)
    given = go_ref[...]
    inner = jnp.sum(given.astype(jnp.float32) * wide_ref[...], axis=0, keepdims=True)
    minus = [part.astype(jnp.float32) for part in three_parts(-inner)]
    minus = jnp.concatenate(minus + [jnp.zeros((FEATURES - 3, length), jnp.float32)], axis=0)
    given_ref[...] = jnp.concatenate([given, minus.astype(jnp.bfloat16)], axis=0)
    ones = jnp.concatenate(
        [jnp.ones((3, length), jnp.float32), jnp.zeros((FEATURES - 3, length), jnp.float32)], axis=0
    ).astype(jnp.bfloat16)
    values = jnp.concatenate([v_ref[...], ones], axis=0).T
    query_rows = q_ref[...].T
    given_rows = given.T
    in_same = jnp.zeros((1, width), jnp.float32)
    in_other = jnp.zeros((1, width), jnp.float32)
    for block in range(blocks):
        at = pl.ds(block * width, width)
        cut = slice(block * width, (block + 1) * width)
        probs = jnp.exp2(contract_depth(keys, query_ref[:, at]))
        grads = (probs * contract_depth(values, given_ref[:, at])).astype(jnp.bfloat16)
        back = contract_depth(keys_low, grads)
        dq = turn_back(back[:depth] * scale, cos_ref[:, at], sin_ref[:, at])
        dq_ref[:, at] = dq.astype(jnp.bfloat16)
        for v in range(4):
            line = back[depth + v : depth + v + 1]
            hit = variates[:, cut] == v
            in_same = in_same + jnp.where(hit, line, 0.0)
            in_other = in_other + jnp.where(hit, 0.0, line)
        dk = contract_depth(grads, query_rows[cut])
        dv = contract_depth(probs.astype(jnp.bfloat16), given_rows[cut])
        if block == 0:
            dk_acc[...] = dk
            dv_acc[...] = dv
        else:
            dk_acc[...] += dk
            dv_acc[...] += dv
    dk_ref[...] = turn_back((dk_acc[...] * scale).T, cos_ref[...], sin_ref[...]).astype(jnp.bfloat16)
    dv_ref[...] = dv_acc[...].T.astype(jnp.bfloat16)
    db_ref[0, 0:1, :] = in_same
    db_ref[0, 1:2, :] = in_other


def attend_backward(qkv_t, given_t, wide_t, log_sums, variates, valid, bias, cos_t, sin_t, heads, carried):
    rows, length = qkv_t.shape
    depth = rows // (3 * heads)
    blocks = 1

    def part(which):
        return pl.BlockSpec((depth, length), lambda head: (which * heads + head, 0))

    one = pl.BlockSpec((depth, length), lambda head: (head, 0))
    grad = jax.ShapeDtypeStruct((heads * depth, length), jnp.bfloat16)
    return carry(
        functools.partial(attend_back_kernel, blocks),
        carried,
        grid=heads,
        out_shape=[grad, grad, grad, jax.ShapeDtypeStruct((heads, 2, length // blocks), jnp.float32)],
        in_specs=[
            pl.BlockSpec(memory_space=pltpu.SMEM),
            part(0),
            part(1),
            part(2),
            one,
            one,
            pl.BlockSpec((1, 1, length), lambda head: (head, 0, 0)),
            whole(1, length),
            whole(1, length),
            whole(depth // 2, length),
            whole(depth // 2, length),
        ],
        out_specs=[one, one, one, pl.BlockSpec((1, 2, length // blocks), lambda head: (head, 0, 0))],
        scratch_shapes=[
            pltpu.VMEM((2 * depth + FEATURES, length), jnp.bfloat16),
            pltpu.VMEM((depth + FEATURES, length), jnp.bfloat16),
            pltpu.VMEM((length, depth), jnp.float32),
            pltpu.VMEM((length, depth), jnp.float32),
        ],
        name="attend_backward",
        operands=[bias, qkv_t, qkv_t, qkv_t, given_t, wide_t, log_sums, variates, valid, cos_t, sin_t],
    )


def rope_tables(time_ids):
    half = HEAD_DIM // 2
    exponent = jnp.arange(half).astype(jnp.float32) * (2.0 / HEAD_DIM)
    inverse = jnp.exp(-jnp.log(rope_base) * exponent)
    angles = inverse[:, None] * time_ids.astype(jnp.float32)
    return jnp.cos(angles), jnp.sin(angles)


def pack_small(attn_gain, ffn_gain, attn_bias):
    heads = attn_bias.shape[1]
    small = jnp.zeros((16, 128), jnp.float32)
    small = small.at[0].set(attn_gain.astype(jnp.float32)).at[1].set(ffn_gain.astype(jnp.float32))
    return small.at[2:4, :heads].set(attn_bias.astype(jnp.float32))


def pack_grads(shards, gain_one, gain_two, bias):
    heads = bias.shape[1] // shards
    small = jnp.zeros((shards, 16, 128), jnp.float32)
    small = small.at[:, 0].set(gain_one.reshape(shards, -1)).at[:, 1].set(gain_two.reshape(shards, -1))
    return small.at[:, 2:4, :heads].set(jnp.swapaxes(bias.reshape(2, shards, heads), 0, 1))


def shards(
    line,
    tokens,
    lengths,
    variate_ids,
    time_ids,
    attn_gain,
    w_qkv,
    attn_bias,
    w_out,
    ffn_gain,
    w_in,
    w_down,
    cotangent,
):
    parts = lax.axis_size("shard")
    length = variate_ids.shape[1]
    heads = attn_bias.shape[1]
    positions = jnp.arange(length)[None, :]
    key_valid = positions < lengths[:, None]
    valid = key_valid.astype(jnp.float32)
    given = jnp.where(key_valid.reshape(length, 1), cotangent, jnp.zeros_like(cotangent))
    cos_t, sin_t = rope_tables(time_ids)

    def joined(part):
        return part.reshape(-1, part.shape[2])

    def cut(grad):
        return grad.reshape(parts, -1, grad.shape[1])

    def gathering(number, *weights):
        return Carried(line, number, gathers=weights) if line else None

    def reducing(number, *grads):
        return Carried(line, number, reduces=grads) if line else None

    if line:
        small, full_qkv = carry_alone(gathering(1, pack_small(attn_gain, ffn_gain, attn_bias), w_qkv), "gather_qkv")
        qkv_weight = joined(full_qkv)
        gain_one, gain_two = small[:, 0].reshape(1, -1), small[:, 1].reshape(1, -1)
        bias = jnp.swapaxes(small[:, 2:4, :heads], 0, 1).reshape(2, -1)
    else:
        gain_one, gain_two, qkv_weight, out_weight, in_weight, down_weight = (
            lax.all_gather(part, "shard", axis=0, tiled=True)
            for part in (attn_gain, ffn_gain, w_qkv, w_out, w_in, w_down)
        )
        bias = lax.all_gather(attn_bias, "shard", axis=1, tiled=True).astype(jnp.float32)
        gain_one = gain_one.astype(jnp.float32).reshape(1, -1)
        gain_two = gain_two.astype(jnp.float32).reshape(1, -1)

    (qkv_t, normed_t), came = project(tokens, gain_one, qkv_weight, cos_t, sin_t, gathering(2, w_out))
    out_weight = joined(came[0]) if line else out_weight
    (attended_t, wide_t, log_sums), came = attend_forward(
        qkv_t, variate_ids, valid, bias, HEADS, gathering(3, w_in)
    )
    in_weight = joined(came[0]) if line else in_weight
    (hidden, normed_two), _ = branch(attended_t, out_weight, tokens, gain_two, None)
    (act, to_gate, to_up), came = widen(normed_two, in_weight, gathering(4, w_down))
    down_weight = joined(came[0]) if line else down_weight
    (result, grad_down, d_gate, d_up), _ = narrow(act, to_gate, to_up, down_weight, given, hidden, None)
    (grad_gate, grad_up), _ = grad_into(normed_two, d_gate, d_up, None)
    (d_hidden, d_branch, grad_gain_two), came_down = ffn_back(
        d_gate, d_up, in_weight, hidden, gain_two, given, reducing(5, [cut(grad_down)])
    )
    (grad_out, given_t), _ = branch_back(attended_t, out_weight, d_branch, None)
    (dq, dk, dv, bias_parts), came_in = attend_backward(
        qkv_t,
        given_t,
        wide_t,
        log_sums,
        variate_ids,
        valid,
        bias,
        cos_t,
        sin_t,
        HEADS,
        reducing(6, [cut(grad_gate), cut(grad_up)]),
    )
    (grad_qkv, grad_tokens, grad_gain_one), came_out = project_back(
        normed_t, dq, dk, dv, qkv_weight, tokens, gain_one, d_hidden, reducing(7, [cut(grad_out)])
    )
    grad_bias = jnp.sum(bias_parts, axis=2).T
    if line:
        packed = pack_grads(parts, grad_gain_one, grad_gain_two, grad_bias)
        sum_qkv, small = carry_alone(reducing(8, [cut(grad_qkv)], [packed]), "reduce_qkv")
        return (
            result,
            grad_tokens,
            small[0],
            sum_qkv,
            small[2:4, :heads],
            came_out[0],
            small[1],
            came_in[0],
            came_down[0],
        )
    grads = (
        (grad_gain_one.reshape(-1), 0),
        (grad_qkv, 0),
        (grad_bias, 1),
        (grad_out, 0),
        (grad_gain_two.reshape(-1), 0),
        (jnp.concatenate([grad_gate, grad_up], axis=1), 0),
        (grad_down, 0),
    )
    owned = [
        lax.psum_scatter(grad.astype(jnp.bfloat16), "shard", scatter_dimension=axis, tiled=True)
        for grad, axis in grads
    ]
    return (result, grad_tokens) + tuple(lax.psum(part, "rep").astype(jnp.float32) for part in owned)


def solution(mesh):
    placed = (
        P(("shard", "rep"), None),
        P(("shard", "rep")),
        P(("shard", "rep"), None),
        P(("shard", "rep"), None),
        P("shard"),
        P("shard", None),
        P(None, "shard"),
        P("shard", None),
        P("shard"),
        P("shard", None),
        P("shard", None),
        P(("shard", "rep"), None),
    )
    line = mesh.shape["shard"] // 2 if (mesh.shape["shard"], mesh.shape["rep"]) == (8, 4) else 0
    return jax.shard_map(
        functools.partial(shards, line),
        mesh=mesh,
        in_specs=placed,
        out_specs=(
            P(("shard", "rep"), None),
            P(("shard", "rep"), None),
            P("shard"),
            P("shard", None),
            P(None, "shard"),
            P("shard", None),
            P("shard"),
            P("shard", None),
            P("shard", None),
        ),
        check_vma=False,
    )
```

time: 955 us -> 660 us (0.69)
  matrix products: 372 us -> 0 us
  Pallas kernels: 394 us -> 623 us
  other arithmetic: 129 us -> 7.76 us
  local copies, waits for them, and re-layouts: 51.5 us -> 19.3 us
    dot_general x24 -> x0, matrix products: 372 us -> none  [the longest x4 67.4 us: times_transpose(): lax.dot_general(first_op, second_op, (((1,), (1,)), ((), ())), preferred_...]
    pallas_call x4 -> x12, Pallas kernels: 394 us -> 623 us  [the longest x8 544 us: carry(): pl.pallas_call(kernel, grid=(grid,), out_shape=list(out_shape) + carried....]
    dot_general x1 -> x0, other arithmetic: 57.1 us -> none  [attend_backward(): jnp.einsum('hqk,qk->h', d_scores, same_mask, preferred_element_type=jnp.f...]
    reduce_sum x3 -> x1, other arithmetic: 29.2 us -> 0.12 us  [shards(): grad_bias = jnp.sum(bias_parts, axis=2).T]
    unnamed x86 -> x21, local copies, waits for them, and re-layouts: 33.9 us -> 12.2 us
    add x5 -> x0, other arithmetic: 12 us -> none  [the longest x1 6.58 us: shards(): grad_rows.astype(jnp.float32)]
where the time goes in v2:
time: 660 us; the launch traced here: 652 us
  Pallas kernels  623 us (94%)
  local copies, waits for them, and re-layouts  19.3 us (3%)
  other arithmetic  7.76 us (1%)
    pallas_call x8, Pallas kernels, carry(): pl.pallas_call(kernel, grid=(grid,), out_shape=list(out_shape) + carried....  544 us
    pallas_call x4, Pallas kernels, carry(): pl.pallas_call(body, grid=(grid,), out_shape=out_shape, in_specs=in_specs...  79.1 us

profile of v2, /device:TPU:1, one launch (start us, length us, event | category | flops | bytes accessed | tf_op | source)
XLA Modules:
  0.0 651.6 jit_solution(15892694630847402165)
XLA Ops:
  5.0 1.2 multiply_sine_fusion
  6.2 3.1 broadcast_select_fusion.given_ref.refs_6_
  9.3 44.5 %gather_qkv.1 = (f32[8,16,128]{2,1,0:T(8,128)}, bf16[8,128,3072]{2,1,0:T(8,128)(2,1)}) custom-call(f32[16,128]{1,0:T(8,128)} %copy-done.6, bf16[128,3072]{1,0:T(8,128)(2,1)} %refs_1_.1), custom_call_target="tpu_custom_call" | custom-call | tf_op jit(solution)/shard_map/gather_qkv/pallas_call | solution.py:546
  53.9 0.8 slice_bitcast_fusion
  54.7 1.4 slice_bitcast_fusion.1
  56.7 26.8 %project.1 = (bf16[3072,1024]{1,0:T(8,128)(2,1)}, bf16[1024,1024]{1,0:T(8,128)(2,1)}, bf16[8,128,1024]{2,1,0:T(8,128)(2,1)}) custom-call(bf16[1024,1024]{1,0:T(8,128)(2,1)} %refs_5_.3, f32[1,1024]{1,0:T(1,128)} %get-tuple-element.158.refs_1_.refs_6_, bf16[1024,3072]{1,0:T(8,128)(2,1)} %bitcast.37, f32[32,1024]{1,0:T(8,128)} %get-tuple-element.162.refs_3_.refs_9_, ...), custom_call_target="tpu_custom_call" | custom-call | tf_op jit(solution)/shard_map/project/pallas_call | solution.py:546
  83.6 89.6 %attend_forward.1 = (bf16[1024,1024]{1,0:T(8,128)(2,1)}, f32[1024,1024]{1,0:T(8,128)}, f32[16,1,1024]{2,1,0:T(1,128)}, bf16[8,128,8192]{2,1,0:T(8,128)(2,1)}) custom-call(f32[2,16]{1,0:T(2,128)} %reshape.260.refs_0_, bf16[3072,1024]{1,0:T(8,128)(2,1)} %get-tuple-element.121.refs_1_.refs_2_.refs_3_, ...), custom_call_target="tpu_custom_call" | custom-call | tf_op jit(solution)/shard_map/attend_forward/pallas_call | solution.py:546
  173.2 7.3 %branch.1 = (f32[1024,1024]{1,0:T(8,128)}, bf16[1024,1024]{1,0:T(8,128)(2,1)}) custom-call(bf16[1024,1024]{1,0:T(8,128)(2,1)} %get-tuple-element.122.att_ref, bf16[1024,1024]{1,0:T(8,128)(2,1)} %bitcast.42, bf16[1024,1024]{1,0:T(8,128)(2,1)} %refs_5_.3, f32[1,1024]{1,0:T(1,128)} %get-tuple-element.157.gain_ref.refs_5_), custom_call_target="tpu_custom_call" | custom-call | tf_op jit(solution)/shard_map/branch/pallas_call | solution.py:505
  180.5 52.2 %widen.1 = (bf16[1024,4096]{1,0:T(8,128)(2,1)}, bf16[1024,4096]{1,0:T(8,128)(2,1)}, bf16[1024,4096]{1,0:T(8,128)(2,1)}, bf16[8,512,1024]{2,1,0:T(8,128)(2,1)}) custom-call(bf16[1024,1024]{1,0:T(8,128)(2,1)} %get-tuple-element.124.refs_0_.normed_ref, bf16[1024,8192]{1,0:T(8,128)(2,1)} %bitcast.33, bf16[1024,8192]{1,0:T(8,128)(2,1)} %bitcast.34, ...), custom_call_target="tpu_custom_call" | custom-call | tf_op jit(solution)/shard_map/widen/pallas_call | solution.py:546
  232.8 40.5 %narrow.1 = (bf16[1024,1024]{1,0:T(8,128)(2,1)}, bf16[4096,1024]{1,0:T(8,128)(2,1)}, bf16[1024,4096]{1,0:T(8,128)(2,1)}, bf16[1024,4096]{1,0:T(8,128)(2,1)}) custom-call(bf16[1024,4096]{1,0:T(8,128)(2,1)} %get-tuple-element.126.act_ref, bf16[1024,4096]{1,0:T(8,128)(2,1)} %get-tuple-element.127.to_gate_ref, bf16[1024,4096]{1,0:T(8,128)(2,1)} %get-tuple-element.128.to_up_ref, ...), custom_call_target="tpu_custom_call" | custom-call | tf_op jit(solution)/shard_map/narrow/pallas_call | solution.py:505
  273.2 93.3 %ffn_back.1 = (f32[1024,1024]{1,0:T(8,128)}, bf16[1024,1024]{1,0:T(8,128)(2,1)}, f32[1,1024]{1,0:T(1,128)}, f32[512,1024]{1,0:T(8,128)}) custom-call(bf16[1024,4096]{1,0:T(8,128)(2,1)} %get-tuple-element.133.refs_0_.d_gate_ref, bf16[1024,4096]{1,0:T(8,128)(2,1)} %get-tuple-element.134.refs_1_.d_up_ref, bf16[1024,8192]{1,0:T(8,128)(2,1)} %bitcast.35, ...), custom_call_target="tpu_custom_call" | custom-call | tf_op jit(solution)/shard_map/ffn_back/pallas_call | solution.py:546
  366.6 23.1 %grad_in.1 = (bf16[1024,4096]{1,0:T(8,128)(2,1)}, bf16[1024,4096]{1,0:T(8,128)(2,1)}) custom-call(bf16[1024,1024]{1,0:T(8,128)(2,1)} %get-tuple-element.124.refs_0_.normed_ref, bf16[1024,4096]{1,0:T(8,128)(2,1)} %get-tuple-element.133.refs_0_.d_gate_ref, bf16[1024,4096]{1,0:T(8,128)(2,1)} %get-tuple-element.134.refs_1_.d_up_ref), custom_call_target="tpu_custom_call" | custom-call | tf_op jit(solution)/shard_map/grad_in/pallas_call | solution.py:505
  389.7 8.2 %branch_back.1 = (bf16[1024,1024]{1,0:T(8,128)(2,1)}, bf16[1024,1024]{1,0:T(8,128)(2,1)}) custom-call(bf16[1024,1024]{1,0:T(8,128)(2,1)} %get-tuple-element.122.att_ref, bf16[1024,1024]{1,0:T(8,128)(2,1)} %bitcast.43, bf16[1024,1024]{1,0:T(8,128)(2,1)} %get-tuple-element.136.d_branch_ref), custom_call_target="tpu_custom_call" | custom-call | tf_op jit(solution)/shard_map/branch_back/pallas_call | solution.py:505
  397.9 111.7 %attend_backward.1 = (bf16[1024,1024]{1,0:T(8,128)(2,1)}, bf16[1024,1024]{1,0:T(8,128)(2,1)}, bf16[1024,1024]{1,0:T(8,128)(2,1)}, f32[16,2,1024]{2,1,0:T(2,128)}, f32[128,8192]{1,0:T(8,128)}) custom-call(f32[2,16]{1,0:T(2,128)} %reshape.260.refs_0_, bf16[3072,1024]{1,0:T(8,128)(2,1)} %get-tuple-element.121.refs_1_.refs_2_.refs_3_, ...), custom_call_target="tpu_custom_call" | custom-call | tf_op jit(solution)/shard_map/attend_backward/pallas_call | solution.py:546
  509.5 54.6 %project_back.1 = (bf16[1024,3072]{1,0:T(8,128)(2,1)}, f32[1024,1024]{1,0:T(8,128)}, f32[1,1024]{1,0:T(1,128)}, f32[128,1024]{1,0:T(8,128)}) custom-call(bf16[1024,1024]{1,0:T(8,128)(2,1)} %get-tuple-element.132.refs_0_, bf16[1024,1024]{1,0:T(8,128)(2,1)} %get-tuple-element.142.refs_1_, bf16[1024,1024]{1,0:T(8,128)(2,1)} %get-tuple-element.143.refs_2_, ...), custom_call_target="tpu_custom_call" | custom-call | tf_op jit(solution)/shard_map/project_back/pallas_call | solution.py:546
  566.2 70.8 %reduce_qkv.1 = (f32[128,3072]{1,0:T(8,128)}, f32[16,128]{1,0:T(8,128)}) custom-call(bf16[8,128,3072]{2,1,0:T(8,128)(2,1)} %bitcast.45, f32[8,16,128]{2,1,0:T(8,128)} %copy-done.4), custom_call_target="tpu_custom_call" | custom-call | tf_op jit(solution)/shard_map/reduce_qkv/pallas_call | solution.py:546
  637.1 1.2 slice.142
  638.3 1.3 slice_bitcast_fusion.3
  639.6 4.9 copy.40
  644.6 1.1 copy.41
  645.9 0.8 copy.42
  646.7 2.1 copy.43
  648.9 1.0 copy-done.1
  649.9 1.3 copy.44
  (31 shorter events, 6.7 us)
Async XLA Ops:
  5.0 4.4 copy-start.6
  509.5 54.6 %copy-start.5 = (f32[16,2,1024]{2,1,0:T(2,128)S(1)}, f32[16,2,1024]{2,1,0:T(2,128)}, u32[]{:S(2)}) copy-start(f32[16,2,1024]{2,1,0:T(2,128)} %get-tuple-element.151) | copy-start | bytes 393220
  509.5 55.5 %copy-start.7 = (f32[1,1024]{1,0:T(1,128)S(1)}, f32[1,1024]{1,0:T(1,128)}, u32[]{:S(2)}) copy-start(f32[1,1024]{1,0:T(1,128)} %get-tuple-element.150) | copy-start | bytes 12292
  565.6 0.6 copy-start.4
  639.6 4.9 copy-start.2
  639.6 7.1 %copy-start = (f32[128,8192]{1,0:T(8,128)S(1)}, f32[128,8192]{1,0:T(8,128)}, u32[]{:S(2)}) copy-start(f32[128,8192]{1,0:T(8,128)} %get-tuple-element.179) | copy-start | bytes 12582916
  644.5 1.4 copy-start.3
  646.7 3.1 copy-start.1

commit v3 on v2

--- a/solution.py
+++ b/solution.py
@@ -58,7 +58,8 @@
 
 def gather_steps(net, source, full, local_sem, send_sem, recv_sem):
     line = net.line
-    half, columns = source.shape[0] // 2, source.shape[1]
+    height, columns = source.shape
+    half = height // 2
     split = columns % 1024 == 0
     only = columns * 3 // 8 if split else 0
     shared = columns - 2 * only
@@ -76,8 +77,12 @@
             device_id_type=MESH,
         )
 
+    def held(z, y, which=None):
+        lines = pl.ds(aligned((z * 2 + y) * height + net.core * half, half), half)
+        return full.at[lines] if which is None else full.at[lines, which]
+
     def piece(z, y):
-        return full.at[z * 2 + y, rows, carried]
+        return held(z, y, carried)
 
     def over_z(z, target, base):
         return remote(piece(z, net.y), piece(z, net.y), base + z, target)
@@ -86,15 +91,15 @@
         return remote(piece(z, net.y), piece(z, net.y), 2 * line + z, net.across_y)
 
     def over_x(z, y):
-        part = full.at[z * 2 + y, rows, lone]
+        part = held(z, y, lone)
         return remote(part, part, 3 * line + y * line + z, net.across_x)
 
     def to_core(z, y):
-        part = full.at[z * 2 + y, rows]
+        part = held(z, y)
         return remote(part, part, 5 * line + y * line + z, net.sibling)
 
     mine = source.at[rows, carried]
-    local = pltpu.make_async_copy(source, full.at[net.own], local_sem)
+    local = pltpu.make_async_copy(source, full.at[pl.ds(aligned(net.own * height, height), height)], local_sem)
     first_y = remote(mine, piece(net.z, net.y), 2 * line + net.z, net.across_y)
     first_up = remote(mine, piece(net.z, net.y), net.z, net.above)
     first_down = remote(mine, piece(net.z, net.y), line + net.z, net.below)
@@ -142,7 +147,7 @@
     def arrive_x(hops, own_y):
         def one(z):
             y = net.y if own_y else 1 - net.y
-            part = full.at[z * 2 + y, rows, pl.ds(aligned((1 - net.x) * (only + shared), 128), only)]
+            part = held(z, y, pl.ds(aligned((1 - net.x) * (only + shared), 128), only))
             remote(part, part, 3 * line + y * line + z, net.across_x).wait_recv()
             to_core(z, y).start()
 
@@ -435,7 +440,7 @@
         self.results = []
         shards = lax.axis_size("shard")
         for part in self.gathers:
-            self.results.append(jax.ShapeDtypeStruct((shards,) + part.shape, part.dtype))
+            self.results.append(jax.ShapeDtypeStruct((shards * part.shape[0], part.shape[1]), part.dtype))
         self.scratch = gather_scratch(line, len(self.gathers)) if self.gathers else []
         self.plans = []
         chunks = 0
@@ -1055,11 +1060,10 @@
     )
 
 
-def attend_back_kernel(
-    blocks, bias_ref, q_ref, k_ref, v_ref, go_ref, wide_ref, lse_ref, var_ref, valid_ref, cos_ref, sin_ref,
+def attend_back_head(
+    blocks, head, bias_ref, q_ref, k_ref, v_ref, go_ref, wide_ref, lse_ref, var_ref, valid_ref, cos_ref, sin_ref,
     dq_ref, dk_ref, dv_ref, db_ref, query_ref, given_ref, dk_acc, dv_acc,
 ):
-    head = pl.program_id(0)
     depth, length = q_ref.shape
     width = length // blocks
     scale = depth ** (-0.5)
@@ -1111,6 +1115,10 @@
     db_ref[0, 1:2, :] = in_other
 
 
+def attend_back_kernel(blocks, *refs):
+    attend_back_head(blocks, pl.program_id(0), *refs)
+
+
 def attend_backward(qkv_t, given_t, wide_t, log_sums, variates, valid, bias, cos_t, sin_t, heads, carried):
     rows, length = qkv_t.shape
     depth = rows // (3 * heads)
@@ -1151,6 +1159,698 @@
     )
 
 
+TILE = 512
+BLOCK = 1024
+KEPT, GIVEN, GOT, OVER_X, OVER_Y, OVER_Z, LATE, ENDS, WIDE = 13, 3, 4, 5, 5, 6, 4, 4, 3
+STAGES = (0, 1, 3, 5, 7, 8, 9, 10, 11, 12)
+SUBSTEPS = 6
+
+
+def stream_scratch(line, shards, half):
+    only, shared = reduce_split(TILE)
+    both = only + shared
+    low = jnp.bfloat16
+    copies = 3 * line + 4
+    return [
+        pltpu.VMEM((KEPT, shards, half, TILE), low),
+        pltpu.VMEM((GIVEN, shards, half, TILE), low),
+        pltpu.VMEM((GOT, shards, half, TILE), low),
+        pltpu.VMEM((OVER_X, shards, half, only), low),
+        pltpu.VMEM((OVER_Y, line, half, both), low),
+        pltpu.VMEM((OVER_Z, line + 1, half, both), low),
+        pltpu.VMEM((LATE, half, both), low),
+        pltpu.VMEM((ENDS, half, TILE), low),
+        pltpu.VMEM((ENDS, half, TILE), low),
+        pltpu.VMEM((WIDE, 2 * half, TILE), jnp.float32),
+        pltpu.SemaphoreType.DMA((KEPT, 4)),
+        pltpu.SemaphoreType.DMA((KEPT, copies)),
+        pltpu.SemaphoreType.DMA((KEPT, copies)),
+    ]
+
+
+class Stream:
+    def __init__(self, net, scratch, writes):
+        self.net, self.writes = net, writes
+        (
+            self.kept,
+            self.give,
+            self.got,
+            self.from_x,
+            self.from_y,
+            self.from_z,
+            self.late,
+            self.final,
+            self.swapped,
+            self.wide,
+            self.local_sem,
+            self.send_sem,
+            self.recv_sem,
+        ) = scratch
+        self.shards, self.half = self.kept.shape[1], self.kept.shape[2]
+        self.only, self.shared = reduce_split(TILE)
+        self.both = self.only + self.shared
+        self.carried = pl.ds(aligned(net.x * self.only, 128), self.both)
+        self.lone = pl.ds(aligned(net.x * self.both, 128), self.only)
+        self.their_lone = pl.ds(aligned((1 - net.x) * self.both, 128), self.only)
+
+    def remote(self, tile, origin, landing, index, target):
+        slot = tile % KEPT
+        return pltpu.make_async_remote_copy(
+            src_ref=origin,
+            dst_ref=landing,
+            send_sem=self.send_sem.at[slot, index],
+            recv_sem=self.recv_sem.at[slot, index],
+            device_id=target,
+            device_id_type=MESH,
+        )
+
+    def halves(self, tile):
+        line = self.net.line
+        return self.remote(tile, self.give.at[tile % GIVEN], self.got.at[tile % GOT], 2 * line, self.net.sibling)
+
+    def over_x(self, tile):
+        origin = self.kept.at[tile % KEPT, :, :, self.their_lone]
+        return self.remote(tile, origin, self.from_x.at[tile % OVER_X], 2 * self.net.line + 1, self.net.across_x)
+
+    def over_y(self, tile, z):
+        net = self.net
+        origin = self.kept.at[tile % KEPT, z * 2 + 1 - net.y, :, self.carried]
+        return self.remote(tile, origin, self.from_y.at[tile % OVER_Y, z], 2 * net.line + 4 + z, net.across_y)
+
+    def up(self, tile, z):
+        net = self.net
+        origin = self.kept.at[tile % KEPT, z * 2 + net.y, :, self.carried]
+        return self.remote(tile, origin, self.from_z.at[tile % OVER_Z, z + 1], z, net.above)
+
+    def down(self, tile, z):
+        net = self.net
+        origin = self.kept.at[tile % KEPT, z * 2 + net.y, :, self.carried]
+        return self.remote(tile, origin, self.from_z.at[tile % OVER_Z, z], net.line + z, net.below)
+
+    def end_x(self, tile):
+        net = self.net
+        origin = self.kept.at[tile % KEPT, net.own, :, self.carried]
+        return self.remote(tile, origin, self.late.at[tile % LATE], 2 * net.line + 2, net.across_x)
+
+    def to_core(self, tile):
+        slot = tile % ENDS
+        return self.remote(tile, self.final.at[slot], self.swapped.at[slot], 2 * self.net.line + 3, self.net.sibling)
+
+    def add(self, tile, shard, part):
+        slot = tile % KEPT
+        self.kept[slot, shard, :, self.carried] = self.kept[slot, shard, :, self.carried] + part
+
+    def born(self, tile):
+        self.halves(tile).start()
+
+    def meet_core(self, tile):
+        copy = self.halves(tile)
+        copy.wait_recv()
+        copy.wait_send()
+        slot, came = tile % KEPT, tile % GOT
+
+        @pl.loop(0, self.shards)
+        def _(shard):
+            self.kept[slot, shard] = self.kept[slot, shard] + self.got[came, shard]
+
+        self.over_x(tile).start()
+
+    def meet_x(self, tile):
+        self.over_x(tile).wait_recv()
+        slot, came = tile % KEPT, tile % OVER_X
+
+        @pl.loop(0, self.shards)
+        def _(shard):
+            self.kept[slot, shard, :, self.lone] = self.kept[slot, shard, :, self.lone] + self.from_x[came, shard]
+
+        for z in range(self.net.line):
+            self.over_y(tile, z).start()
+
+    def meet_y(self, tile):
+        for z in range(self.net.line):
+            self.over_y(tile, z).wait_recv()
+            self.add(tile, z * 2 + self.net.y, self.from_y[tile % OVER_Y, z])
+        self.hop(tile, 0)
+
+    def hop(self, tile, step):
+        net, came = self.net, tile % OVER_Z
+
+        @pl.when(net.z == step)
+        def _():
+            for z in range(net.line - 1, step, -1):
+                if step > 0:
+                    self.up(tile, z).wait_recv()
+                    self.add(tile, z * 2 + net.y, self.from_z[came, z + 1])
+                self.up(tile, z).start()
+
+        @pl.when(net.z == net.line - 1 - step)
+        def _():
+            for z in range(net.line - 1 - step):
+                if step > 0:
+                    self.down(tile, z).wait_recv()
+                    self.add(tile, z * 2 + net.y, self.from_z[came, z])
+                self.down(tile, z).start()
+
+    def land(self, tile):
+        net, came = self.net, tile % OVER_Z
+
+        @pl.when(net.has_below)
+        def _():
+            self.up(tile, net.z).wait_recv()
+            self.add(tile, net.own, self.from_z[came, net.z + 1])
+
+        @pl.when(net.has_above)
+        def _():
+            self.down(tile, net.z).wait_recv()
+            self.add(tile, net.own, self.from_z[came, net.z])
+
+        self.end_x(tile).start()
+
+    def meet(self, tile):
+        net, only, both, shared = self.net, self.only, self.both, self.shared
+        slot, came, end = tile % KEPT, tile % LATE, tile % ENDS
+        self.end_x(tile).wait_recv()
+        self.final[end, :, self.lone] = self.kept[slot, net.own, :, self.lone]
+        for x in range(2):
+
+            @pl.when(net.x == x)
+            def _():
+                theirs = 0 if x == 1 else shared
+                middle = only if x == 1 else 0
+                at = (1 - x) * both
+                self.final[end, :, at : at + only] = self.late[came, :, theirs : theirs + only]
+                self.final[end, :, only:both] = (
+                    self.kept[slot, net.own, :, only:both] + self.late[came, :, middle : middle + shared]
+                )
+
+        self.to_core(tile).start()
+        mine = pl.ds(aligned(net.core * self.half, self.half), self.half)
+        self.wide[tile % WIDE, mine, :] = self.final[end].astype(jnp.float32)
+
+    def swap(self, tile):
+        self.to_core(tile).wait_recv()
+        theirs = pl.ds(aligned((1 - self.net.core) * self.half, self.half), self.half)
+        self.wide[tile % WIDE, theirs, :] = self.swapped[tile % ENDS].astype(jnp.float32)
+        self.writes(tile, self.wide.at[tile % WIDE], self.local_sem.at[tile % KEPT], True)
+
+    def finish(self, tile):
+        net = self.net
+        self.writes(tile, self.wide.at[tile % WIDE], self.local_sem.at[tile % KEPT], False)
+        self.over_x(tile).wait_send()
+        for z in range(net.line):
+            self.over_y(tile, z).wait_send()
+            pl.when(net.z < z)(self.up(tile, z).wait_send)
+            pl.when(net.z > z)(self.down(tile, z).wait_send)
+        self.end_x(tile).wait_send()
+        self.to_core(tile).wait_send()
+
+    def stages(self):
+        return [
+            self.born,
+            self.meet_core,
+            self.meet_x,
+            self.meet_y,
+            lambda tile: self.hop(tile, 1),
+            lambda tile: self.hop(tile, 2),
+            self.land,
+            self.meet,
+            self.swap,
+            self.finish,
+        ]
+
+
+class Plan:
+    def __init__(self, blocks, heads):
+        self.blocks, self.heads = blocks, heads
+        self.ffn = blocks * SUBSTEPS
+        self.norm = self.ffn
+        self.branch = self.ffn + 1
+        self.attend = self.ffn + 2
+        self.groups = 4
+        self.per_group = heads // self.groups
+        self.out = self.ffn + SUBSTEPS
+        self.ready = [self.attend + self.per_group * (group + 1) for group in range(self.groups)]
+        self.births = list(range(SUBSTEPS, self.out + 2))
+        self.ffn_tiles = self.ffn
+        self.keys_tiles, self.value_tiles = [], []
+        for group in range(self.groups):
+            self.keys_tiles.append(len(self.births))
+            self.births.append(max(self.ready[group], self.births[-1] + 1))
+            if group % 2 == 1:
+                self.value_tiles.append(len(self.births))
+                self.births.append(self.births[-1] + 1)
+        self.last = self.births[-1]
+        self.grid = self.last + STAGES[-1] + 1
+
+    def tile_at(self, step):
+        regular = self.out + 2 - SUBSTEPS
+        tile = step - SUBSTEPS
+        known = (step >= SUBSTEPS) & (step < self.out + 2)
+        for index in range(regular, len(self.births)):
+            hit = step == self.births[index]
+            tile = jnp.where(hit, index, tile)
+            known = known | hit
+        return tile, known
+
+
+def back_kernel(plan, line, shards, *refs):
+    step = pl.program_id(0)
+    refs = list(refs)
+
+    def take(count):
+        out = refs[:count]
+        del refs[:count]
+        return out
+
+    normed_hbm, given_hbm, hidden_hbm = take(3)
+    early = take(4)
+    gather_from = take(4)
+    attended_hbm, out_hbm, normed_one_hbm, x_hbm, qkv_hbm = take(5)
+    gain_one_ref, gain_two_ref = take(2)
+    bias_ref, q_ref, k_ref, v_ref, wide_ref, lse_ref, var_ref, valid_ref, cos_ref, sin_ref = take(10)
+    result_hbm, tokens_hbm, sum_in, sum_down, sum_out, sum_qkv = take(6)
+    gather_to = take(4)
+    grad_gain_one_ref, grad_gain_two_ref, db_ref = take(3)
+    normed, turned, given, w_down, w_gate, w_up, act, act_t = take(8)
+    d_gate, d_up, acc, through = take(4)
+    query_ref, given_aug_ref, dk_acc, dv_acc = take(4)
+    load_sem, = take(1)
+    gather_local, gather_send, gather_recv = take(3)
+    net = Net(line)
+    half = BLOCK // shards // 2
+    heads_at = step - plan.attend
+
+    def writes(tile, wide, sems, begin):
+        rows = 2 * half
+
+        def move(index, origin, landing):
+            copy = pltpu.make_async_copy(origin, landing, sems.at[index])
+            copy.start() if begin else copy.wait()
+
+        block, kind = tile // SUBSTEPS, tile % SUBSTEPS
+        in_ffn = tile < plan.ffn_tiles
+
+        @pl.when(in_ffn & (kind < 2))
+        def _():
+            lines = pl.ds(aligned(block * rows, rows), rows)
+            move(0, wide, sum_down.at[lines, pl.ds(aligned(kind * TILE, TILE), TILE)])
+
+        @pl.when(in_ffn & (kind >= 2))
+        def _():
+            inner = plan.blocks * BLOCK
+            base = ((kind - 2) // 2) * inner
+            for piece in range(4):
+                shard = (kind % 2) * 4 + piece
+                start = base + shard * (inner // shards) + block * (BLOCK // shards)
+                columns = pl.ds(aligned(start, 128), 128)
+                move(piece, wide.at[:, piece * 128 : (piece + 1) * 128], sum_in.at[:, columns])
+
+        @pl.when((tile >= plan.ffn_tiles) & (tile < plan.ffn_tiles + 2))
+        def _():
+            start = aligned((tile - plan.ffn_tiles) * TILE, TILE)
+            move(0, wide, sum_out.at[:, pl.ds(start, TILE)])
+
+        width = plan.heads * q_ref.shape[0]
+        for group, number in enumerate(plan.keys_tiles):
+
+            @pl.when(tile == number)
+            def _():
+                for part in range(2):
+                    start = part * width + group * (TILE // 2)
+                    columns = slice(part * (TILE // 2), (part + 1) * (TILE // 2))
+                    move(part, wide.at[:, columns], sum_qkv.at[:, pl.ds(start, TILE // 2)])
+
+        for pair, number in enumerate(plan.value_tiles):
+
+            @pl.when(tile == number)
+            def _():
+                move(0, wide, sum_qkv.at[:, pl.ds(2 * width + pair * TILE, TILE)])
+
+    stream = Stream(net, refs, writes)
+    stages = stream.stages()
+
+    def load(index, origin, landing):
+        return pltpu.make_async_copy(origin, landing, load_sem.at[index])
+
+    def weight_loads(block):
+        if block < 2:
+            into, down = early[2 * block], early[2 * block + 1]
+        else:
+            into, down = gather_to[2 * (block - 2)], gather_to[2 * (block - 2) + 1]
+        return [
+            load(0, into.at[:, pl.ds(0, BLOCK)], w_gate),
+            load(1, into.at[:, pl.ds(BLOCK, BLOCK)], w_up),
+            load(2, down, w_down),
+        ]
+
+    first_loads = [load(3, normed_hbm, normed), load(4, given_hbm, given), load(5, hidden_hbm, acc)]
+    hidden_load = load(5, hidden_hbm, acc)
+    result_store = load(6, act, result_hbm)
+    attended_load = load(7, attended_hbm, w_down)
+    out_load = load(8, out_hbm, d_up.at[0])
+    normed_one_load = load(9, normed_one_hbm, turned)
+    x_load = load(10, x_hbm, normed)
+    tokens_store = load(11, acc, tokens_hbm)
+
+    def qkv_loads(group):
+        width = qkv_hbm.shape[1] // 3
+        part = width // plan.groups
+        page = act_t if group % 2 == 0 else d_up.at[0]
+        return [
+            load(
+                12 + index,
+                qkv_hbm.at[:, pl.ds(index * width + group * part, part)],
+                page.at[:, pl.ds(index * part, part)],
+            )
+            for index in range(3)
+        ]
+
+    def at(place):
+        return pl.when(step == place)
+
+    def start(copies):
+        for copy in copies:
+            copy.start()
+
+    def wait(copies):
+        for copy in copies:
+            copy.wait()
+
+    gathers = [
+        gather_steps(
+            net, gather_from[i], gather_to[i], gather_local.at[i], gather_send.at[i], gather_recv.at[i]
+        )
+        for i in range(4)
+    ]
+    gather_places = ((0, 1, 3, 5, 6, 7, 9), (6, 8, 9, 11, 12, 14, 15))
+
+    @at(0)
+    def _():
+        net.greet()
+        start(weight_loads(0) + first_loads)
+
+    for pair, places in enumerate(gather_places):
+        for index, place in enumerate(places):
+
+            @at(place)
+            def _():
+                gathers[2 * pair][index]()
+                gathers[2 * pair + 1][index]()
+
+    for stage in range(len(STAGES) - 1, 0, -1):
+        tile, known = plan.tile_at(step - STAGES[stage])
+        pl.when(known)(functools.partial(stages[stage], tile))
+
+    @at(0)
+    def _():
+        wait(first_loads)
+        turned[...] = normed[...].T
+
+    for block in range(plan.blocks):
+
+        @at(block * SUBSTEPS)
+        def _():
+            wait(weight_loads(block))
+
+        if block + 1 < plan.blocks:
+
+            @at(block * SUBSTEPS + SUBSTEPS - 1)
+            def _():
+                start(weight_loads(block + 1))
+
+    block, sub = step // SUBSTEPS, step % SUBSTEPS
+    slot = block % 2
+    in_ffn = step < plan.ffn
+
+    @pl.when(in_ffn & (sub < 2))
+    def _():
+        columns = pl.ds(aligned(sub * TILE, TILE), TILE)
+        d_act = product(given[...], w_down[columns, :], COLUMNS_BY_COLUMNS)
+        gate = product(normed[...], w_gate[:, columns])
+        up = product(normed[...], w_up[:, columns])
+        sigmoid = jax.nn.sigmoid(gate)
+        swish = gate * sigmoid
+        act[:, columns] = (swish * up).astype(jnp.bfloat16)
+        d_gate[slot, :, columns] = (d_act * up * sigmoid * (1.0 + gate * (1.0 - sigmoid))).astype(jnp.bfloat16)
+        d_up[slot, :, columns] = (d_act * swish).astype(jnp.bfloat16)
+
+    @pl.when(in_ffn & (sub == 2))
+    def _():
+        acc[...] += product(act[...], w_down[...])
+        act_t[...] = act[...].T
+
+    @pl.when(in_ffn & (sub == 3))
+    def _():
+        part = product(d_gate[slot], w_gate[...], COLUMNS_BY_COLUMNS)
+
+        @pl.when(block == 0)
+        def _():
+            through[...] = part
+
+        @pl.when(block > 0)
+        def _():
+            through[...] += part
+
+    @pl.when(in_ffn & (sub == 4))
+    def _():
+        through[...] += product(d_up[slot], w_up[...], COLUMNS_BY_COLUMNS)
+
+    last_sum = plan.ffn - SUBSTEPS + 2
+
+    @at(last_sum)
+    def _():
+        act[...] = acc[...].astype(jnp.bfloat16)
+        result_store.start()
+
+    @at(last_sum + 1)
+    def _():
+        start([hidden_load, attended_load])
+
+    @at(last_sum + 3)
+    def _():
+        result_store.wait()
+
+    row_block = 128
+
+    @at(plan.norm)
+    def _():
+        out_load.start()
+        hidden_load.wait()
+        grad_gain_two_ref[...] = jnp.zeros_like(grad_gain_two_ref)
+
+        @pl.loop(0, acc.shape[0] // row_block)
+        def _(index):
+            lines = pl.ds(aligned(index * row_block, row_block), row_block)
+            back, grad_gain = norm_back(through[lines, :], acc[lines, :], gain_two_ref[...])
+            d_hidden = given[lines, :].astype(jnp.float32) + back
+            acc[lines, :] = d_hidden
+            d_gate[0, lines, :] = d_hidden.astype(jnp.bfloat16)
+            grad_gain_two_ref[...] += grad_gain
+
+    @at(plan.branch)
+    def _():
+        out_load.wait()
+        act[...] = product(d_up[0], d_gate[0], COLUMNS_BY_COLUMNS).astype(jnp.bfloat16)
+
+    for group in range(plan.groups):
+        ready = plan.ready[group]
+
+        if group == 0:
+
+            @at(plan.attend)
+            def _():
+                start(qkv_loads(0))
+
+        @at(ready)
+        def _():
+            wait(qkv_loads(group))
+            if group + 1 < plan.groups:
+                start(qkv_loads(group + 1))
+            page = act_t if group % 2 == 0 else d_up.at[0]
+            quarter = TILE // 2
+            base = (group % 2) * TILE
+            part = product(page[:, :TILE], w_gate[base : base + TILE, :])
+            values = (group // 2) * TILE + (group % 2) * quarter
+            part = part + product(page[:, TILE : TILE + quarter], w_up[values : values + quarter, :])
+            if group == 0:
+                through[...] = part
+            else:
+                through[...] += part
+
+    @at(plan.out)
+    def _():
+        attended_load.wait()
+        start([normed_one_load, x_load])
+
+    @at(plan.births[plan.keys_tiles[0]])
+    def _():
+        normed_one_load.wait()
+
+    @pl.when((heads_at >= 0) & (heads_at < plan.heads))
+    def _():
+        depth = q_ref.shape[0]
+        head = heads_at
+        group = head // plan.per_group
+        q_at = (group % 2) * TILE + (head % plan.per_group) * depth
+        k_at = q_at + TILE // 2
+        v_at = (group // 2) * TILE + (head % (2 * plan.per_group)) * depth
+
+        def rows(start):
+            return pl.ds(aligned(start, depth), depth)
+
+        attend_back_head(
+            2,
+            head,
+            bias_ref,
+            q_ref,
+            k_ref,
+            v_ref,
+            act.at[rows(head * depth)],
+            wide_ref,
+            lse_ref,
+            var_ref,
+            valid_ref,
+            cos_ref,
+            sin_ref,
+            w_gate.at[rows(q_at)],
+            w_gate.at[rows(k_at)],
+            w_up.at[rows(v_at)],
+            db_ref,
+            query_ref,
+            given_aug_ref,
+            dk_acc,
+            dv_acc,
+        )
+
+    tile, known = plan.tile_at(step)
+
+    def birth(left, right, dims=(((1,), (0,)), ((), ()))):
+        for which, target in ((net.core, stream.kept.at[tile % KEPT]), (1 - net.core, stream.give.at[tile % GIVEN])):
+            lines = [
+                left[pl.ds(aligned(shard * 2 * half + which * half, half), half), :] for shard in range(shards)
+            ]
+            out = product(jnp.concatenate(lines, axis=0), right, dims).astype(jnp.bfloat16)
+            for shard in range(shards):
+                target[shard] = out[shard * half : (shard + 1) * half]
+
+    kind, source = tile % SUBSTEPS, (tile // SUBSTEPS) % 2
+    in_tiles = known & (tile < plan.ffn_tiles)
+    columns = pl.ds(aligned((kind % 2) * TILE, TILE), TILE)
+    pl.when(in_tiles & (kind < 2))(lambda: birth(act_t, given[:, columns]))
+    pl.when(in_tiles & (kind >= 2) & (kind < 4))(lambda: birth(turned, d_gate[source, :, columns]))
+    pl.when(in_tiles & (kind >= 4))(lambda: birth(turned, d_up[source, :, columns]))
+    for number in range(2):
+        at(plan.out + number)(
+            lambda: birth(w_down, d_gate[0, :, number * TILE : (number + 1) * TILE])
+        )
+    for group, number in enumerate(plan.keys_tiles):
+        base = (group % 2) * TILE
+        at(plan.births[number])(lambda: birth(turned, w_gate[base : base + TILE, :], COLUMNS_BY_COLUMNS))
+    for pair, number in enumerate(plan.value_tiles):
+        base = pair * TILE
+        at(plan.births[number])(lambda: birth(turned, w_up[base : base + TILE, :], COLUMNS_BY_COLUMNS))
+    pl.when(known)(lambda: stream.born(tile))
+
+    @at(plan.last)
+    def _():
+        x_load.wait()
+        grad_gain_one_ref[...] = jnp.zeros_like(grad_gain_one_ref)
+
+        @pl.loop(0, acc.shape[0] // row_block)
+        def _(index):
+            lines = pl.ds(aligned(index * row_block, row_block), row_block)
+            values = normed[lines, :].astype(jnp.float32)
+            back, grad_gain = norm_back(through[:, lines].T, values, gain_one_ref[...])
+            acc[lines, :] = acc[lines, :] + back
+            grad_gain_one_ref[...] += grad_gain
+
+        tokens_store.start()
+
+    @at(plan.grid - 1)
+    def _():
+        tokens_store.wait()
+
+
+def back(line, early, sources, normed_two, given, hidden, attended_t, out_weight, normed_t, x, qkv_weight,
+         gain_one, gain_two, bias, qkv_t, wide_t, log_sums, variates, valid, cos_t, sin_t):
+    shards = lax.axis_size("shard")
+    rows, width = x.shape
+    heads = log_sums.shape[0]
+    depth = width // heads
+    blocks = 4
+    plan = Plan(blocks, heads)
+    low = jnp.bfloat16
+    owned = width // shards
+    inner = blocks * BLOCK
+
+    def head_at(step):
+        return jnp.clip(step - plan.attend, 0, heads - 1)
+
+    def part(which):
+        return pl.BlockSpec((depth, rows), lambda step: (which * heads + head_at(step), 0))
+
+    page = pltpu.VMEM((BLOCK, BLOCK), low)
+    copies = gather_count(line)
+    row = pl.BlockSpec((1, width), lambda step: (0, 0))
+    return pl.pallas_call(
+        functools.partial(back_kernel, plan, line, shards),
+        grid=(plan.grid,),
+        out_shape=[
+            like((rows, width), low),
+            like((rows, width), jnp.float32),
+            like((owned, 2 * inner), jnp.float32),
+            like((inner // shards, width), jnp.float32),
+            like((owned, width), jnp.float32),
+            like((owned, 3 * width), jnp.float32),
+        ]
+        + [like((shards * source.shape[0], source.shape[1]), low) for source in sources]
+        + [
+            like((1, width), jnp.float32),
+            like((1, width), jnp.float32),
+            like((heads, 2, rows // 2), jnp.float32),
+        ],
+        in_specs=[ANY] * 16
+        + [whole(1, width), whole(1, width)]
+        + [
+            pl.BlockSpec(memory_space=pltpu.SMEM),
+            part(0),
+            part(1),
+            part(2),
+            pl.BlockSpec((depth, rows), lambda step: (head_at(step), 0)),
+            pl.BlockSpec((1, 1, rows), lambda step: (head_at(step), 0, 0)),
+            whole(1, rows),
+            whole(1, rows),
+            whole(*cos_t.shape),
+            whole(*sin_t.shape),
+        ],
+        out_specs=[ANY] * 10
+        + [row, row, pl.BlockSpec((1, 2, rows // 2), lambda step: (head_at(step), 0, 0))],
+        scratch_shapes=[page] * 8
+        + [
+            pltpu.VMEM((2, BLOCK, BLOCK), low),
+            pltpu.VMEM((2, BLOCK, BLOCK), low),
+            pltpu.VMEM((rows, width), jnp.float32),
+            pltpu.VMEM((rows, width), jnp.float32),
+            pltpu.VMEM((2 * depth + FEATURES, rows), low),
+            pltpu.VMEM((depth + FEATURES, rows), low),
+            pltpu.VMEM((rows, depth), jnp.float32),
+            pltpu.VMEM((rows, depth), jnp.float32),
+            pltpu.SemaphoreType.DMA((15,)),
+            pltpu.SemaphoreType.DMA((4,)),
+            pltpu.SemaphoreType.DMA((4, copies)),
+            pltpu.SemaphoreType.DMA((4, copies)),
+        ]
+        + stream_scratch(line, shards, owned // 2),
+        compiler_params=pltpu.CompilerParams(
+            collective_id=9, has_side_effects=True, vmem_limit_bytes=64 << 20
+        ),
+        name="back",
+    )(
+        normed_two, given, hidden, *early, *sources, attended_t, out_weight, normed_t, x, qkv_weight,
+        gain_one, gain_two, bias, qkv_t, qkv_t, qkv_t, wide_t, log_sums, variates, valid, cos_t, sin_t,
+    )
+
+
 def rope_tables(time_ids):
     half = HEAD_DIM // 2
     exponent = jnp.arange(half).astype(jnp.float32) * (2.0 / HEAD_DIM)
@@ -1197,12 +1897,6 @@
     given = jnp.where(key_valid.reshape(length, 1), cotangent, jnp.zeros_like(cotangent))
     cos_t, sin_t = rope_tables(time_ids)
 
-    def joined(part):
-        return part.reshape(-1, part.shape[2])
-
-    def cut(grad):
-        return grad.reshape(parts, -1, grad.shape[1])
-
     def gathering(number, *weights):
         return Carried(line, number, gathers=weights) if line else None
 
@@ -1211,7 +1905,8 @@
 
     if line:
         small, full_qkv = carry_alone(gathering(1, pack_small(attn_gain, ffn_gain, attn_bias), w_qkv), "gather_qkv")
-        qkv_weight = joined(full_qkv)
+        qkv_weight = full_qkv
+        small = small.reshape(parts, -1, small.shape[1])
         gain_one, gain_two = small[:, 0].reshape(1, -1), small[:, 1].reshape(1, -1)
         bias = jnp.swapaxes(small[:, 2:4, :heads], 0, 1).reshape(2, -1)
     else:
@@ -1224,21 +1919,51 @@
         gain_two = gain_two.astype(jnp.float32).reshape(1, -1)
 
     (qkv_t, normed_t), came = project(tokens, gain_one, qkv_weight, cos_t, sin_t, gathering(2, w_out))
-    out_weight = joined(came[0]) if line else out_weight
+    out_weight = came[0] if line else out_weight
+    if line:
+        owned = w_in.shape[1] // (2 * parts)
+        into = [
+            jnp.concatenate(
+                [w_in[:, piece * owned + block * 128 :][:, :128] for piece in range(2 * parts)], axis=1
+            )
+            for block in range(4)
+        ]
+        down = [w_down[block * 128 : (block + 1) * 128] for block in range(4)]
+        pairs = [part for pair in zip(into, down) for part in pair]
+        (attended_t, wide_t, log_sums), early = attend_forward(
+            qkv_t, variate_ids, valid, bias, HEADS, gathering(3, *pairs[:4])
+        )
+        (hidden, normed_two), _ = branch(attended_t, out_weight, tokens, gain_two, None)
+        result, grad_tokens, sum_in, sum_down, sum_out, sum_qkv, *rest = back(
+            line, early, pairs[4:], normed_two, given, hidden, attended_t, out_weight, normed_t, tokens, qkv_weight,
+            gain_one, gain_two, bias, qkv_t, wide_t, log_sums, variate_ids, valid, cos_t, sin_t,
+        )
+        grad_gain_one, grad_gain_two, bias_parts = rest[4:]
+        packed = pack_grads(parts, grad_gain_one, grad_gain_two, jnp.sum(bias_parts, axis=2).T)
+        (small,) = carry_alone(reducing(8, [packed]), "reduce_small")
+        return (
+            result,
+            grad_tokens,
+            small[0],
+            sum_qkv,
+            small[2:4, :heads],
+            sum_out,
+            small[1],
+            sum_in,
+            sum_down,
+        )
     (attended_t, wide_t, log_sums), came = attend_forward(
-        qkv_t, variate_ids, valid, bias, HEADS, gathering(3, w_in)
+        qkv_t, variate_ids, valid, bias, HEADS, None
     )
-    in_weight = joined(came[0]) if line else in_weight
     (hidden, normed_two), _ = branch(attended_t, out_weight, tokens, gain_two, None)
-    (act, to_gate, to_up), came = widen(normed_two, in_weight, gathering(4, w_down))
-    down_weight = joined(came[0]) if line else down_weight
+    (act, to_gate, to_up), _ = widen(normed_two, in_weight, None)
     (result, grad_down, d_gate, d_up), _ = narrow(act, to_gate, to_up, down_weight, given, hidden, None)
     (grad_gate, grad_up), _ = grad_into(normed_two, d_gate, d_up, None)
-    (d_hidden, d_branch, grad_gain_two), came_down = ffn_back(
-        d_gate, d_up, in_weight, hidden, gain_two, given, reducing(5, [cut(grad_down)])
+    (d_hidden, d_branch, grad_gain_two), _ = ffn_back(
+        d_gate, d_up, in_weight, hidden, gain_two, given, None
     )
     (grad_out, given_t), _ = branch_back(attended_t, out_weight, d_branch, None)
-    (dq, dk, dv, bias_parts), came_in = attend_backward(
+    (dq, dk, dv, bias_parts), _ = attend_backward(
         qkv_t,
         given_t,
         wide_t,
@@ -1249,26 +1974,12 @@
         cos_t,
         sin_t,
         HEADS,
-        reducing(6, [cut(grad_gate), cut(grad_up)]),
+        None,
     )
-    (grad_qkv, grad_tokens, grad_gain_one), came_out = project_back(
-        normed_t, dq, dk, dv, qkv_weight, tokens, gain_one, d_hidden, reducing(7, [cut(grad_out)])
+    (grad_qkv, grad_tokens, grad_gain_one), _ = project_back(
+        normed_t, dq, dk, dv, qkv_weight, tokens, gain_one, d_hidden, None
     )
     grad_bias = jnp.sum(bias_parts, axis=2).T
-    if line:
-        packed = pack_grads(parts, grad_gain_one, grad_gain_two, grad_bias)
-        sum_qkv, small = carry_alone(reducing(8, [cut(grad_qkv)], [packed]), "reduce_qkv")
-        return (
-            result,
-            grad_tokens,
-            small[0],
-            sum_qkv,
-            small[2:4, :heads],
-            came_out[0],
-            small[1],
-            came_in[0],
-            came_down[0],
-        )
     grads = (
         (grad_gain_one.reshape(-1), 0),
         (grad_qkv, 0),

time: 660 us -> 552 us (0.84)
  Pallas kernels: 623 us -> 486 us
  local copies, waits for them, and re-layouts: 19.3 us -> 47.8 us
    pallas_call x8 -> x4, Pallas kernels: 544 us -> 151 us  [carry(): pl.pallas_call(kernel, grid=(grid,), out_shape=list(out_shape) + carried....]
    pallas_call x0 -> x1, Pallas kernels: none -> 328 us  [back(): pl.pallas_call(functools.partial(back_kernel, plan, line, shards), grid=(...]
    pallas_call x4 -> x1, Pallas kernels: 79.1 us -> 7.33 us  [carry(): pl.pallas_call(body, grid=(grid,), out_shape=out_shape, in_specs=in_specs...]
    unnamed x21 -> x42, local copies, waits for them, and re-layouts: 12.2 us -> 36.4 us
where the time goes in v3:
time: 552 us; the launch traced here: 543 us
  Pallas kernels  486 us (88%)
  local copies, waits for them, and re-layouts  47.8 us (9%)
  other arithmetic  7 us (1%)
    pallas_call x1, Pallas kernels, back(): pl.pallas_call(functools.partial(back_kernel, plan, line, shards), grid=(...  328 us
    pallas_call x4, Pallas kernels, carry(): pl.pallas_call(kernel, grid=(grid,), out_shape=list(out_shape) + carried....  151 us
    unnamed x42, local copies, waits for them, and re-layouts  36.4 us

profile of v3, /device:TPU:1, one launch (start us, length us, event | category | flops | bytes accessed | tf_op | source)
XLA Modules:
  0.0 542.8 jit_solution(9800208088866094839)
XLA Ops:
  6.4 2.2 fusion
  8.5 1.5 broadcast_select_fusion.refs_1_
  10.1 1.4 constant_dynamic-update-slice_fusion.63
  11.5 1.4 constant_dynamic-update-slice_fusion.62
  13.0 1.4 constant_dynamic-update-slice_fusion.61
  14.4 1.4 constant_dynamic-update-slice_fusion.60
  15.9 1.4 constant_dynamic-update-slice_fusion.59
  17.3 1.5 constant_dynamic-update-slice_fusion.58
  18.8 1.4 constant_dynamic-update-slice_fusion.57
  20.2 1.4 constant_dynamic-update-slice_fusion.56
  21.7 1.4 constant_dynamic-update-slice_fusion.55
  23.1 1.4 constant_dynamic-update-slice_fusion.54
  24.5 1.4 constant_dynamic-update-slice_fusion.53
  26.0 1.4 constant_dynamic-update-slice_fusion.52
  27.4 1.4 constant_dynamic-update-slice_fusion.51
  34.0 44.5 %gather_qkv.1 = (f32[128,128]{1,0:T(8,128)}, bf16[1024,3072]{1,0:T(8,128)(2,1)}) custom-call(f32[16,128]{1,0:T(8,128)} %copy-done.9, bf16[128,3072]{1,0:T(8,128)(2,1)} %refs_1_.1), custom_call_target="tpu_custom_call" | custom-call | tf_op jit(solution)/shard_map/gather_qkv/pallas_call | solution.py:551
  81.4 26.8 %project.1 = (bf16[3072,1024]{1,0:T(8,128)(2,1)}, bf16[1024,1024]{1,0:T(8,128)(2,1)}, bf16[1024,1024]{1,0:T(8,128)(2,1)}) custom-call(bf16[1024,1024]{1,0:T(8,128)(2,1)} %refs_14_.1, f32[1,1024]{1,0:T(1,128)} %get-tuple-element.196.refs_1_.refs_16_, bf16[1024,3072]{1,0:T(8,128)(2,1)} %get-tuple-element.105.refs_2_.refs_15_, ...), custom_call_target="tpu_custom_call" | custom-call | tf_op jit(solution)/shard_map/project/pallas_call | solution.py:551
  108.2 62.8 %attend_forward.1 = (bf16[1024,1024]{1,0:T(8,128)(2,1)}, f32[1024,1024]{1,0:T(8,128)}, f32[16,1,1024]{2,1,0:T(1,128)}, bf16[1024,2048]{1,0:T(8,128)(2,1)}, bf16[...) custom-call(f32[2,16]{1,0:T(2,128)} %reshape.237.refs_0_.refs_18_, ...), custom_call_target="tpu_custom_call" | custom-call | tf_op jit(solution)/shard_map/attend_forward/pallas_call | solution.py:551
  171.0 7.3 %branch.1 = (f32[1024,1024]{1,0:T(8,128)}, bf16[1024,1024]{1,0:T(8,128)(2,1)}) custom-call(bf16[1024,1024]{1,0:T(8,128)(2,1)} %get-tuple-element.107.att_ref.refs_11_, bf16[1024,1024]{1,0:T(8,128)(2,1)} %get-tuple-element.108.w_ref.refs_12_, bf16[1024,1024]{1,0:T(8,128)(2,1)} %refs_14_.1, f32[1,1024]{1,0:T(1,128)} %get-tuple-element.195.gain_ref.refs_17_), custom_call_target="tpu_custom_call" | custom-call | tf_op jit(solution)/shard_map/branch/pallas_call | solution.py:510
  178.3 327.7 %back.1 = (bf16[1024,1024]{1,0:T(8,128)(2,1)}, f32[1024,1024]{1,0:T(8,128)}, f32[128,8192]{1,0:T(8,128)}, f32[512,1024]{1,0:T(8,128)}, f32[128,1024]{1,0:T(8,128...) custom-call(bf16[1024,1024]{1,0:T(8,128)(2,1)} %get-tuple-element.10, ...), custom_call_target="tpu_custom_call" | custom-call | tf_op jit(solution)/shard_map/back/pallas_call | solution.py:1795
  509.7 16.9 %reduce_small.1 = f32[16,128]{1,0:T(8,128)} custom-call(f32[8,16,128]{2,1,0:T(8,128)} %copy-done.8), custom_call_target="tpu_custom_call" | custom-call | tf_op jit(solution)/shard_map/reduce_small/pallas_call | solution.py:551
  529.1 3.2 copy.112
  532.4 2.1 copy.113
  538.0 2.1 copy.116
  (47 shorter events, 24.8 us)
Async XLA Ops:
  0.6 7.9 %copy-start.2 = (bf16[1024,1024]{1,0:T(8,128)(2,1)S(1)}, bf16[1024,1024]{1,0:T(8,128)(2,1)}, u32[]{:S(2)}) copy-start(bf16[1024,1024]{1,0:T(8,128)(2,1)} %param.35) | copy-start | bytes 6291460
  5.1 5.0 copy-start.9
  33.2 0.8 copy-start.6
  34.0 74.2 %copy-start.5 = (bf16[128,2048]{1,0:T(8,128)(2,1)}, bf16[128,2048]{1,0:T(8,128)(2,1)S(1)}, u32[]{:S(2)}) copy-start(bf16[128,2048]{1,0:T(8,128)(2,1)S(1)} %get-tuple-element.129.refs_8_) | copy-start | bytes 1572868
  509.0 0.6 copy-start.8
  529.1 3.2 copy-start.1
  532.4 2.5 copy-start.4
  532.4 5.6 %copy-start = (f32[128,8192]{1,0:T(8,128)S(1)}, f32[128,8192]{1,0:T(8,128)}, u32[]{:S(2)}) copy-start(f32[128,8192]{1,0:T(8,128)} %get-tuple-element.217) | copy-start | bytes 12582916
  534.9 2.3 copy-start.7
  538.0 3.1 copy-start.3

commit v4 on v3

--- a/solution.py
+++ b/solution.py
@@ -203,15 +203,6 @@
             to_core(z, 1 - net.y).wait()
 
     return [start] + [step(hops) for hops in range(1, line + 1)] + [last, finish]
-
-
-def gather_scratch(line, tensors):
-    copies = gather_count(line)
-    return [
-        pltpu.SemaphoreType.DMA((tensors,)),
-        pltpu.SemaphoreType.DMA((tensors, copies)),
-        pltpu.SemaphoreType.DMA((tensors, copies)),
-    ]
 
 
 REDUCE_BUFFERS = 9
@@ -399,27 +390,6 @@
     return [first, second, third, fourth_and_hop] + hops[1:] + [land, meet, swap, finish]
 
 
-def staggered(step_lists, gap=1):
-    ticks = (len(step_lists) - 1) * gap + max(len(steps) for steps in step_lists)
-    out = []
-    for tick in range(ticks):
-        row = []
-        for index, steps in enumerate(step_lists):
-            at = tick - index * gap
-            if 0 <= at < len(steps):
-                row.append(steps[at])
-        out.append(row)
-    return out
-
-
-def reduce_chunks(shape):
-    shards, rows, columns = shape
-    width = columns
-    while width % 1024 == 0 and shards * (rows // 2) * width > (1 << 19):
-        width //= 2
-    return width, columns // width
-
-
 ROWS_BY_ROWS = (((0,), (0,)), ((), ()))
 COLUMNS_BY_COLUMNS = (((1,), (1,)), ((), ()))
 
@@ -432,149 +402,17 @@
     return lax.rsqrt(jnp.mean(values * values, axis=1, keepdims=True) + norm_eps)
 
 
-class Carried:
-    def __init__(self, line, collective, gathers=(), reduces=()):
-        self.line, self.collective = line, collective
-        self.gathers, self.reduces = list(gathers), list(reduces)
-        self.operands = list(self.gathers)
-        self.results = []
-        shards = lax.axis_size("shard")
-        for part in self.gathers:
-            self.results.append(jax.ShapeDtypeStruct((shards * part.shape[0], part.shape[1]), part.dtype))
-        self.scratch = gather_scratch(line, len(self.gathers)) if self.gathers else []
-        self.plans = []
-        chunks = 0
-        for grads in self.reduces:
-            plan = [reduce_chunks(grad.shape) for grad in grads]
-            self.plans.append(plan)
-            chunks += sum(count for _, count in plan)
-            self.operands += grads
-            columns = sum(grad.shape[2] for grad in grads)
-            self.results.append(jax.ShapeDtypeStruct((grads[0].shape[1], columns), jnp.float32))
-        if chunks:
-            copies = reduce_count(line)
-            self.scratch += [
-                pltpu.SemaphoreType.DMA((chunks, 2)),
-                pltpu.SemaphoreType.DMA((chunks, copies)),
-                pltpu.SemaphoreType.DMA((chunks, copies)),
-            ]
-        for grads, plan in zip(self.reduces, self.plans):
-            for grad, (width, count) in zip(grads, plan):
-                for _ in range(count):
-                    self.scratch += reduce_scratch(line, grad.shape[0], grad.shape[1] // 2, width, grad.dtype)
-
-    def rows(self, net, operands, results, scratch):
-        lists = []
-        if self.gathers:
-            local, send, recv = scratch[:3]
-            scratch = scratch[3:]
-            for index in range(len(self.gathers)):
-                lists.append(
-                    gather_steps(
-                        net, operands[index], results[index], local.at[index], send.at[index], recv.at[index]
-                    )
-                )
-        operands, results = operands[len(self.gathers) :], results[len(self.gathers) :]
-        if self.reduces:
-            local, send, recv = scratch[:3]
-            scratch = scratch[3:]
-        number = 0
-        for target, (grads, plan) in enumerate(zip(self.reduces, self.plans)):
-            start = 0
-            for grad, (width, count) in zip(grads, plan):
-                source = operands[0]
-                operands = operands[1:]
-                for chunk in range(count):
-                    lists.append(
-                        reduce_steps(
-                            net,
-                            source,
-                            results[target],
-                            chunk * width,
-                            start + chunk * width,
-                            scratch[:REDUCE_BUFFERS],
-                            local.at[number],
-                            send.at[number],
-                            recv.at[number],
-                        )
-                    )
-                    scratch = scratch[REDUCE_BUFFERS:]
-                    number += 1
-                start += grad.shape[2]
-        return staggered(lists)
-
-
-def carry(body, carried, *, grid, out_shape, in_specs, out_specs, scratch_shapes, name, operands, head=0):
-    if carried is None:
-        return list(
-            pl.pallas_call(
-                body,
-                grid=(grid,),
-                out_shape=out_shape,
-                in_specs=in_specs,
-                out_specs=out_specs,
-                scratch_shapes=scratch_shapes,
-                compiler_params=pltpu.CompilerParams(vmem_limit_bytes=60 << 20),
-                name=name,
-            )(*operands)
-        ), []
-    counts = [len(in_specs), len(carried.operands), len(out_specs), len(carried.results), len(scratch_shapes)]
-    ends = [sum(counts[: i + 1]) for i in range(len(counts))]
-
-    def kernel(*refs):
-        own_in, more_in = refs[: ends[0]], refs[ends[0] : ends[1]]
-        own_out, more_out = refs[ends[1] : ends[2]], refs[ends[2] : ends[3]]
-        own_scratch, more_scratch = refs[ends[3] : ends[4]], refs[ends[4] :]
-        step = pl.program_id(0)
-        net = Net(carried.line)
-        rows = carried.rows(net, more_in, more_out, more_scratch)
-        pl.when(step == 0)(net.greet)
-        middle = rows[:-1]
-        at = [head + (index * (grid - head)) // len(middle) for index in range(len(middle))]
-        at[0] = 0
-        for place in sorted(set(at)):
-
-            @pl.when(step == place)
-            def _():
-                for index, row in enumerate(middle):
-                    if at[index] == place:
-                        for action in row:
-                            action()
-
-        body(*own_in, *own_out, *own_scratch)
-
-        @pl.when(step == grid - 1)
-        def _():
-            for action in rows[-1]:
-                action()
-
-    results = pl.pallas_call(
-        kernel,
+def run(body, *, grid, out_shape, in_specs, out_specs, scratch_shapes, name, operands):
+    return pl.pallas_call(
+        body,
         grid=(grid,),
-        out_shape=list(out_shape) + carried.results,
-        in_specs=list(in_specs) + [ANY] * len(carried.operands),
-        out_specs=list(out_specs) + [ANY] * len(carried.results),
-        scratch_shapes=list(scratch_shapes) + carried.scratch,
-        compiler_params=pltpu.CompilerParams(
-            collective_id=carried.collective, has_side_effects=True, vmem_limit_bytes=63 << 20
-        ),
+        out_shape=out_shape,
+        in_specs=in_specs,
+        out_specs=out_specs,
+        scratch_shapes=scratch_shapes,
+        compiler_params=pltpu.CompilerParams(vmem_limit_bytes=60 << 20),
         name=name,
-    )(*operands, *carried.operands)
-    return list(results[: len(out_shape)]), list(results[len(out_shape) :])
-
-
-def carry_alone(carried, name):
-    return carry(
-        lambda: None,
-        carried,
-        grid=1,
-        out_shape=[],
-        in_specs=[],
-        out_specs=[],
-        scratch_shapes=[],
-        name=name,
-        operands=[],
-    )[1]
+    )(*operands)
 
 
 def whole(*shape):
@@ -610,13 +448,12 @@
         out_ref[...] = out.astype(jnp.bfloat16)
 
 
-def project(x, gain, weight, cos_t, sin_t, carried):
+def project(x, gain, weight, cos_t, sin_t):
     rows, width = x.shape
     columns = weight.shape[1]
     block = 512
-    return carry(
+    return run(
         functools.partial(project_kernel, 2 * width // block),
-        carried,
         grid=columns // block,
         out_shape=[like((columns, rows), jnp.bfloat16), like((width, rows), jnp.bfloat16)],
         in_specs=[
@@ -642,13 +479,12 @@
     normed_ref[...] = (hidden * inverse_rms(hidden) * gain_ref[...]).astype(jnp.bfloat16)
 
 
-def branch(attended_t, weight, x, gain, carried):
+def branch(attended_t, weight, x, gain):
     rows, width = x.shape
     block = 256
     row = pl.BlockSpec((block, width), lambda step: (step, 0))
-    return carry(
+    return run(
         branch_kernel,
-        carried,
         grid=rows // block,
         out_shape=[like((rows, width), jnp.float32), like((rows, width), jnp.bfloat16)],
         in_specs=[
@@ -675,15 +511,14 @@
     to_up_ref[...] = swish.astype(jnp.bfloat16)
 
 
-def widen(normed, weight, carried):
+def widen(normed, weight):
     rows, width = normed.shape
     inner = weight.shape[1] // 2
     block = 512
     steps = inner // block
     part = pl.BlockSpec((rows, block), lambda step: (0, step))
-    return carry(
+    return run(
         widen_kernel,
-        carried,
         grid=steps,
         out_shape=[like((rows, inner), jnp.bfloat16)] * 3,
         in_specs=[
@@ -723,16 +558,15 @@
     d_up_ref[...] = (d_act * to_up_ref[...].astype(jnp.float32)).astype(jnp.bfloat16)
 
 
-def narrow(act, to_gate, to_up, weight, given, hidden, carried):
+def narrow(act, to_gate, to_up, weight, given, hidden):
     rows, inner = act.shape
     width = weight.shape[1]
     block = 512
     steps = inner // block
     part = pl.BlockSpec((rows, block), lambda step: (0, step))
     down = pl.BlockSpec((block, width), lambda step: (step, 0))
-    return carry(
+    return run(
         functools.partial(narrow_kernel, steps),
-        carried,
         grid=steps,
         out_shape=[
             like((rows, width), jnp.bfloat16),
@@ -757,15 +591,14 @@
     to_up_ref[...] = product(turned_ref[...], d_up_ref[...]).astype(jnp.bfloat16)
 
 
-def grad_into(normed, d_gate, d_up, carried):
+def grad_into(normed, d_gate, d_up):
     rows, width = normed.shape
     inner = d_gate.shape[1]
     block = 512
     part = pl.BlockSpec((rows, block), lambda step: (0, step))
     out = pl.BlockSpec((width, block), lambda step: (0, step))
-    return carry(
+    return run(
         grad_in_kernel,
-        carried,
         grid=inner // block,
         out_shape=[like((width, inner), jnp.bfloat16)] * 2,
         in_specs=[whole(rows, width), part, part],
@@ -808,16 +641,15 @@
         grad_gain_ref[...] = grad_gain
 
 
-def ffn_back(d_gate, d_up, weight, hidden, gain, given, carried):
+def ffn_back(d_gate, d_up, weight, hidden, gain, given):
     rows, width = hidden.shape
     inner = d_gate.shape[1]
     block = 512
     steps = inner // block
     part = pl.BlockSpec((rows, block), lambda step: (0, step))
     full = pl.BlockSpec((rows, width), lambda step: (0, 0))
-    return carry(
+    return run(
         functools.partial(ffn_back_kernel, steps),
-        carried,
         grid=steps,
         out_shape=[
             like((rows, width), jnp.float32),
@@ -846,14 +678,13 @@
     given_ref[...] = product(w_ref[...], d_branch, COLUMNS_BY_COLUMNS).astype(jnp.bfloat16)
 
 
-def branch_back(attended_t, weight, d_branch, carried):
+def branch_back(attended_t, weight, d_branch):
     rows, width = d_branch.shape
     block = 256
     out = pl.BlockSpec((block, width), lambda step: (step, 0))
     turned = pl.BlockSpec((block, rows), lambda step: (step, 0))
-    return carry(
+    return run(
         branch_back_kernel,
-        carried,
         grid=attended_t.shape[0] // block,
         out_shape=[like(weight.shape, jnp.bfloat16), like(attended_t.shape, jnp.bfloat16)],
         in_specs=[turned, out, whole(rows, width)],
@@ -894,7 +725,7 @@
         grad_gain_ref[...] = grad_gain
 
 
-def project_back(normed_t, dq, dk, dv, weight, x, gain, d_hidden, carried):
+def project_back(normed_t, dq, dk, dv, weight, x, gain, d_hidden):
     rows, width = x.shape
     columns = weight.shape[1]
     block = 512
@@ -907,9 +738,8 @@
             (block, rows), lambda step: (jnp.clip(step - which * third, 0, third - 1), 0)
         )
 
-    return carry(
+    return run(
         functools.partial(project_back_kernel, steps),
-        carried,
         grid=steps,
         out_shape=[
             like((width, columns), jnp.bfloat16),
@@ -989,11 +819,14 @@
     return two_parts(query_t.astype(jnp.float32) * (score_scale * LOG2E))
 
 
-def attend_kernel(blocks, bias_ref, q_ref, k_ref, v_ref, var_ref, valid_ref, o_ref, wide_ref, lse_ref, query_ref):
+def attend_kernel(blocks, bias_ref, *refs):
     head = pl.program_id(0)
+    attend_head(blocks, bias_ref[0, head], bias_ref[1, head], *refs)
+
+
+def attend_head(blocks, same, other, q_ref, k_ref, v_ref, var_ref, valid_ref, o_ref, wide_ref, lse_ref, query_ref):
     depth, length = q_ref.shape
     width = length // blocks
-    same, other = bias_ref[0, head], bias_ref[1, head]
     variates = var_ref[...]
     high, low = scaled_query(q_ref[...], depth ** (-0.5))
     query_ref[...] = jnp.concatenate([high, low, query_features(variates, same, other, None)], axis=0)
@@ -1016,7 +849,7 @@
         lse_ref[0, :, at] = peak + jnp.log2(total)
 
 
-def attend_forward(qkv_t, variates, valid, bias, heads, carried):
+def attend_forward(qkv_t, variates, valid, bias, heads):
     rows, length = qkv_t.shape
     depth = rows // (3 * heads)
 
@@ -1024,9 +857,8 @@
         return pl.BlockSpec((depth, length), lambda head: (which * heads + head, 0))
 
     row = pl.BlockSpec((1, length), lambda head: (0, 0))
-    return carry(
+    return run(
         functools.partial(attend_kernel, 1),
-        carried,
         grid=heads,
         out_shape=[
             jax.ShapeDtypeStruct((heads * depth, length), jnp.bfloat16),
@@ -1061,13 +893,12 @@
 
 
 def attend_back_head(
-    blocks, head, bias_ref, q_ref, k_ref, v_ref, go_ref, wide_ref, lse_ref, var_ref, valid_ref, cos_ref, sin_ref,
-    dq_ref, dk_ref, dv_ref, db_ref, query_ref, given_ref, dk_acc, dv_acc,
+    blocks, same, other, q_ref, k_ref, v_ref, go_ref, wide_ref, lse_ref, var_ref, valid_ref, cos_ref, sin_ref,
+    dq_ref, dk_ref, dv_ref, query_ref, given_ref, dk_acc, dv_acc,
 ):
     depth, length = q_ref.shape
     width = length // blocks
     scale = depth ** (-0.5)
-    same, other = bias_ref[0, head], bias_ref[1, head]
     variates = var_ref[...]
     features = key_features(variates, valid_ref[...])
     high, low = scaled_query(q_ref[...], scale)
@@ -1111,15 +942,20 @@
             dv_acc[...] += dv
     dk_ref[...] = turn_back((dk_acc[...] * scale).T, cos_ref[...], sin_ref[...]).astype(jnp.bfloat16)
     dv_ref[...] = dv_acc[...].T.astype(jnp.bfloat16)
+    return in_same, in_other
+
+
+def attend_back_kernel(blocks, bias_ref, *refs):
+    head = pl.program_id(0)
+    *refs, db_ref, query_ref, given_ref, dk_acc, dv_acc = refs
+    in_same, in_other = attend_back_head(
+        blocks, bias_ref[0, head], bias_ref[1, head], *refs, query_ref, given_ref, dk_acc, dv_acc
+    )
     db_ref[0, 0:1, :] = in_same
     db_ref[0, 1:2, :] = in_other
 
 
-def attend_back_kernel(blocks, *refs):
-    attend_back_head(blocks, pl.program_id(0), *refs)
-
-
-def attend_backward(qkv_t, given_t, wide_t, log_sums, variates, valid, bias, cos_t, sin_t, heads, carried):
+def attend_backward(qkv_t, given_t, wide_t, log_sums, variates, valid, bias, cos_t, sin_t, heads):
     rows, length = qkv_t.shape
     depth = rows // (3 * heads)
     blocks = 1
@@ -1129,9 +965,8 @@
 
     one = pl.BlockSpec((depth, length), lambda head: (head, 0))
     grad = jax.ShapeDtypeStruct((heads * depth, length), jnp.bfloat16)
-    return carry(
+    return run(
         functools.partial(attend_back_kernel, blocks),
-        carried,
         grid=heads,
         out_shape=[grad, grad, grad, jax.ShapeDtypeStruct((heads, 2, length // blocks), jnp.float32)],
         in_specs=[
@@ -1159,6 +994,289 @@
     )
 
 
+PRELUDE = 7
+FRONT_PLACES = (
+    (0, 1, 2, 3, 4, 5, 6),
+    (1, 3, 4, 5, 7, 8, 9),
+    (3, 6, 8, 10, 13, 16, 18),
+    (8, 12, 15, 18, 21, 24, 28),
+)
+
+
+def bias_of(small_ref, head, per_shard):
+    row = 16 * (head // per_shard) + 2
+    return small_ref[row, head % per_shard], small_ref[row + 1, head % per_shard]
+
+
+def gain_of(small_ref, shards, which):
+    rows = [small_ref[16 * shard + which : 16 * shard + which + 1, :] for shard in range(shards)]
+    return jnp.concatenate(rows, axis=1)
+
+
+def front_kernel(line, shards, heads, *refs):
+    step = pl.program_id(0)
+    refs = list(refs)
+
+    def take(count):
+        out = refs[:count]
+        del refs[:count]
+        return out
+
+    small, w_qkv, w_out, w_in, w_down, x_hbm = take(6)
+    var_ref, valid_ref, cos_ref, sin_ref = take(4)
+    small_all, qkv_all, out_all, into_0, down_0, into_1, down_1 = take(7)
+    intos = take(4)
+    qkv_hbm, normed_hbm, attended_hbm, hidden_hbm, normed_two_hbm = take(5)
+    wide_ref, lse_ref = take(2)
+    x, weight, normed_t, qkv, attended, hidden, normed_two, small_ref, query_ref, bias_ref, wide_rows, cut_rows = take(12)
+    load_sem, cut_sem, local_sem, send_sem, recv_sem = refs
+    net = Net(line)
+    rows, width = x.shape
+    block = 512
+    projected = 3 * width // block
+    attend = PRELUDE + projected
+    last = attend + heads
+    depth = width // heads
+
+    def load(index, origin, landing):
+        return pltpu.make_async_copy(origin, landing, load_sem.at[index])
+
+    def at(place):
+        return pl.when(step == place)
+
+    inner = w_in.shape[1] // 2
+    owned = inner // shards
+    piece_width = BLOCK // shards
+
+    w_in_load = pltpu.make_async_copy(w_in, wide_rows, cut_sem.at[4])
+
+    def cut_store(number):
+        return pltpu.make_async_copy(cut_rows.at[number], intos[number], cut_sem.at[number])
+
+    def down_part(number):
+        return w_down.at[pl.ds(number * piece_width, piece_width)]
+
+    tensors = (
+        ((small, small_all), (w_qkv, qkv_all)),
+        ((w_out, out_all),),
+        ((intos[0], into_0), (down_part(0), down_0)),
+        ((intos[1], into_1), (down_part(1), down_1)),
+    )
+    number = 0
+    groups = []
+    for group in tensors:
+        lists = []
+        for source, full in group:
+            lists.append(
+                gather_steps(
+                    net, source, full, local_sem.at[number], send_sem.at[number], recv_sem.at[number]
+                )
+            )
+            number += 1
+        groups.append(lists)
+
+    x_load = load(0, x_hbm, x)
+    small_load = load(1, small_all, small_ref)
+    weight_load = load(2, qkv_all, weight)
+    bias_load = load(9, small_all, bias_ref)
+    normed_store = load(3, normed_t, normed_hbm)
+    qkv_store = load(4, qkv, qkv_hbm)
+    attended_store = load(5, attended, attended_hbm)
+    out_load = load(6, out_all, weight.at[:, pl.ds(0, width)])
+    hidden_store = load(7, hidden, hidden_hbm)
+    normed_two_store = load(8, normed_two, normed_two_hbm)
+
+    @at(0)
+    def _():
+        net.greet()
+        x_load.start()
+        w_in_load.start()
+
+    for lists, places in zip(groups, FRONT_PLACES):
+        for index, place in enumerate(places):
+
+            @at(place)
+            def _():
+                if place == FRONT_PLACES[2][0] and lists is groups[2]:
+                    cut_store(0).wait()
+                if place == FRONT_PLACES[3][0] and lists is groups[3]:
+                    cut_store(1).wait()
+                for steps in lists:
+                    steps[index]()
+
+    @at(0)
+    def _():
+        w_in_load.wait()
+        for index in range(4):
+            for piece in range(2 * shards):
+                start = piece * owned + index * piece_width
+                cut_rows[index, :, piece * piece_width : (piece + 1) * piece_width] = wide_rows[
+                    :, start : start + piece_width
+                ]
+            cut_store(index).start()
+
+    @at(PRELUDE - 1)
+    def _():
+        cut_store(2).wait()
+        cut_store(3).wait()
+        weight_load.start()
+        small_load.start()
+        bias_load.start()
+        x_load.wait()
+        small_load.wait()
+        bias_load.wait()
+        gain = gain_of(small_ref, shards, 0)
+        values = x[...].astype(jnp.float32)
+        normed = values * inverse_rms(values) * gain
+        normed_t[...] = normed.T.astype(jnp.bfloat16)
+        normed_store.start()
+        weight_load.wait()
+
+    @pl.when((step >= PRELUDE) & (step < attend))
+    def _():
+        index = step - PRELUDE
+        columns = pl.ds(aligned(index * block, block), block)
+        out = product(weight[:, columns], normed_t[...], ROWS_BY_ROWS)
+        lines = qkv.at[columns]
+
+        @pl.when(index < 2 * width // block)
+        def _():
+            cos, sin = cos_ref[...], sin_ref[...]
+            half = depth // 2
+            for start in range(0, block, depth):
+                first, second = out[start : start + half], out[start + half : start + depth]
+                lines[start : start + half, :] = (first * cos - second * sin).astype(jnp.bfloat16)
+                lines[start + half : start + depth, :] = (second * cos + first * sin).astype(jnp.bfloat16)
+
+        @pl.when(index >= 2 * width // block)
+        def _():
+            lines[...] = out.astype(jnp.bfloat16)
+
+    @at(attend)
+    def _():
+        qkv_store.start()
+
+    @pl.when((step >= attend) & (step < last))
+    def _():
+        head = step - attend
+
+        def part(which):
+            return qkv.at[pl.ds(aligned(which * width + head * depth, depth), depth)]
+
+        same, other = bias_of(bias_ref, head, heads // shards)
+        attend_head(
+            1,
+            same,
+            other,
+            part(0),
+            part(1),
+            part(2),
+            var_ref,
+            valid_ref,
+            attended.at[pl.ds(aligned(head * depth, depth), depth)],
+            wide_ref,
+            lse_ref,
+            query_ref,
+        )
+
+    @at(last - 1)
+    def _():
+        out_load.start()
+        attended_store.start()
+
+    @at(last)
+    def _():
+        out_load.wait()
+        gain = gain_of(small_ref, shards, 1)
+        part = 256
+        for index in range(rows // part):
+            lines = slice(index * part, (index + 1) * part)
+            sums = product(attended[:, lines], weight[:, :width], ROWS_BY_ROWS)
+            values = x[lines, :].astype(jnp.float32) + sums
+            hidden[lines, :] = values
+            normed_two[lines, :] = (values * inverse_rms(values) * gain).astype(jnp.bfloat16)
+        hidden_store.start()
+        normed_two_store.start()
+        for store in (normed_store, qkv_store, attended_store, hidden_store, normed_two_store):
+            store.wait()
+
+
+def front(line, small, w_qkv, w_out, w_in, w_down, x, variates, valid, cos_t, sin_t, heads):
+    shards = lax.axis_size("shard")
+    rows, width = x.shape
+    depth = width // heads
+    low = jnp.bfloat16
+    piece = BLOCK // shards
+    grid = PRELUDE + 3 * width // 512 + heads + 1
+    copies = gather_count(line)
+
+    def head_at(step):
+        return jnp.clip(step - (PRELUDE + 3 * width // 512), 0, heads - 1)
+
+    def gathered(rows, columns, dtype=low):
+        return like((shards * rows, columns), dtype)
+
+    owned = w_qkv.shape[0]
+    return pl.pallas_call(
+        functools.partial(front_kernel, line, shards, heads),
+        grid=(grid,),
+        out_shape=[
+            gathered(16, 128, jnp.float32),
+            gathered(*w_qkv.shape),
+            gathered(*w_out.shape),
+            gathered(owned, 2 * BLOCK),
+            gathered(piece, width),
+            gathered(owned, 2 * BLOCK),
+            gathered(piece, width),
+        ]
+        + [like((owned, 2 * BLOCK), low)] * 4
+        + [
+            like((3 * width, rows), low),
+            like((width, rows), low),
+            like((width, rows), low),
+            like((rows, width), jnp.float32),
+            like((rows, width), low),
+            like((width, rows), jnp.float32),
+            like((heads, 1, rows), jnp.float32),
+        ],
+        in_specs=[ANY] * 6
+        + [
+            whole(1, rows),
+            whole(1, rows),
+            whole(*cos_t.shape),
+            whole(*sin_t.shape),
+        ],
+        out_specs=[ANY] * 16
+        + [
+            pl.BlockSpec((depth, rows), lambda step: (head_at(step), 0)),
+            pl.BlockSpec((1, 1, rows), lambda step: (head_at(step), 0, 0)),
+        ],
+        scratch_shapes=[
+            pltpu.VMEM((rows, width), low),
+            pltpu.VMEM((width, 3 * width), low),
+            pltpu.VMEM((width, rows), low),
+            pltpu.VMEM((3 * width, rows), low),
+            pltpu.VMEM((width, rows), low),
+            pltpu.VMEM((rows, width), jnp.float32),
+            pltpu.VMEM((rows, width), low),
+            pltpu.VMEM((16 * shards, 128), jnp.float32),
+            pltpu.VMEM((2 * depth + FEATURES, rows), low),
+            pltpu.SMEM((16 * shards, 128), jnp.float32),
+            pltpu.VMEM(w_in.shape, low),
+            pltpu.VMEM((4, owned, 2 * BLOCK), low),
+            pltpu.SemaphoreType.DMA((10,)),
+            pltpu.SemaphoreType.DMA((5,)),
+            pltpu.SemaphoreType.DMA((7,)),
+            pltpu.SemaphoreType.DMA((7, copies)),
+            pltpu.SemaphoreType.DMA((7, copies)),
+        ],
+        compiler_params=pltpu.CompilerParams(
+            collective_id=1, has_side_effects=True, vmem_limit_bytes=62 << 20
+        ),
+        name="front",
+    )(small, w_qkv, w_out, w_in, w_down, x, variates, valid, cos_t, sin_t)
+
+
 TILE = 512
 BLOCK = 1024
 KEPT, GIVEN, GOT, OVER_X, OVER_Y, OVER_Z, LATE, ENDS, WIDE = 13, 3, 4, 5, 5, 6, 4, 4, 3
@@ -1424,19 +1542,28 @@
 
     normed_hbm, given_hbm, hidden_hbm = take(3)
     early = take(4)
-    gather_from = take(4)
+    into_2, into_3, down_hbm = take(3)
     attended_hbm, out_hbm, normed_one_hbm, x_hbm, qkv_hbm = take(5)
-    gain_one_ref, gain_two_ref = take(2)
-    bias_ref, q_ref, k_ref, v_ref, wide_ref, lse_ref, var_ref, valid_ref, cos_ref, sin_ref = take(10)
-    result_hbm, tokens_hbm, sum_in, sum_down, sum_out, sum_qkv = take(6)
+    small_hbm, = take(1)
+    q_ref, k_ref, v_ref, wide_ref, lse_ref, var_ref, valid_ref, cos_ref, sin_ref = take(9)
+    result_hbm, tokens_hbm, sum_in, sum_down, sum_out, sum_qkv, sum_small = take(7)
     gather_to = take(4)
-    grad_gain_one_ref, grad_gain_two_ref, db_ref = take(3)
     normed, turned, given, w_down, w_gate, w_up, act, act_t = take(8)
     d_gate, d_up, acc, through = take(4)
     query_ref, given_aug_ref, dk_acc, dv_acc = take(4)
     load_sem, = take(1)
     gather_local, gather_send, gather_recv = take(3)
+    small_ref, bias_ref, grad_gain_one_ref, grad_gain_two_ref, grad_small = take(5)
+    small_buffers = take(REDUCE_BUFFERS)
+    small_local, small_send, small_recv = take(3)
     net = Net(line)
+    piece = BLOCK // shards
+    gather_from = [
+        into_2,
+        down_hbm.at[pl.ds(2 * piece, piece)],
+        into_3,
+        down_hbm.at[pl.ds(3 * piece, piece)],
+    ]
     half = BLOCK // shards // 2
     heads_at = step - plan.attend
 
@@ -1503,7 +1630,13 @@
             load(2, down, w_down),
         ]
 
-    first_loads = [load(3, normed_hbm, normed), load(4, given_hbm, given), load(5, hidden_hbm, acc)]
+    first_loads = [
+        load(3, normed_hbm, normed),
+        load(4, given_hbm, given),
+        load(5, hidden_hbm, acc),
+        load(15, small_hbm, small_ref),
+        load(16, small_hbm, bias_ref),
+    ]
     hidden_load = load(5, hidden_hbm, acc)
     result_store = load(6, act, result_hbm)
     attended_load = load(7, attended_hbm, w_down)
@@ -1564,6 +1697,7 @@
     @at(0)
     def _():
         wait(first_loads)
+        grad_small[...] = jnp.zeros_like(grad_small)
         turned[...] = normed[...].T
 
     for block in range(plan.blocks):
@@ -1637,11 +1771,12 @@
         out_load.start()
         hidden_load.wait()
         grad_gain_two_ref[...] = jnp.zeros_like(grad_gain_two_ref)
+        gain_two = gain_of(small_ref, shards, 1)
 
         @pl.loop(0, acc.shape[0] // row_block)
         def _(index):
             lines = pl.ds(aligned(index * row_block, row_block), row_block)
-            back, grad_gain = norm_back(through[lines, :], acc[lines, :], gain_two_ref[...])
+            back, grad_gain = norm_back(through[lines, :], acc[lines, :], gain_two)
             d_hidden = given[lines, :].astype(jnp.float32) + back
             acc[lines, :] = d_hidden
             d_gate[0, lines, :] = d_hidden.astype(jnp.bfloat16)
@@ -1698,10 +1833,12 @@
         def rows(start):
             return pl.ds(aligned(start, depth), depth)
 
-        attend_back_head(
+        per_shard = plan.heads // shards
+        same, other = bias_of(bias_ref, head, per_shard)
+        sums = attend_back_head(
             2,
-            head,
-            bias_ref,
+            same,
+            other,
             q_ref,
             k_ref,
             v_ref,
@@ -1715,12 +1852,14 @@
             w_gate.at[rows(q_at)],
             w_gate.at[rows(k_at)],
             w_up.at[rows(v_at)],
-            db_ref,
             query_ref,
             given_aug_ref,
             dk_acc,
             dv_acc,
         )
+        for which, lanes in enumerate(sums):
+            folded = sum(lanes[:, start : start + 128] for start in range(0, lanes.shape[1], 128))
+            grad_small[head // per_shard, pl.ds(2 + 2 * (head % per_shard) + which, 1), :] = folded
 
     tile, known = plan.tile_at(step)
 
@@ -1755,24 +1894,35 @@
     def _():
         x_load.wait()
         grad_gain_one_ref[...] = jnp.zeros_like(grad_gain_one_ref)
+        gain_one = gain_of(small_ref, shards, 0)
 
         @pl.loop(0, acc.shape[0] // row_block)
         def _(index):
             lines = pl.ds(aligned(index * row_block, row_block), row_block)
             values = normed[lines, :].astype(jnp.float32)
-            back, grad_gain = norm_back(through[:, lines].T, values, gain_one_ref[...])
+            back, grad_gain = norm_back(through[:, lines].T, values, gain_one)
             acc[lines, :] = acc[lines, :] + back
             grad_gain_one_ref[...] += grad_gain
 
         tokens_store.start()
+        for shard in range(shards):
+            columns = slice(shard * 128, (shard + 1) * 128)
+            grad_small[shard, 0:1, :] = grad_gain_one_ref[:, columns]
+            grad_small[shard, 1:2, :] = grad_gain_two_ref[:, columns]
+
+    small_steps = reduce_steps(
+        net, grad_small, sum_small, 0, 0, small_buffers, small_local, small_send, small_recv
+    )
+    for index, action in enumerate(small_steps):
+        at(plan.last + 1 + index)(action)
 
     @at(plan.grid - 1)
     def _():
         tokens_store.wait()
 
 
-def back(line, early, sources, normed_two, given, hidden, attended_t, out_weight, normed_t, x, qkv_weight,
-         gain_one, gain_two, bias, qkv_t, wide_t, log_sums, variates, valid, cos_t, sin_t):
+def back(line, early, sources, own_down, normed_two, given, hidden, attended_t, out_weight, normed_t, x, qkv_weight,
+         small, qkv_t, wide_t, log_sums, variates, valid, cos_t, sin_t):
     shards = lax.axis_size("shard")
     rows, width = x.shape
     heads = log_sums.shape[0]
@@ -1791,7 +1941,6 @@
 
     page = pltpu.VMEM((BLOCK, BLOCK), low)
     copies = gather_count(line)
-    row = pl.BlockSpec((1, width), lambda step: (0, 0))
     return pl.pallas_call(
         functools.partial(back_kernel, plan, line, shards),
         grid=(plan.grid,),
@@ -1802,17 +1951,12 @@
             like((inner // shards, width), jnp.float32),
             like((owned, width), jnp.float32),
             like((owned, 3 * width), jnp.float32),
+            like((16, 128), jnp.float32),
         ]
-        + [like((shards * source.shape[0], source.shape[1]), low) for source in sources]
+        + [like((width, 2 * BLOCK), low), like((BLOCK, width), low)] * 2
+,
+        in_specs=[ANY] * 16
         + [
-            like((1, width), jnp.float32),
-            like((1, width), jnp.float32),
-            like((heads, 2, rows // 2), jnp.float32),
-        ],
-        in_specs=[ANY] * 16
-        + [whole(1, width), whole(1, width)]
-        + [
-            pl.BlockSpec(memory_space=pltpu.SMEM),
             part(0),
             part(1),
             part(2),
@@ -1823,8 +1967,7 @@
             whole(*cos_t.shape),
             whole(*sin_t.shape),
         ],
-        out_specs=[ANY] * 10
-        + [row, row, pl.BlockSpec((1, 2, rows // 2), lambda step: (head_at(step), 0, 0))],
+        out_specs=[ANY] * 11,
         scratch_shapes=[page] * 8
         + [
             pltpu.VMEM((2, BLOCK, BLOCK), low),
@@ -1835,10 +1978,21 @@
             pltpu.VMEM((depth + FEATURES, rows), low),
             pltpu.VMEM((rows, depth), jnp.float32),
             pltpu.VMEM((rows, depth), jnp.float32),
-            pltpu.SemaphoreType.DMA((15,)),
+            pltpu.SemaphoreType.DMA((17,)),
             pltpu.SemaphoreType.DMA((4,)),
             pltpu.SemaphoreType.DMA((4, copies)),
             pltpu.SemaphoreType.DMA((4, copies)),
+            pltpu.VMEM((16 * shards, 128), jnp.float32),
+            pltpu.SMEM((16 * shards, 128), jnp.float32),
+            pltpu.VMEM((1, width), jnp.float32),
+            pltpu.VMEM((1, width), jnp.float32),
+            pltpu.VMEM((shards, 16, 128), jnp.float32),
+        ]
+        + reduce_scratch(line, shards, 8, 128, jnp.float32)
+        + [
+            pltpu.SemaphoreType.DMA((2,)),
+            pltpu.SemaphoreType.DMA((reduce_count(line),)),
+            pltpu.SemaphoreType.DMA((reduce_count(line),)),
         ]
         + stream_scratch(line, shards, owned // 2),
         compiler_params=pltpu.CompilerParams(
@@ -1846,8 +2000,8 @@
         ),
         name="back",
     )(
-        normed_two, given, hidden, *early, *sources, attended_t, out_weight, normed_t, x, qkv_weight,
-        gain_one, gain_two, bias, qkv_t, qkv_t, qkv_t, wide_t, log_sums, variates, valid, cos_t, sin_t,
+        normed_two, given, hidden, *early, *sources, own_down, attended_t, out_weight, normed_t, x, qkv_weight,
+        small, qkv_t, qkv_t, qkv_t, wide_t, log_sums, variates, valid, cos_t, sin_t,
     )
 
 
@@ -1864,13 +2018,6 @@
     small = jnp.zeros((16, 128), jnp.float32)
     small = small.at[0].set(attn_gain.astype(jnp.float32)).at[1].set(ffn_gain.astype(jnp.float32))
     return small.at[2:4, :heads].set(attn_bias.astype(jnp.float32))
-
-
-def pack_grads(shards, gain_one, gain_two, bias):
-    heads = bias.shape[1] // shards
-    small = jnp.zeros((shards, 16, 128), jnp.float32)
-    small = small.at[:, 0].set(gain_one.reshape(shards, -1)).at[:, 1].set(gain_two.reshape(shards, -1))
-    return small.at[:, 2:4, :heads].set(jnp.swapaxes(bias.reshape(2, shards, heads), 0, 1))
 
 
 def shards(
@@ -1888,102 +2035,86 @@
     w_down,
     cotangent,
 ):
-    parts = lax.axis_size("shard")
     length = variate_ids.shape[1]
     heads = attn_bias.shape[1]
-    positions = jnp.arange(length)[None, :]
-    key_valid = positions < lengths[:, None]
+    key_valid = jnp.arange(length)[None, :] < lengths[:, None]
     valid = key_valid.astype(jnp.float32)
     given = jnp.where(key_valid.reshape(length, 1), cotangent, jnp.zeros_like(cotangent))
     cos_t, sin_t = rope_tables(time_ids)
-
-    def gathering(number, *weights):
-        return Carried(line, number, gathers=weights) if line else None
-
-    def reducing(number, *grads):
-        return Carried(line, number, reduces=grads) if line else None
-
     if line:
-        small, full_qkv = carry_alone(gathering(1, pack_small(attn_gain, ffn_gain, attn_bias), w_qkv), "gather_qkv")
-        qkv_weight = full_qkv
-        small = small.reshape(parts, -1, small.shape[1])
-        gain_one, gain_two = small[:, 0].reshape(1, -1), small[:, 1].reshape(1, -1)
-        bias = jnp.swapaxes(small[:, 2:4, :heads], 0, 1).reshape(2, -1)
-    else:
-        gain_one, gain_two, qkv_weight, out_weight, in_weight, down_weight = (
-            lax.all_gather(part, "shard", axis=0, tiled=True)
-            for part in (attn_gain, ffn_gain, w_qkv, w_out, w_in, w_down)
+        small, qkv_weight, out_weight, into_0, down_0, into_1, down_1, *rest = front(
+            line,
+            pack_small(attn_gain, ffn_gain, attn_bias),
+            w_qkv,
+            w_out,
+            w_in,
+            w_down,
+            tokens,
+            variate_ids,
+            valid,
+            cos_t,
+            sin_t,
+            HEADS,
         )
-        bias = lax.all_gather(attn_bias, "shard", axis=1, tiled=True).astype(jnp.float32)
-        gain_one = gain_one.astype(jnp.float32).reshape(1, -1)
-        gain_two = gain_two.astype(jnp.float32).reshape(1, -1)
-
-    (qkv_t, normed_t), came = project(tokens, gain_one, qkv_weight, cos_t, sin_t, gathering(2, w_out))
-    out_weight = came[0] if line else out_weight
-    if line:
-        owned = w_in.shape[1] // (2 * parts)
-        into = [
-            jnp.concatenate(
-                [w_in[:, piece * owned + block * 128 :][:, :128] for piece in range(2 * parts)], axis=1
-            )
-            for block in range(4)
-        ]
-        down = [w_down[block * 128 : (block + 1) * 128] for block in range(4)]
-        pairs = [part for pair in zip(into, down) for part in pair]
-        (attended_t, wide_t, log_sums), early = attend_forward(
-            qkv_t, variate_ids, valid, bias, HEADS, gathering(3, *pairs[:4])
-        )
-        (hidden, normed_two), _ = branch(attended_t, out_weight, tokens, gain_two, None)
-        result, grad_tokens, sum_in, sum_down, sum_out, sum_qkv, *rest = back(
-            line, early, pairs[4:], normed_two, given, hidden, attended_t, out_weight, normed_t, tokens, qkv_weight,
-            gain_one, gain_two, bias, qkv_t, wide_t, log_sums, variate_ids, valid, cos_t, sin_t,
-        )
-        grad_gain_one, grad_gain_two, bias_parts = rest[4:]
-        packed = pack_grads(parts, grad_gain_one, grad_gain_two, jnp.sum(bias_parts, axis=2).T)
-        (small,) = carry_alone(reducing(8, [packed]), "reduce_small")
+        intos, (qkv_t, normed_t, attended_t, hidden, normed_two, wide_t, log_sums) = rest[:4], rest[4:]
+        result, grad_tokens, sum_in, sum_down, sum_out, sum_qkv, small = back(
+            line,
+            [into_0, down_0, into_1, down_1],
+            [intos[2], intos[3]],
+            w_down,
+            normed_two,
+            given,
+            hidden,
+            attended_t,
+            out_weight,
+            normed_t,
+            tokens,
+            qkv_weight,
+            small,
+            qkv_t,
+            wide_t,
+            log_sums,
+            variate_ids,
+            valid,
+            cos_t,
+            sin_t,
+        )[:7]
         return (
             result,
             grad_tokens,
             small[0],
             sum_qkv,
-            small[2:4, :heads],
+            jnp.sum(small[2 : 2 + 2 * heads], axis=1).reshape(heads, 2).T,
             sum_out,
             small[1],
             sum_in,
             sum_down,
         )
-    (attended_t, wide_t, log_sums), came = attend_forward(
-        qkv_t, variate_ids, valid, bias, HEADS, None
+    gain_one, gain_two, qkv_weight, out_weight, in_weight, down_weight = (
+        lax.all_gather(part, "shard", axis=0, tiled=True)
+        for part in (attn_gain, ffn_gain, w_qkv, w_out, w_in, w_down)
     )
-    (hidden, normed_two), _ = branch(attended_t, out_weight, tokens, gain_two, None)
-    (act, to_gate, to_up), _ = widen(normed_two, in_weight, None)
-    (result, grad_down, d_gate, d_up), _ = narrow(act, to_gate, to_up, down_weight, given, hidden, None)
-    (grad_gate, grad_up), _ = grad_into(normed_two, d_gate, d_up, None)
-    (d_hidden, d_branch, grad_gain_two), _ = ffn_back(
-        d_gate, d_up, in_weight, hidden, gain_two, given, None
+    bias = lax.all_gather(attn_bias, "shard", axis=1, tiled=True).astype(jnp.float32)
+    gain_one = gain_one.astype(jnp.float32).reshape(1, -1)
+    gain_two = gain_two.astype(jnp.float32).reshape(1, -1)
+    qkv_t, normed_t = project(tokens, gain_one, qkv_weight, cos_t, sin_t)
+    attended_t, wide_t, log_sums = attend_forward(qkv_t, variate_ids, valid, bias, HEADS)
+    hidden, normed_two = branch(attended_t, out_weight, tokens, gain_two)
+    act, to_gate, to_up = widen(normed_two, in_weight)
+    result, grad_down, d_gate, d_up = narrow(act, to_gate, to_up, down_weight, given, hidden)
+    grad_gate, grad_up = grad_into(normed_two, d_gate, d_up)
+    d_hidden, d_branch, grad_gain_two = ffn_back(d_gate, d_up, in_weight, hidden, gain_two, given)
+    grad_out, given_t = branch_back(attended_t, out_weight, d_branch)
+    dq, dk, dv, bias_parts = attend_backward(
+        qkv_t, given_t, wide_t, log_sums, variate_ids, valid, bias, cos_t, sin_t, HEADS
     )
-    (grad_out, given_t), _ = branch_back(attended_t, out_weight, d_branch, None)
-    (dq, dk, dv, bias_parts), _ = attend_backward(
-        qkv_t,
-        given_t,
-        wide_t,
-        log_sums,
-        variate_ids,
-        valid,
-        bias,
-        cos_t,
-        sin_t,
-        HEADS,
-        None,
+    grad_qkv, grad_tokens, grad_gain_one = project_back(
+        normed_t, dq, dk, dv, qkv_weight, tokens, gain_one, d_hidden
     )
-    (grad_qkv, grad_tokens, grad_gain_one), _ = project_back(
-        normed_t, dq, dk, dv, qkv_weight, tokens, gain_one, d_hidden, None
-    )
-    grad_bias = jnp.sum(bias_parts, axis=2).T
     grads = (
         (grad_gain_one.reshape(-1), 0),
         (grad_qkv, 0),
-        (grad_bias, 1),
+        (jnp.sum(bias_parts, axis=2).T, 1),
         (grad_out, 0),
         (grad_gain_two.reshape(-1), 0),
         (jnp.concatenate([grad_gate, grad_up], axis=1), 0),

time: 552 us -> 483 us (0.88)
  Pallas kernels: 486 us -> 448 us
  local copies, waits for them, and re-layouts: 47.8 us -> 15.7 us
    pallas_call x5 -> x1, Pallas kernels: 158 us -> 118 us  [front(): pl.pallas_call(functools.partial(front_kernel, line, shards, heads), grid...]
    unnamed x42 -> x19, local copies, waits for them, and re-layouts: 36.4 us -> 13.9 us
where the time goes in v4:
time: 483 us; the launch traced here: 474 us
  Pallas kernels  448 us (93%)
  local copies, waits for them, and re-layouts  15.7 us (3%)
  other arithmetic  8.45 us (2%)
    pallas_call x1, Pallas kernels, back(): pl.pallas_call(functools.partial(back_kernel, plan, line, shards), grid=(...  330 us
    pallas_call x1, Pallas kernels, front(): pl.pallas_call(functools.partial(front_kernel, line, shards, heads), grid...  118 us
    unnamed x19, local copies, waits for them, and re-layouts  13.9 us

profile of v4, /device:TPU:1, one launch (start us, length us, event | category | flops | bytes accessed | tf_op | source)
XLA Modules:
  0.0 474.1 jit_solution(17363641491663368067)
XLA Ops:
  1.3 0.7 bitcast_convert_fusion
  2.0 0.7 convert_element_type.18
  2.6 0.6 compare_convert_fusion.refs_7_.refs_22_
  3.2 0.7 convert_element_type.21
  3.9 0.7 pad_convert_fusion
  4.6 0.4 scatter.20.refs_0_
  5.0 0.0 copy-start.5
  5.0 1.2 multiply_sine_fusion
  6.2 3.1 broadcast_select_fusion.refs_1_
  9.3 117.9 %front.1 = (f32[128,128]{1,0:T(8,128)}, bf16[1024,3072]{1,0:T(8,128)(2,1)}, bf16[1024,1024]{1,0:T(8,128)(2,1)}, bf16[1024,2048]{1,0:T(8,128)(2,1)}, bf16[1024,10...) custom-call(f32[16,128]{1,0:T(8,128)} %copy-done.5, ...), custom_call_target="tpu_custom_call" | custom-call | tf_op jit(solution)/shard_map/front/pallas_call | solution.py:1220
  127.2 330.4 %back.1 = (bf16[1024,1024]{1,0:T(8,128)(2,1)}, f32[1024,1024]{1,0:T(8,128)}, f32[128,8192]{1,0:T(8,128)}, f32[512,1024]{1,0:T(8,128)}, f32[128,1024]{1,0:T(8,128...) custom-call(bf16[1024,1024]{1,0:T(8,128)(2,1)} %get-tuple-element.68, ...), custom_call_target="tpu_custom_call" | custom-call | tf_op jit(solution)/shard_map/back/pallas_call | solution.py:1944
  457.7 0.8 slice_reduce_fusion
  458.4 1.3 slice_bitcast_fusion
  459.7 0.1 reshape.134
  459.8 0.7 copy.21
  460.5 3.2 copy.31
  463.7 2.1 copy.32
  465.8 0.4 copy-done.3
  466.2 1.1 copy.33
  467.4 1.1 copy-done.4
  468.5 0.8 copy.34
  469.3 2.1 copy.35
  471.5 1.0 copy-done.2
  472.4 1.3 copy.36
  (11 shorter events, 0.1 us)
Async XLA Ops:
  5.0 4.4 copy-start.5
  460.5 3.2 copy-start.1
  463.7 2.5 copy-start.3
  463.7 5.6 %copy-start = (f32[128,8192]{1,0:T(8,128)S(1)}, f32[128,8192]{1,0:T(8,128)}, u32[]{:S(2)}) copy-start(f32[128,8192]{1,0:T(8,128)} %get-tuple-element.120) | copy-start | bytes 12582916
  466.2 2.3 copy-start.4
  469.3 3.1 copy-start.2

commit v5 on v4

--- a/solution.py
+++ b/solution.py
@@ -1288,7 +1288,7 @@
     only, shared = reduce_split(TILE)
     both = only + shared
     low = jnp.bfloat16
-    copies = 3 * line + 4
+    copies = 7
     return [
         pltpu.VMEM((KEPT, shards, half, TILE), low),
         pltpu.VMEM((GIVEN, shards, half, TILE), low),
@@ -1325,6 +1325,7 @@
             self.recv_sem,
         ) = scratch
         self.shards, self.half = self.kept.shape[1], self.kept.shape[2]
+        self.own = net.y * net.line + net.z
         self.only, self.shared = reduce_split(TILE)
         self.both = self.only + self.shared
         self.carried = pl.ds(aligned(net.x * self.only, 128), self.both)
@@ -1343,36 +1344,35 @@
         )
 
     def halves(self, tile):
-        line = self.net.line
-        return self.remote(tile, self.give.at[tile % GIVEN], self.got.at[tile % GOT], 2 * line, self.net.sibling)
+        return self.remote(tile, self.give.at[tile % GIVEN], self.got.at[tile % GOT], 3, self.net.sibling)
 
     def over_x(self, tile):
         origin = self.kept.at[tile % KEPT, :, :, self.their_lone]
-        return self.remote(tile, origin, self.from_x.at[tile % OVER_X], 2 * self.net.line + 1, self.net.across_x)
-
-    def over_y(self, tile, z):
+        return self.remote(tile, origin, self.from_x.at[tile % OVER_X], 4, self.net.across_x)
+
+    def over_y(self, tile):
         net = self.net
-        origin = self.kept.at[tile % KEPT, z * 2 + 1 - net.y, :, self.carried]
-        return self.remote(tile, origin, self.from_y.at[tile % OVER_Y, z], 2 * net.line + 4 + z, net.across_y)
+        origin = self.kept.at[tile % KEPT, pl.ds((1 - net.y) * net.line, net.line), :, self.carried]
+        return self.remote(tile, origin, self.from_y.at[tile % OVER_Y], 2, net.across_y)
 
     def up(self, tile, z):
-        net = self.net
-        origin = self.kept.at[tile % KEPT, z * 2 + net.y, :, self.carried]
-        return self.remote(tile, origin, self.from_z.at[tile % OVER_Z, z + 1], z, net.above)
+        net, count = self.net, self.net.line - 1 - z
+        origin = self.kept.at[tile % KEPT, pl.ds(net.y * net.line + z + 1, count), :, self.carried]
+        return self.remote(tile, origin, self.from_z.at[tile % OVER_Z, pl.ds(z + 2, count)], 0, net.above)
 
     def down(self, tile, z):
         net = self.net
-        origin = self.kept.at[tile % KEPT, z * 2 + net.y, :, self.carried]
-        return self.remote(tile, origin, self.from_z.at[tile % OVER_Z, z], net.line + z, net.below)
+        origin = self.kept.at[tile % KEPT, pl.ds(net.y * net.line, z), :, self.carried]
+        return self.remote(tile, origin, self.from_z.at[tile % OVER_Z, pl.ds(0, z)], 1, net.below)
 
     def end_x(self, tile):
         net = self.net
-        origin = self.kept.at[tile % KEPT, net.own, :, self.carried]
-        return self.remote(tile, origin, self.late.at[tile % LATE], 2 * net.line + 2, net.across_x)
+        origin = self.kept.at[tile % KEPT, self.own, :, self.carried]
+        return self.remote(tile, origin, self.late.at[tile % LATE], 5, net.across_x)
 
     def to_core(self, tile):
         slot = tile % ENDS
-        return self.remote(tile, self.final.at[slot], self.swapped.at[slot], 2 * self.net.line + 3, self.net.sibling)
+        return self.remote(tile, self.final.at[slot], self.swapped.at[slot], 6, self.net.sibling)
 
     def add(self, tile, shard, part):
         slot = tile % KEPT
@@ -1401,46 +1401,50 @@
         def _(shard):
             self.kept[slot, shard, :, self.lone] = self.kept[slot, shard, :, self.lone] + self.from_x[came, shard]
 
-        for z in range(self.net.line):
-            self.over_y(tile, z).start()
+        self.over_y(tile).start()
 
     def meet_y(self, tile):
-        for z in range(self.net.line):
-            self.over_y(tile, z).wait_recv()
-            self.add(tile, z * 2 + self.net.y, self.from_y[tile % OVER_Y, z])
+        self.over_y(tile).wait_recv()
+        came, base = tile % OVER_Y, self.net.y * self.net.line
+
+        @pl.loop(0, self.net.line)
+        def _(z):
+            self.add(tile, base + z, self.from_y[came, z])
+
         self.hop(tile, 0)
 
     def hop(self, tile, step):
         net, came = self.net, tile % OVER_Z
+        base, end = net.y * net.line, net.line - 1
 
         @pl.when(net.z == step)
         def _():
-            for z in range(net.line - 1, step, -1):
-                if step > 0:
-                    self.up(tile, z).wait_recv()
-                    self.add(tile, z * 2 + net.y, self.from_z[came, z + 1])
-                self.up(tile, z).start()
-
-        @pl.when(net.z == net.line - 1 - step)
+            if step > 0:
+                self.up(tile, step - 1).wait_recv()
+                for z in range(step + 1, net.line):
+                    self.add(tile, base + z, self.from_z[came, z + 1])
+            self.up(tile, step).start()
+
+        @pl.when(net.z == end - step)
         def _():
-            for z in range(net.line - 1 - step):
-                if step > 0:
-                    self.down(tile, z).wait_recv()
-                    self.add(tile, z * 2 + net.y, self.from_z[came, z])
-                self.down(tile, z).start()
+            if step > 0:
+                self.down(tile, end - step + 1).wait_recv()
+                for z in range(end - step):
+                    self.add(tile, base + z, self.from_z[came, z])
+            self.down(tile, end - step).start()
 
     def land(self, tile):
-        net, came = self.net, tile % OVER_Z
+        net, came, end = self.net, tile % OVER_Z, self.net.line - 1
+        pl.when(net.z == end)(self.up(tile, end - 1).wait_recv)
+        pl.when(net.z == 0)(self.down(tile, 1).wait_recv)
 
         @pl.when(net.has_below)
         def _():
-            self.up(tile, net.z).wait_recv()
-            self.add(tile, net.own, self.from_z[came, net.z + 1])
+            self.add(tile, self.own, self.from_z[came, net.z + 1])
 
         @pl.when(net.has_above)
         def _():
-            self.down(tile, net.z).wait_recv()
-            self.add(tile, net.own, self.from_z[came, net.z])
+            self.add(tile, self.own, self.from_z[came, net.z])
 
         self.end_x(tile).start()
 
@@ -1448,7 +1452,7 @@
         net, only, both, shared = self.net, self.only, self.both, self.shared
         slot, came, end = tile % KEPT, tile % LATE, tile % ENDS
         self.end_x(tile).wait_recv()
-        self.final[end, :, self.lone] = self.kept[slot, net.own, :, self.lone]
+        self.final[end, :, self.lone] = self.kept[slot, self.own, :, self.lone]
         for x in range(2):
 
             @pl.when(net.x == x)
@@ -1458,7 +1462,7 @@
                 at = (1 - x) * both
                 self.final[end, :, at : at + only] = self.late[came, :, theirs : theirs + only]
                 self.final[end, :, only:both] = (
-                    self.kept[slot, net.own, :, only:both] + self.late[came, :, middle : middle + shared]
+                    self.kept[slot, self.own, :, only:both] + self.late[came, :, middle : middle + shared]
                 )
 
         self.to_core(tile).start()
@@ -1475,10 +1479,10 @@
         net = self.net
         self.writes(tile, self.wide.at[tile % WIDE], self.local_sem.at[tile % KEPT], False)
         self.over_x(tile).wait_send()
-        for z in range(net.line):
-            self.over_y(tile, z).wait_send()
-            pl.when(net.z < z)(self.up(tile, z).wait_send)
-            pl.when(net.z > z)(self.down(tile, z).wait_send)
+        self.over_y(tile).wait_send()
+        for z in range(net.line - 1):
+            pl.when(net.z == z)(self.up(tile, z).wait_send)
+            pl.when(net.z == z + 1)(self.down(tile, z + 1).wait_send)
         self.end_x(tile).wait_send()
         self.to_core(tile).wait_send()
 
@@ -1639,11 +1643,27 @@
     ]
     hidden_load = load(5, hidden_hbm, acc)
     result_store = load(6, act, result_hbm)
-    attended_load = load(7, attended_hbm, w_down)
+    attended_wait = load(7, attended_hbm, w_down)
     out_load = load(8, out_hbm, d_up.at[0])
-    normed_one_load = load(9, normed_one_hbm, turned)
+    normed_one_wait = load(9, normed_one_hbm, turned)
     x_load = load(10, x_hbm, normed)
     tokens_store = load(11, acc, tokens_hbm)
+
+    def placed():
+        for shard in range(shards):
+            order = (shard % 2) * line + shard // 2
+            for part in range(2):
+                which = net.core if part == 0 else 1 - net.core
+                start = (shard * 2 + part) * half
+                yield start, aligned((which * shards + order) * half, half)
+
+    def in_order(index, origin, landing):
+        return [load(index, origin.at[pl.ds(start, half)], landing.at[pl.ds(to, half)]) for start, to in placed()]
+
+    def turn_into(page, value):
+        flipped = value.T
+        for start, to in placed():
+            page[pl.ds(to, half), :] = flipped[start : start + half]
 
     def qkv_loads(group):
         width = qkv_hbm.shape[1] // 3
@@ -1675,7 +1695,7 @@
         )
         for i in range(4)
     ]
-    gather_places = ((0, 1, 3, 5, 6, 7, 9), (6, 8, 9, 11, 12, 14, 15))
+    gather_places = ((0, 2, 4, 6, 8, 9, 10), (7, 9, 11, 12, 14, 15, 16))
 
     @at(0)
     def _():
@@ -1698,7 +1718,7 @@
     def _():
         wait(first_loads)
         grad_small[...] = jnp.zeros_like(grad_small)
-        turned[...] = normed[...].T
+        turn_into(turned, normed[...])
 
     for block in range(plan.blocks):
 
@@ -1731,7 +1751,7 @@
     @pl.when(in_ffn & (sub == 2))
     def _():
         acc[...] += product(act[...], w_down[...])
-        act_t[...] = act[...].T
+        turn_into(act_t, act[...])
 
     @pl.when(in_ffn & (sub == 3))
     def _():
@@ -1758,7 +1778,7 @@
 
     @at(last_sum + 1)
     def _():
-        start([hidden_load, attended_load])
+        start([hidden_load] + in_order(7, attended_hbm, w_down))
 
     @at(last_sum + 3)
     def _():
@@ -1786,6 +1806,7 @@
     def _():
         out_load.wait()
         act[...] = product(d_up[0], d_gate[0], COLUMNS_BY_COLUMNS).astype(jnp.bfloat16)
+        through[...] = jnp.zeros_like(through)
 
     for group in range(plan.groups):
         ready = plan.ready[group]
@@ -1801,25 +1822,27 @@
             wait(qkv_loads(group))
             if group + 1 < plan.groups:
                 start(qkv_loads(group + 1))
-            page = act_t if group % 2 == 0 else d_up.at[0]
-            quarter = TILE // 2
-            base = (group % 2) * TILE
-            part = product(page[:, :TILE], w_gate[base : base + TILE, :])
-            values = (group // 2) * TILE + (group % 2) * quarter
-            part = part + product(page[:, TILE : TILE + quarter], w_up[values : values + quarter, :])
-            if group == 0:
-                through[...] = part
-            else:
-                through[...] += part
+
+    quarter = TILE // 2
+    for parity, page in enumerate((act_t, d_up.at[0])):
+        base = parity * TILE
+        now = (step == plan.ready[parity]) | (step == plan.ready[parity + 2])
+        pair = jnp.where(step == plan.ready[parity + 2], 1, 0)
+        value_at = pl.ds(aligned(pair * TILE + parity * quarter, quarter), quarter)
+
+        @pl.when(now)
+        def _():
+            through[...] += product(page[:, :TILE], w_gate[base : base + TILE, :])
+            through[...] += product(page[:, TILE : TILE + quarter], w_up[value_at, :])
 
     @at(plan.out)
     def _():
-        attended_load.wait()
-        start([normed_one_load, x_load])
+        attended_wait.wait()
+        start(in_order(9, normed_one_hbm, turned) + [x_load])
 
     @at(plan.births[plan.keys_tiles[0]])
     def _():
-        normed_one_load.wait()
+        normed_one_wait.wait()
 
     @pl.when((heads_at >= 0) & (heads_at < plan.heads))
     def _():
@@ -1864,13 +1887,18 @@
     tile, known = plan.tile_at(step)
 
     def birth(left, right, dims=(((1,), (0,)), ((), ()))):
-        for which, target in ((net.core, stream.kept.at[tile % KEPT]), (1 - net.core, stream.give.at[tile % GIVEN])):
-            lines = [
-                left[pl.ds(aligned(shard * 2 * half + which * half, half), half), :] for shard in range(shards)
-            ]
-            out = product(jnp.concatenate(lines, axis=0), right, dims).astype(jnp.bfloat16)
-            for shard in range(shards):
-                target[shard] = out[shard * half : (shard + 1) * half]
+        out = product(left[...], right, dims).astype(jnp.bfloat16)
+        kept, give = stream.kept.at[tile % KEPT], stream.give.at[tile % GIVEN]
+        for order in range(shards):
+            kept[order] = out[order * half : (order + 1) * half]
+            give[order] = out[(shards + order) * half : (shards + order + 1) * half]
+
+    def chosen(numbers, bases):
+        base, hit = 0, False
+        for number, start in zip(numbers, bases):
+            now = step == plan.births[number]
+            base, hit = jnp.where(now, start, base), now | hit
+        return pl.ds(aligned(base, TILE), TILE), hit
 
     kind, source = tile % SUBSTEPS, (tile // SUBSTEPS) % 2
     in_tiles = known & (tile < plan.ffn_tiles)
@@ -1878,19 +1906,15 @@
     pl.when(in_tiles & (kind < 2))(lambda: birth(act_t, given[:, columns]))
     pl.when(in_tiles & (kind >= 2) & (kind < 4))(lambda: birth(turned, d_gate[source, :, columns]))
     pl.when(in_tiles & (kind >= 4))(lambda: birth(turned, d_up[source, :, columns]))
-    for number in range(2):
-        at(plan.out + number)(
-            lambda: birth(w_down, d_gate[0, :, number * TILE : (number + 1) * TILE])
-        )
-    for group, number in enumerate(plan.keys_tiles):
-        base = (group % 2) * TILE
-        at(plan.births[number])(lambda: birth(turned, w_gate[base : base + TILE, :], COLUMNS_BY_COLUMNS))
-    for pair, number in enumerate(plan.value_tiles):
-        base = pair * TILE
-        at(plan.births[number])(lambda: birth(turned, w_up[base : base + TILE, :], COLUMNS_BY_COLUMNS))
+    out_columns = pl.ds(aligned(jnp.clip(step - plan.out, 0, 1) * TILE, TILE), TILE)
+    pl.when((step == plan.out) | (step == plan.out + 1))(lambda: birth(w_down, d_gate[0, :, out_columns]))
+    lines, hit = chosen(plan.keys_tiles, [(group % 2) * TILE for group in range(plan.groups)])
+    pl.when(hit)(lambda: birth(turned, w_gate[lines, :], COLUMNS_BY_COLUMNS))
+    value_lines, value_hit = chosen(plan.value_tiles, [pair * TILE for pair in range(plan.groups // 2)])
+    pl.when(value_hit)(lambda: birth(turned, w_up[value_lines, :], COLUMNS_BY_COLUMNS))
     pl.when(known)(lambda: stream.born(tile))
 
-    @at(plan.last)
+    @at(plan.last + 1)
     def _():
         x_load.wait()
         grad_gain_one_ref[...] = jnp.zeros_like(grad_gain_one_ref)
@@ -1914,7 +1938,7 @@
         net, grad_small, sum_small, 0, 0, small_buffers, small_local, small_send, small_recv
     )
     for index, action in enumerate(small_steps):
-        at(plan.last + 1 + index)(action)
+        at(plan.last + 2 + index)(action)
 
     @at(plan.grid - 1)
     def _():

time: 483 us -> 476 us (0.986)
  Pallas kernels: 448 us -> 442 us
    pallas_call x1, Pallas kernels: 330 us -> 324 us  [back(): pl.pallas_call(functools.partial(back_kernel, plan, line, shards), grid=(...]
where the time goes in v5:
time: 476 us; the launch traced here: 467 us
  Pallas kernels  442 us (93%)
  local copies, waits for them, and re-layouts  15.7 us (3%)
  other arithmetic  8.45 us (2%)
    pallas_call x1, Pallas kernels, back(): pl.pallas_call(functools.partial(back_kernel, plan, line, shards), grid=(...  324 us
    pallas_call x1, Pallas kernels, front(): pl.pallas_call(functools.partial(front_kernel, line, shards, heads), grid...  118 us
    unnamed x19, local copies, waits for them, and re-layouts  13.9 us

profile of v5, /device:TPU:1, one launch (start us, length us, event | category | flops | bytes accessed | tf_op | source)
XLA Modules:
  0.0 467.3 jit_solution(13568296190274956890)
XLA Ops:
  1.3 0.7 bitcast_convert_fusion
  2.0 0.7 convert_element_type.18
  2.6 0.6 compare_convert_fusion.refs_7_.refs_22_
  3.2 0.7 convert_element_type.21
  3.9 0.7 pad_convert_fusion
  4.6 0.4 scatter.20.refs_0_
  5.0 0.0 copy-start.5
  5.0 1.2 multiply_sine_fusion
  6.2 3.1 broadcast_select_fusion.refs_1_
  9.3 117.8 %front.1 = (f32[128,128]{1,0:T(8,128)}, bf16[1024,3072]{1,0:T(8,128)(2,1)}, bf16[1024,1024]{1,0:T(8,128)(2,1)}, bf16[1024,2048]{1,0:T(8,128)(2,1)}, bf16[1024,10...) custom-call(f32[16,128]{1,0:T(8,128)} %copy-done.5, ...), custom_call_target="tpu_custom_call" | custom-call | tf_op jit(solution)/shard_map/front/pallas_call | solution.py:1220
  127.2 323.7 %back.1 = (bf16[1024,1024]{1,0:T(8,128)(2,1)}, f32[1024,1024]{1,0:T(8,128)}, f32[128,8192]{1,0:T(8,128)}, f32[512,1024]{1,0:T(8,128)}, f32[128,1024]{1,0:T(8,128...) custom-call(bf16[1024,1024]{1,0:T(8,128)(2,1)} %get-tuple-element.68, ...), custom_call_target="tpu_custom_call" | custom-call | tf_op jit(solution)/shard_map/back/pallas_call | solution.py:1968
  450.9 0.8 slice_reduce_fusion
  451.7 1.3 slice_bitcast_fusion
  452.9 0.1 reshape.134
  453.0 0.7 copy.21
  453.7 3.2 copy.31
  456.9 2.1 copy.32
  459.1 0.4 copy-done.3
  459.5 1.1 copy.33
  460.6 1.1 copy-done.4
  461.7 0.8 copy.34
  462.5 2.1 copy.35
  464.7 1.0 copy-done.2
  465.6 1.3 copy.36
  (11 shorter events, 0.1 us)
Async XLA Ops:
  5.0 4.4 copy-start.5
  453.7 3.2 copy-start.1
  456.9 2.5 copy-start.3
  456.9 5.6 %copy-start = (f32[128,8192]{1,0:T(8,128)S(1)}, f32[128,8192]{1,0:T(8,128)}, u32[]{:S(2)}) copy-start(f32[128,8192]{1,0:T(8,128)} %get-tuple-element.120) | copy-start | bytes 12582916
  459.5 2.3 copy-start.4
  462.5 3.1 copy-start.2

commit v6 on v5

--- a/solution.py
+++ b/solution.py
@@ -1549,7 +1549,7 @@
     into_2, into_3, down_hbm = take(3)
     attended_hbm, out_hbm, normed_one_hbm, x_hbm, qkv_hbm = take(5)
     small_hbm, = take(1)
-    q_ref, k_ref, v_ref, wide_ref, lse_ref, var_ref, valid_ref, cos_ref, sin_ref = take(9)
+    length_ref, q_ref, k_ref, v_ref, wide_ref, lse_ref, var_ref, valid_ref, cos_ref, sin_ref = take(10)
     result_hbm, tokens_hbm, sum_in, sum_down, sum_out, sum_qkv, sum_small = take(7)
     gather_to = take(4)
     normed, turned, given, w_down, w_gate, w_up, act, act_t = take(8)
@@ -1717,6 +1717,9 @@
     @at(0)
     def _():
         wait(first_loads)
+        position = lax.broadcasted_iota(jnp.int32, (given.shape[0], 1), 0)
+        counted = jnp.where(position < length_ref[0], 1.0, 0.0).astype(jnp.bfloat16)
+        given[...] = given[...] * counted
         grad_small[...] = jnp.zeros_like(grad_small)
         turn_into(turned, normed[...])
 
@@ -1832,8 +1835,8 @@
 
         @pl.when(now)
         def _():
-            through[...] += product(page[:, :TILE], w_gate[base : base + TILE, :])
-            through[...] += product(page[:, TILE : TILE + quarter], w_up[value_at, :])
+            part = product(page[:, :TILE], w_gate[base : base + TILE, :])
+            through[...] += part + product(page[:, TILE : TILE + quarter], w_up[value_at, :])
 
     @at(plan.out)
     def _():
@@ -1946,7 +1949,7 @@
 
 
 def back(line, early, sources, own_down, normed_two, given, hidden, attended_t, out_weight, normed_t, x, qkv_weight,
-         small, qkv_t, wide_t, log_sums, variates, valid, cos_t, sin_t):
+         small, lengths, qkv_t, wide_t, log_sums, variates, valid, cos_t, sin_t):
     shards = lax.axis_size("shard")
     rows, width = x.shape
     heads = log_sums.shape[0]
@@ -1981,6 +1984,7 @@
 ,
         in_specs=[ANY] * 16
         + [
+            pl.BlockSpec(memory_space=pltpu.SMEM),
             part(0),
             part(1),
             part(2),
@@ -2025,7 +2029,7 @@
         name="back",
     )(
         normed_two, given, hidden, *early, *sources, own_down, attended_t, out_weight, normed_t, x, qkv_weight,
-        small, qkv_t, qkv_t, qkv_t, wide_t, log_sums, variates, valid, cos_t, sin_t,
+        small, lengths, qkv_t, qkv_t, qkv_t, wide_t, log_sums, variates, valid, cos_t, sin_t,
     )
 
 
@@ -2063,7 +2067,6 @@
     heads = attn_bias.shape[1]
     key_valid = jnp.arange(length)[None, :] < lengths[:, None]
     valid = key_valid.astype(jnp.float32)
-    given = jnp.where(key_valid.reshape(length, 1), cotangent, jnp.zeros_like(cotangent))
     cos_t, sin_t = rope_tables(time_ids)
     if line:
         small, qkv_weight, out_weight, into_0, down_0, into_1, down_1, *rest = front(
@@ -2087,7 +2090,7 @@
             [intos[2], intos[3]],
             w_down,
             normed_two,
-            given,
+            cotangent,
             hidden,
             attended_t,
             out_weight,
@@ -2095,6 +2098,7 @@
             tokens,
             qkv_weight,
             small,
+            lengths,
             qkv_t,
             wide_t,
             log_sums,
@@ -2114,6 +2118,7 @@
             sum_in,
             sum_down,
         )
+    given = jnp.where(key_valid.reshape(length, 1), cotangent, jnp.zeros_like(cotangent))
     gain_one, gain_two, qkv_weight, out_weight, in_weight, down_weight = (
         lax.all_gather(part, "shard", axis=0, tiled=True)
         for part in (attn_gain, ffn_gain, w_qkv, w_out, w_in, w_down)

time: 476 us -> 473 us (level)
  no operation moved by 1% of the time
where the time goes in v6:
time: 473 us; the launch traced here: 465 us
  Pallas kernels  442 us (93%)
  local copies, waits for them, and re-layouts  15.7 us (3%)
  other arithmetic  5.31 us (1%)
    pallas_call x1, Pallas kernels, back(): pl.pallas_call(functools.partial(back_kernel, plan, line, shards), grid=(...  324 us
    pallas_call x1, Pallas kernels, front(): pl.pallas_call(functools.partial(front_kernel, line, shards, heads), grid...  118 us
    unnamed x19, local copies, waits for them, and re-layouts  13.9 us

profile of v6, /device:TPU:1, one launch (start us, length us, event | category | flops | bytes accessed | tf_op | source)
XLA Modules:
  0.0 464.8 jit_solution(2232071977742654237)
XLA Ops:
  1.3 0.7 bitcast_convert_fusion
  2.0 0.7 convert_element_type.18
  2.6 0.6 compare_convert_fusion.refs_7_.refs_23_
  3.2 0.7 convert_element_type.21
  3.9 0.7 pad_convert_fusion
  4.6 0.4 scatter.20.refs_0_
  5.0 0.0 copy-start.5
  5.0 1.2 multiply_sine_fusion
  6.2 0.0 copy-done.5
  6.2 117.9 %front.1 = (f32[128,128]{1,0:T(8,128)}, bf16[1024,3072]{1,0:T(8,128)(2,1)}, bf16[1024,1024]{1,0:T(8,128)(2,1)}, bf16[1024,2048]{1,0:T(8,128)(2,1)}, bf16[1024,10...) custom-call(f32[16,128]{1,0:T(8,128)} %copy-done.5, ...), custom_call_target="tpu_custom_call" | custom-call | tf_op jit(solution)/shard_map/front/pallas_call | solution.py:1220
  124.1 324.2 %back.1 = (bf16[1024,1024]{1,0:T(8,128)(2,1)}, f32[1024,1024]{1,0:T(8,128)}, f32[128,8192]{1,0:T(8,128)}, f32[512,1024]{1,0:T(8,128)}, f32[128,1024]{1,0:T(8,128...) custom-call(bf16[1024,1024]{1,0:T(8,128)(2,1)} %get-tuple-element.68, ...), custom_call_target="tpu_custom_call" | custom-call | tf_op jit(solution)/shard_map/back/pallas_call | solution.py:1971
  448.3 0.8 slice_reduce_fusion
  449.1 1.3 slice_bitcast_fusion
  450.4 0.1 reshape.129
  450.5 0.7 copy.21
  451.1 3.2 copy.31
  454.4 2.1 copy.32
  456.5 0.4 copy-done.3
  456.9 1.1 copy.33
  458.0 1.1 copy-done.4
  459.2 0.8 copy.34
  460.0 2.1 copy.35
  462.1 1.0 copy-done.2
  463.1 1.3 copy.36
  (9 shorter events, 0.0 us)
Async XLA Ops:
  5.0 1.3 copy-start.5
  451.1 3.2 copy-start.1
  454.4 2.5 copy-start.3
  454.4 5.6 %copy-start = (f32[128,8192]{1,0:T(8,128)S(1)}, f32[128,8192]{1,0:T(8,128)}, u32[]{:S(2)}) copy-start(f32[128,8192]{1,0:T(8,128)} %get-tuple-element.120) | copy-start | bytes 12582916
  456.9 2.3 copy-start.4
  460.0 3.1 copy-start.2

commit v7 on v6

--- a/solution.py
+++ b/solution.py
@@ -1552,8 +1552,10 @@
     length_ref, q_ref, k_ref, v_ref, wide_ref, lse_ref, var_ref, valid_ref, cos_ref, sin_ref = take(10)
     result_hbm, tokens_hbm, sum_in, sum_down, sum_out, sum_qkv, sum_small = take(7)
     gather_to = take(4)
-    normed, turned, given, w_down, w_gate, w_up, act, act_t = take(8)
-    d_gate, d_up, acc, through = take(4)
+    normed, turned, given, w_down, act, act_t = take(6)
+    w_both, d_both, acc, through = take(4)
+    w_gate, w_up = w_both.at[0], w_both.at[1]
+    d_gate, d_up = d_both.at[pl.ds(0, 2)], d_both.at[pl.ds(2, 2)]
     query_ref, given_aug_ref, dk_acc, dv_acc = take(4)
     load_sem, = take(1)
     gather_local, gather_send, gather_recv = take(3)
@@ -1756,21 +1758,19 @@
         acc[...] += product(act[...], w_down[...])
         turn_into(act_t, act[...])
 
-    @pl.when(in_ffn & (sub == 3))
-    def _():
-        part = product(d_gate[slot], w_gate[...], COLUMNS_BY_COLUMNS)
-
-        @pl.when(block == 0)
+    @pl.when(in_ffn & ((sub == 3) | (sub == 4)))
+    def _():
+        which = jnp.clip(sub - 3, 0, 1)
+        part = product(d_both[2 * which + slot], w_both[which], COLUMNS_BY_COLUMNS)
+        first = (block == 0) & (sub == 3)
+
+        @pl.when(first)
         def _():
             through[...] = part
 
-        @pl.when(block > 0)
+        @pl.when(jnp.logical_not(first))
         def _():
             through[...] += part
-
-    @pl.when(in_ffn & (sub == 4))
-    def _():
-        through[...] += product(d_up[slot], w_up[...], COLUMNS_BY_COLUMNS)
 
     last_sum = plan.ffn - SUBSTEPS + 2
 
@@ -1901,20 +1901,21 @@
         for number, start in zip(numbers, bases):
             now = step == plan.births[number]
             base, hit = jnp.where(now, start, base), now | hit
-        return pl.ds(aligned(base, TILE), TILE), hit
+        return base, hit
 
     kind, source = tile % SUBSTEPS, (tile // SUBSTEPS) % 2
     in_tiles = known & (tile < plan.ffn_tiles)
     columns = pl.ds(aligned((kind % 2) * TILE, TILE), TILE)
     pl.when(in_tiles & (kind < 2))(lambda: birth(act_t, given[:, columns]))
-    pl.when(in_tiles & (kind >= 2) & (kind < 4))(lambda: birth(turned, d_gate[source, :, columns]))
-    pl.when(in_tiles & (kind >= 4))(lambda: birth(turned, d_up[source, :, columns]))
+    page_at = jnp.where(kind >= 4, 2, 0) + source
+    pl.when(in_tiles & (kind >= 2))(lambda: birth(turned, d_both[page_at, :, columns]))
     out_columns = pl.ds(aligned(jnp.clip(step - plan.out, 0, 1) * TILE, TILE), TILE)
     pl.when((step == plan.out) | (step == plan.out + 1))(lambda: birth(w_down, d_gate[0, :, out_columns]))
-    lines, hit = chosen(plan.keys_tiles, [(group % 2) * TILE for group in range(plan.groups)])
-    pl.when(hit)(lambda: birth(turned, w_gate[lines, :], COLUMNS_BY_COLUMNS))
-    value_lines, value_hit = chosen(plan.value_tiles, [pair * TILE for pair in range(plan.groups // 2)])
-    pl.when(value_hit)(lambda: birth(turned, w_up[value_lines, :], COLUMNS_BY_COLUMNS))
+    key_base, key_hit = chosen(plan.keys_tiles, [(group % 2) * TILE for group in range(plan.groups)])
+    value_base, value_hit = chosen(plan.value_tiles, [pair * TILE for pair in range(plan.groups // 2)])
+    lines = pl.ds(aligned(key_base + value_base, TILE), TILE)
+    late_page = jnp.where(value_hit, 1, 0)
+    pl.when(key_hit | value_hit)(lambda: birth(turned, w_both[late_page, lines, :], COLUMNS_BY_COLUMNS))
     pl.when(known)(lambda: stream.born(tile))
 
     @at(plan.last + 1)
@@ -1996,10 +1997,10 @@
             whole(*sin_t.shape),
         ],
         out_specs=[ANY] * 11,
-        scratch_shapes=[page] * 8
+        scratch_shapes=[page] * 6
         + [
             pltpu.VMEM((2, BLOCK, BLOCK), low),
-            pltpu.VMEM((2, BLOCK, BLOCK), low),
+            pltpu.VMEM((4, BLOCK, BLOCK), low),
             pltpu.VMEM((rows, width), jnp.float32),
             pltpu.VMEM((rows, width), jnp.float32),
             pltpu.VMEM((2 * depth + FEATURES, rows), low),

time: 473 us -> 447 us (0.945); the launches traced: 465 us -> 446 us
  Pallas kernels: 442 us -> 424 us
    pallas_call x1, Pallas kernels: 324 us -> 306 us  [back(): pl.pallas_call(functools.partial(back_kernel, plan, line, shards), grid=(...]
where the time goes in v7:
time: 447 us; the launch traced here: 446 us
  Pallas kernels  424 us (95%)
  local copies, waits for them, and re-layouts  15.7 us (4%)
  other arithmetic  5.31 us (1%)
    pallas_call x1, Pallas kernels, back(): pl.pallas_call(functools.partial(back_kernel, plan, line, shards), grid=(...  306 us
    pallas_call x1, Pallas kernels, front(): pl.pallas_call(functools.partial(front_kernel, line, shards, heads), grid...  118 us
    unnamed x19, local copies, waits for them, and re-layouts  13.9 us

profile of v7, /device:TPU:1, one launch (start us, length us, event | category | flops | bytes accessed | tf_op | source)
XLA Modules:
  0.0 446.4 jit_solution(6969279854709102427)
XLA Ops:
  1.3 0.7 bitcast_convert_fusion
  2.0 0.7 convert_element_type.18
  2.6 0.6 compare_convert_fusion.refs_7_.refs_23_
  3.2 0.7 convert_element_type.21
  3.9 0.7 pad_convert_fusion
  4.6 0.4 scatter.20.refs_0_
  5.0 0.0 copy-start.5
  5.0 1.2 multiply_sine_fusion
  6.2 0.0 copy-done.5
  6.2 117.8 %front.1 = (f32[128,128]{1,0:T(8,128)}, bf16[1024,3072]{1,0:T(8,128)(2,1)}, bf16[1024,1024]{1,0:T(8,128)(2,1)}, bf16[1024,2048]{1,0:T(8,128)(2,1)}, bf16[1024,10...) custom-call(f32[16,128]{1,0:T(8,128)} %copy-done.5, ...), custom_call_target="tpu_custom_call" | custom-call | tf_op jit(solution)/shard_map/front/pallas_call | solution.py:1220
  124.0 306.2 %back.1 = (bf16[1024,1024]{1,0:T(8,128)(2,1)}, f32[1024,1024]{1,0:T(8,128)}, f32[128,8192]{1,0:T(8,128)}, f32[512,1024]{1,0:T(8,128)}, f32[128,1024]{1,0:T(8,128...) custom-call(bf16[1024,1024]{1,0:T(8,128)(2,1)} %get-tuple-element.68, ...), custom_call_target="tpu_custom_call" | custom-call | tf_op jit(solution)/shard_map/back/pallas_call | solution.py:1972
  430.3 0.8 slice_reduce_fusion
  431.1 1.3 slice_bitcast_fusion
  432.3 0.1 reshape.129
  432.4 0.7 copy.21
  433.1 3.2 copy.31
  436.3 2.1 copy.32
  438.4 0.4 copy-done.3
  438.9 1.1 copy.33
  440.0 1.1 copy-done.4
  441.1 0.8 copy.34
  441.9 2.1 copy.35
  444.1 1.0 copy-done.2
  445.0 1.3 copy.36
  (9 shorter events, 0.0 us)
Async XLA Ops:
  5.0 1.3 copy-start.5
  433.1 3.2 copy-start.1
  436.3 2.5 copy-start.3
  436.3 5.6 %copy-start = (f32[128,8192]{1,0:T(8,128)S(1)}, f32[128,8192]{1,0:T(8,128)}, u32[]{:S(2)}) copy-start(f32[128,8192]{1,0:T(8,128)} %get-tuple-element.120) | copy-start | bytes 12582916
  438.9 2.3 copy-start.4
  441.9 3.1 copy-start.2
